TPU v7x, 32 devices: a whole 2x2x4 slice. The times are simulated.
32 devices in a mesh: grp: 2 (over x), ctx: 16 (over z, y, core).
Axes of the slice: x: 2, y: 2, z: 4, core: 2. Of those that a mesh axis runs over, the one named last changes fastest.
Arguments:
- queries: bfloat16 [2, 24, 64, 576], P('grp', None, 'ctx'), parts along dimension 0, may hold values from -40 to 40
- cache: bfloat16 [2, 8192, 576], P('grp', 'ctx'), parts along dimension 0, may hold values from -6 to 6
- draft_latent: bfloat16 [2, 24, 576], P('grp'), parts along dimension 0, may hold values from -9 to 9
- lengths: int32 [2], P('grp'), parts along dimension 0, may hold values from 4096 to 8192
- parents: int32 [2, 24], P('grp'), parts along dimension 0, may hold values from -1 to 22, as said below
- value_up: bfloat16 [64, 512, 128], P('ctx'), may hold values from -0.25 to 0.25
- out_proj: bfloat16 [8192, 7168], P('ctx'), may hold values from -0.09375 to 0.09375
Outputs:
- attended: bfloat16 [48, 7168], P('grp', 'ctx'), parts along dimension 0
There are 2 independent parts, one for each index of `grp`. A program takes and returns all parts, laid end to end along the dimension named above; an argument that names none is the same for every part. Nothing has to cross between parts.
Inputs may be any that keep to these rules, and one draw needn't show every extreme that they name: parents[r, 0] = -1 and 0 <= parents[r, i] < i for i >= 1.
All inputs are finite; a program needn't handle non-finite values.
Results may differ from a plain program's by a relative error of at most 0.007.
Values may be sent and summed in bfloat16 or wider, within the bound.
No kernel may reach another device: no remote copies, remote signals or barrier semaphores. Data moves between devices by JAX's collectives and lax.ppermute only.
A program may use at most 64 MiB of HBM per device.

v0:
```python
import math

import jax
import jax.numpy as jnp
from jax import lax
from jax.experimental import pallas as pl
from jax.experimental.pallas import tpu as pltpu
from jax.sharding import PartitionSpec as P


yarn_factor = 1.0 + 0.1 * math.log(32.0)
score_scale = yarn_factor * yarn_factor / math.sqrt(192.0)
log2_scale = score_scale / math.log(2.0)
neg_fill = -1e30
low_top = -1e29
PACK_ROWS = 8


def tree_bias(parents):
    drafts = parents.shape[0]
    order = jnp.arange(drafts, dtype=jnp.int32)
    step = (parents[:, None] == order[None, :]) | (order[:, None] == order[None, :])
    reach = step.astype(jnp.bfloat16)
    covered = 1
    while covered < drafts:
        grown = jnp.dot(reach, reach, preferred_element_type=jnp.float32)
        reach = (grown > 0.5).astype(jnp.bfloat16)
        covered *= 2
    return jnp.where(reach > 0.5, 0.0, neg_fill).astype(jnp.float32)


NT = (((1,), (1,)), ((), ()))


def weights_of(masked, top):
    weights = jnp.exp2(masked - top).astype(jnp.bfloat16)
    return weights, jnp.sum(weights.astype(jnp.float32), axis=1, keepdims=True)


def draft_kernel(q_ref, keys_ref, bias_ref, up_from, numer_ref, top_ref, total_ref, up_ref):
    up_ref[...] = up_from[...]
    latent = numer_ref.shape[1]
    keys = keys_ref[...]
    repeats = q_ref.shape[0] // bias_ref.shape[0]
    bias = jnp.concatenate([bias_ref[...]] * repeats, axis=0)
    scores = lax.dot_general(q_ref[...], keys, NT, preferred_element_type=jnp.float32)
    masked = scores * log2_scale + bias
    top = jnp.max(masked, axis=1, keepdims=True)
    weights, total = weights_of(masked, top)
    numer_ref[...] = jnp.dot(weights, keys[:, :latent], preferred_element_type=jnp.float32)
    top_ref[...] = top
    total_ref[...] = total


def fold(rows, key_refs, bias_ref, carry, latent):
    blocks, tops = [], []
    for spot, key_ref in enumerate(key_refs):
        scores = jnp.dot(rows, key_ref[...], preferred_element_type=jnp.float32)
        masked = scores * log2_scale + bias_ref[spot : spot + 1, :]
        blocks.append(masked)
        tops.append(jnp.max(masked, axis=1, keepdims=True))
    top = carry[1] if carry is not None else jnp.full_like(tops[0], low_top)
    for other in tops:
        top = jnp.maximum(top, other)
    numer = total = None
    if carry is not None:
        factor = jnp.exp2(carry[1] - top)
        numer, total = carry[0] * factor, carry[2] * factor
    for key_ref, masked in zip(key_refs, blocks):
        weights, count = weights_of(masked, top)
        part = lax.dot_general(weights, key_ref[:latent, :], NT, preferred_element_type=jnp.float32)
        numer = part if numer is None else numer + part
        total = count if total is None else total + count
    return numer, top, total


def join_rows(q_refs):
    return jnp.concatenate([q[...] for q in q_refs], axis=0)


def first_kernel(peers, bias_ref, *refs):
    q_refs, refs = refs[:peers], refs[peers:]
    key_refs, (numer_ref, top_ref, total_ref) = refs[:-3], refs[-3:]
    numer, top, total = fold(join_rows(q_refs), key_refs, bias_ref, None, numer_ref.shape[1])
    numer_ref[...] = numer
    top_ref[...] = top
    total_ref[...] = total


def middle_kernel(peers, bias_ref, *refs):
    q_refs, (key_ref, *carry_refs, numer_ref, top_ref, total_ref) = refs[:peers], refs[peers:]
    carry = tuple(ref[...] for ref in carry_refs)
    numer, top, total = fold(join_rows(q_refs), [key_ref], bias_ref, carry, numer_ref.shape[1])
    numer_ref[...] = numer
    top_ref[...] = top
    total_ref[...] = total


def as_row(column):
    count = column.shape[0]
    eye = lax.broadcasted_iota(jnp.int32, (count, count), 0) == lax.broadcasted_iota(
        jnp.int32, (count, count), 1
    )
    return jnp.sum(jnp.where(eye, column, 0.0), axis=0, keepdims=True)


def as_column(row):
    count = row.shape[1]
    eye = lax.broadcasted_iota(jnp.int32, (count, count), 0) == lax.broadcasted_iota(
        jnp.int32, (count, count), 1
    )
    return jnp.sum(jnp.where(eye, row, 0.0), axis=1, keepdims=True)


def pieces(row):
    high = row.astype(jnp.bfloat16).astype(jnp.float32)
    rest = row - high
    middle = rest.astype(jnp.bfloat16).astype(jnp.float32)
    return [high, middle, rest - middle]


def last_kernel(peers, bias_ref, *refs):
    q_refs, (key_ref, *rest) = refs[:peers], refs[peers:]
    numer_ref, top_ref, total_ref, own_refs, out_refs = *rest[:3], rest[3:6], rest[6:]
    carry = (numer_ref[...], top_ref[...], total_ref[...])
    latent = numer_ref.shape[1]
    numer, top, total = fold(join_rows(q_refs), [key_ref], bias_ref, carry, latent)
    each = q_refs[0].shape[0]
    for own_ref, value in zip(own_refs, (numer, top, total)):
        own_ref[...] = value[:each]
    for peer, out_ref in enumerate(out_refs, 1):
        here = slice(peer * each, (peer + 1) * each)
        out_ref[:each, :] = numer[here].astype(jnp.bfloat16)
        lines = pieces(as_row(top[here])) + pieces(as_row(total[here]))
        lines += [jnp.zeros_like(lines[0])] * (PACK_ROWS - len(lines))
        packed = jnp.concatenate(lines, axis=0)
        packed = jnp.concatenate(
            [packed, jnp.zeros((PACK_ROWS, latent - each), jnp.float32)], axis=1
        )
        out_ref[each:, :] = packed.astype(jnp.bfloat16)


def project_kernel(peers, *refs):
    state_refs, refs = refs[: peers - 1], refs[peers - 1 :]
    full_refs, refs = refs[:6], refs[6:]
    up_ref, proj_from, keep_ref, send_ref, flat_ref, proj_ref, done = refs
    each = full_refs[0].shape[0]
    heads, _, width = up_ref.shape
    columns = keep_ref.shape[2]
    span = math.lcm(2 * columns, 128)
    blocks = proj_ref.shape[1] // span
    copies = []
    for block in range(blocks):
        strip = (slice(None), pl.ds(block * span, span))
        copies.append(
            pltpu.make_async_copy(proj_from.at[strip], proj_ref.at[strip], done.at[block])
        )
    for copy in copies:
        copy.start()
    drafts = each // heads
    numers = [full_refs[0][...], full_refs[3][...]]
    tops = [full_refs[1][...], full_refs[4][...]]
    totals = [full_refs[2][...], full_refs[5][...]]
    for state in state_refs:
        lines = state[each:, :each].astype(jnp.float32)
        numers.append(state[:each, :].astype(jnp.float32))
        tops.append(as_column(lines[0:1] + lines[1:2] + lines[2:3]))
        totals.append(as_column(lines[3:4] + lines[4:5] + lines[5:6]))
    best = tops[0]
    for other in tops[1:]:
        best = jnp.maximum(best, other)
    numer = total = 0.0
    for part, top, count in zip(numers, tops, totals):
        factor = jnp.exp2(top - best)
        numer = numer + part * factor
        total = total + count * factor
    latent_out = (numer / total).astype(jnp.bfloat16)
    for head in range(heads):
        value = jnp.dot(
            latent_out[head * drafts : (head + 1) * drafts],
            up_ref[head],
            preferred_element_type=jnp.float32,
        )
        flat_ref[:, head * width : (head + 1) * width] = value.astype(jnp.bfloat16)
    flat = flat_ref[...]
    first_core = lax.rem(lax.axis_index("ctx"), 2) == 0
    for block in range(blocks):
        copies[block].wait()
        part = jnp.dot(
            flat,
            proj_ref[:, block * span : (block + 1) * span],
            preferred_element_type=jnp.float32,
        )
        for pair in range(span // (2 * columns)):
            halves = []
            for side in range(2):
                shift = (2 * pair + side) * columns
                moved = part if shift == 0 else pltpu.roll(part, span - shift, 1)
                halves.append(moved[:, :columns])
            spot = block * (span // (2 * columns)) + pair
            keep_ref[spot] = jnp.where(first_core, halves[0], halves[1])
            send_ref[spot] = jnp.where(first_core, halves[1], halves[0]).astype(jnp.bfloat16)


def pair_kernel(keep_ref, got_ref, stay_ref, send_ref):
    side = lax.rem(lax.div(lax.axis_index("ctx"), 2), 2)
    for spot in range(stay_ref.shape[0]):
        mine = 2 * spot + side
        yours = 2 * spot + 1 - side
        stay_ref[spot] = keep_ref[mine] + got_ref[mine].astype(jnp.float32)
        send_ref[spot] = (keep_ref[yours] + got_ref[yours].astype(jnp.float32)).astype(jnp.bfloat16)


def quad_kernel(stay_ref, got_ref, own_ref, *out_refs):
    outer = lax.div(lax.axis_index("ctx"), 4)

    def both(spot):
        return stay_ref[spot] + got_ref[spot].astype(jnp.float32)

    for peer, out_ref in enumerate(out_refs, 1):
        out_ref[...] = both(lax.bitwise_xor(outer, peer)).astype(jnp.bfloat16)
    own_ref[...] = both(outer)


def call(kernel, outs, values, specs=None, scratch=(), limit=24):
    return pl.pallas_call(
        kernel,
        out_shape=outs,
        in_specs=specs or [pl.BlockSpec() for _ in values],
        scratch_shapes=list(scratch),
        compiler_params=pltpu.CompilerParams(vmem_limit_bytes=limit << 20),
    )(*values)


def shaped(*shape, dtype=jnp.float32):
    return jax.ShapeDtypeStruct(shape, dtype)


def on_device(count, queries, cache, draft_latent, lengths, parents, value_up, out_proj):
    drafts, heads_here, width = queries.shape[1:]
    latent = value_up.shape[1]
    block_len = cache.shape[1]
    inner = 4
    outer = count // inner
    chips = count // 2
    columns = out_proj.shape[1] // count
    each = heads_here * drafts
    bf16 = jnp.bfloat16
    myself = lax.axis_index("ctx")

    def bias_of(*bits):
        firsts = jnp.stack([lax.bitwise_xor(myself, bit) * block_len for bit in bits])
        spots = firsts[:, None] + jnp.arange(block_len, dtype=jnp.int32)[None, :]
        return jnp.where(spots < lengths[0], 0.0, neg_fill).astype(jnp.float32)

    def swap(value, bits):
        return lax.ppermute(value, "ctx", [(i, i ^ bits) for i in range(count)])

    keys_own = jnp.transpose(cache[0])
    keys_across = swap(keys_own, 2)
    keys_core = swap(keys_own, 1)
    own_rows = jnp.transpose(queries[0], (1, 0, 2)).reshape(each, width)
    rows = [own_rows] + [swap(own_rows, inner * peer) for peer in range(outer - 1, 0, -1)][::-1]
    keys_far = swap(keys_across, 1)

    state_shape = (shaped(outer * each, latent), shaped(outer * each, 1), shaped(outer * each, 1))
    own_shape = (shaped(each, latent), shaped(each, 1), shaped(each, 1))
    *drafted, up_here = call(
        draft_kernel,
        own_shape + (shaped(*value_up.shape, dtype=bf16),),
        (own_rows, draft_latent[0], tree_bias(parents[0]), value_up),
    )
    state = call(
        lambda *refs: first_kernel(outer, *refs),
        state_shape,
        (bias_of(0, 1), *rows, keys_own, keys_core),
    )
    state = call(
        lambda *refs: middle_kernel(outer, *refs),
        state_shape,
        (bias_of(2), *rows, keys_across, *state),
    )
    done = call(
        lambda *refs: last_kernel(outer, *refs),
        own_shape
        + tuple(shaped(each + PACK_ROWS, latent, dtype=bf16) for _ in range(outer - 1)),
        (bias_of(3), *rows, keys_far, *state),
    )
    whole, states = done[:3], done[3:]
    got = [swap(states[peer - 1], inner * peer) for peer in range(outer - 1, 0, -1)]
    keep, send = call(
        lambda *refs: project_kernel(outer, *refs),
        (shaped(chips, drafts, columns), shaped(chips, drafts, columns, dtype=bf16)),
        (*got, *whole, *drafted, up_here, out_proj),
        specs=[pl.BlockSpec()] * (outer + 6) + [pl.BlockSpec(memory_space=pl.ANY)],
        scratch=[
            pltpu.VMEM((drafts, heads_here * value_up.shape[2]), bf16),
            pltpu.VMEM(out_proj.shape, bf16),
            pltpu.SemaphoreType.DMA((out_proj.shape[1] // math.lcm(2 * columns, 128),)),
        ],
        limit=50,
    )
    stay, send = call(
        pair_kernel,
        (shaped(chips // 2, drafts, columns), shaped(chips // 2, drafts, columns, dtype=bf16)),
        (keep, swap(send, 1)),
    )
    own, *parts = call(
        quad_kernel,
        (shaped(drafts, columns),)
        + tuple(shaped(drafts, columns, dtype=bf16) for _ in range(outer - 1)),
        (stay, swap(send, 2)),
    )
    result = own
    for peer in range(outer - 1, 0, -1):
        result = result + swap(parts[peer - 1], inner * peer).astype(jnp.float32)
    return result.astype(bf16)


def solution(mesh):
    in_specs = (
        P("grp", None, "ctx", None),
        P("grp", "ctx", None),
        P("grp", None, None),
        P("grp"),
        P("grp", None),
        P("ctx", None, None),
        P("ctx", None),
    )
    count = mesh.shape["ctx"]

    def body(*args):
        return on_device(count, *args)

    return jax.shard_map(
        body, mesh=mesh, in_specs=in_specs, out_specs=P("grp", "ctx"), check_vma=False
    )
```

profile of v0, /device:TPU:0, one launch (start us, length us, event | category | flops | bytes accessed | tf_op | source)
XLA Modules:
  0.0 54.0 jit_solution(590275123563413122)
XLA Ops:
  0.0 3.0 %collective-permute-start.3 = (bf16[576,512]{1,0:T(8,128)(2,1)}, bf16[576,512]{1,0:T(8,128)(2,1)S(1)}, u32[]{:S(2)}, u32[]{:S(2)}) collective-permute-start(bf16[576,512]{1,0:T(8,128)(2,1)} %bitcast.26), channel_id=1, source_target_pairs={{0,2},{1,3},{2,0},{3,1},{4,6},{5,7},{6,4},{7,5},{8,10},{9,11},{10,... | collective-permute-start | bytes 1769480 | tf_op jit(solution)/shard_map/ppermute | solution.py:257
  3.0 0.9 %copy.8 = bf16[4,24,576]{2,1,0:T(8,128)(2,1)S(1)} copy(bf16[4,24,576]{2,0,1:T(4,128)(2,1)} %bitcast.30) | data formatting | bytes 221184 | tf_op jit(solution)/shard_map/transpose | solution.py:262
  3.9 1.6 %collective-permute-start = (bf16[96,576]{1,0:T(8,128)(2,1)S(1)}, bf16[96,576]{1,0:T(8,128)(2,1)S(1)}, u32[]{:S(2)}, u32[]{:S(2)}) collective-permute-start(bf16[96,576]{1,0:T(8,128)(2,1)S(1)} %bitcast.19), channel_id=1, source_target_pairs={{0,4},{1,5},{2,6},{3,7},{4,0},{5,1},{6,2},{7,3},{8,12},{9,13},{10,... | collective-permute-start | bytes 331784 | tf_op jit(solution)/shard_map/ppermute | solution.py:257
  5.6 2.6 %collective-permute-start.1 = (bf16[96,576]{1,0:T(8,128)(2,1)S(1)}, bf16[96,576]{1,0:T(8,128)(2,1)S(1)}, u32[]{:S(2)}, u32[]{:S(2)}) collective-permute-start(bf16[96,576]{1,0:T(8,128)(2,1)S(1)} %bitcast.20), channel_id=1, source_target_pairs={{0,8},{1,9},{2,10},{3,11},{4,12},{5,13},{6,14},{7,15},{8,0},{9,1},... | collective-permute-start | bytes 331784 | tf_op jit(solution)/shard_map/ppermute | solution.py:257
  8.1 0.2 collective-permute-start.2
  8.4 0.0 collective-permute-start.5
  9.0 0.9 %convolution_compare_fusion.4 = pred[24,24]{1,0:T(8,128)(4,1)S(1)} fusion(s32[24]{0:T(128)} %bitcast.31), kind=kOutput, calls=%fused_computation.4 | convolution fusion | flops 29952 | bytes 672 | tf_op jit(solution)/shard_map/dot_general | solution.py:26
  10.0 6.6 %collective-permute-done.3.refs_5_ = bf16[576,512]{1,0:T(8,128)(2,1)S(1)} collective-permute-done((bf16[576,512]{1,0:T(8,128)(2,1)}, bf16[576,512]{1,0:T(8,128)(2,1)S(1)}, u32[]{:S(2)}, u32[]{:S(2)}) %collective-permute-start.3) | collective-permute-done | bytes 589856 | tf_op jit(solution)/shard_map/ppermute | solution.py:257
  16.5 0.0 collective-permute-start.4
  16.5 0.1 pad_add_fusion
  16.6 0.1 compare_select_fusion.refs_0_
  16.7 0.2 convolution_compare_fusion.2
  16.9 0.0 collective-permute-done.refs_2_
  17.0 0.6 %collective-permute-done.1.refs_3_ = bf16[96,576]{1,0:T(8,128)(2,1)S(1)} collective-permute-done((bf16[96,576]{1,0:T(8,128)(2,1)S(1)}, bf16[96,576]{1,0:T(8,128)(2,1)S(1)}, u32[]{:S(2)}, u32[]{:S(2)}) %collective-permute-start.1) | collective-permute-done | bytes 110624 | tf_op jit(solution)/shard_map/ppermute | solution.py:257
  17.6 0.0 collective-permute-done.2.refs_4_
  17.6 0.0 collective-permute-done.5.refs_6_
  17.6 0.0 copy-start
  17.6 1.1 %copy-done = bf16[1,512,576]{1,2,0:T(8,128)(2,1)S(1)} copy-done((bf16[1,512,576]{1,2,0:T(8,128)(2,1)S(1)}, bf16[1,512,576]{1,2,0:T(8,128)(2,1)}, u32[]{:S(2)}) %copy-start) | copy-done | bytes 589848
  18.7 1.4 %shard_map.73 = (f32[384,512]{1,0:T(8,128)S(1)}, f32[384,1]{1,0:T(8,128)S(1)}, f32[384,1]{1,0:T(8,128)S(1)}) custom-call(f32[2,512]{1,0:T(2,128)S(1)} %compare_select_fusion.refs_0_, bf16[96,576]{1,0:T(8,128)(2,1)S(1)} %bitcast.22, bf16[96,576]{1,0:T(8,128)(2,1)S(1)} %collective-permute-done.refs_2_, bf16[96,576]{1,0:T(8,128)(2,1)S(1)} %collective-permute-done.1.refs_3_, ...), custom_call_target="tpu_custom_call" | custom-call | tf_op jit(solution)/shard_map/pallas_call | solution.py:226
  20.1 1.1 %shard_map.74 = (f32[384,512]{1,0:T(8,128)S(1)}, f32[384,1]{1,0:T(8,128)S(1)}, f32[384,1]{1,0:T(8,128)S(1)}) custom-call(f32[1,512]{1,0:T(1,128)S(1)} %compare_select_fusion.1.refs_0_, bf16[96,576]{1,0:T(8,128)(2,1)S(1)} %bitcast.23, bf16[96,576]{1,0:T(8,128)(2,1)S(1)} %collective-permute-done.refs_2_, bf16[96,576]{1,0:T(8,128)(2,1)S(1)} %collective-permute-done.1.refs_3_, ...), custom_call_target="tpu_custom_call" | custom-call | tf_op jit(solution)/shard_map/pallas_call | solution.py:226
  21.2 0.0 collective-permute-done.4.refs_5_
  21.2 1.1 %shard_map.75 = (f32[96,512]{1,0:T(8,128)S(1)}, f32[96,1]{1,0:T(8,128)S(1)}, f32[96,1]{1,0:T(8,128)S(1)}, bf16[104,512]{1,0:T(8,128)(2,1)S(1)}, bf16[104,512]{1,...) custom-call(f32[1,512]{1,0:T(1,128)S(1)} %compare_select_fusion.2.refs_0_, bf16[96,576]{1,0:T(8,128)(2,1)S(1)} %bitcast.24, ...), custom_call_target="tpu_custom_call" | custom-call | tf_op jit(solution)/shard_map/pallas_call | solution.py:226
  22.3 3.3 %collective-permute-start.6 = (bf16[104,512]{1,0:T(8,128)(2,1)S(1)}, bf16[104,512]{1,0:T(8,128)(2,1)S(1)}, u32[]{:S(2)}, u32[]{:S(2)}) collective-permute-start(bf16[104,512]{1,0:T(8,128)(2,1)S(1)} %get-tuple-element.35), channel_id=1, source_target_pairs={{0,12},{1,13},{2,14},{3,15},{4,8},{5,9},{6,10},{7,11},{8,4},{9,5},... | collective-permute-start | bytes 319496 | tf_op jit(solution)/shard_map/ppermute | solution.py:257
  25.6 0.1 collective-permute-start.7
  25.7 1.1 %collective-permute-start.8 = (bf16[104,512]{1,0:T(8,128)(2,1)S(1)}, bf16[104,512]{1,0:T(8,128)(2,1)S(1)}, u32[]{:S(2)}, u32[]{:S(2)}) collective-permute-start(bf16[104,512]{1,0:T(8,128)(2,1)S(1)} %get-tuple-element.37), channel_id=1, source_target_pairs={{0,4},{1,5},{2,6},{3,7},{4,0},{5,1},{6,2},{7,3},{8,12},{9,13},{10,... | collective-permute-start | bytes 319496 | tf_op jit(solution)/shard_map/ppermute | solution.py:257
  26.8 0.2 fusion.2.bias_ref
  27.0 0.0 copy-start.1
  27.0 1.0 %copy-done.1 = bf16[4,512,128]{2,1,0:T(8,128)(2,1)S(1)} copy-done((bf16[4,512,128]{2,1,0:T(8,128)(2,1)S(1)}, bf16[4,512,128]{2,1,0:T(8,128)(2,1)}, u32[]{:S(2)}) %copy-start.1) | copy-done | bytes 524312
  28.1 0.0 copy-start.2
  28.1 0.8 %copy-done.2 = bf16[1,24,576]{2,1,0:T(8,128)(2,1)S(1)} copy-done((bf16[1,24,576]{2,1,0:T(8,128)(2,1)S(1)}, bf16[1,24,576]{2,1,0:T(8,128)(2,1)}, u32[]{:S(2)}) %copy-start.2) | copy-done | bytes 27672
  28.8 0.5 shard_map.76
  29.3 0.8 %collective-permute-done.6.refs_0_ = bf16[104,512]{1,0:T(8,128)(2,1)S(1)} collective-permute-done((bf16[104,512]{1,0:T(8,128)(2,1)S(1)}, bf16[104,512]{1,0:T(8,128)(2,1)S(1)}, u32[]{:S(2)}, u32[]{:S(2)}) %collective-permute-start.6) | collective-permute-done | bytes 106528 | tf_op jit(solution)/shard_map/ppermute | solution.py:257
  30.1 5.1 %collective-permute-done.7.refs_1_ = bf16[104,512]{1,0:T(8,128)(2,1)S(1)} collective-permute-done((bf16[104,512]{1,0:T(8,128)(2,1)S(1)}, bf16[104,512]{1,0:T(8,128)(2,1)S(1)}, u32[]{:S(2)}, u32[]{:S(2)}) %collective-permute-start.7) | collective-permute-done | bytes 106528 | tf_op jit(solution)/shard_map/ppermute | solution.py:257
  35.2 0.0 collective-permute-done.8.refs_2_
  35.2 4.3 %shard_map.77 = (f32[8,24,448]{2,1,0:T(8,128)S(1)}, bf16[8,24,448]{2,1,0:T(8,128)(2,1)S(1)}) custom-call(bf16[104,512]{1,0:T(8,128)(2,1)S(1)} %collective-permute-done.6.refs_0_, bf16[104,512]{1,0:T(8,128)(2,1)S(1)} %collective-permute-done.7.refs_1_, bf16[104,512]{1,0:T(8,128)(2,1)S(1)} %collective-permute-done.8.refs_2_, ...), custom_call_target="tpu_custom_call" | custom-call | tf_op jit(solution)/shard_map/pallas_call | solution.py:226
  39.6 0.1 collective-permute-start.9
  39.7 1.4 %collective-permute-done.9.got_ref = bf16[8,24,448]{2,1,0:T(8,128)(2,1)S(1)} collective-permute-done((bf16[8,24,448]{2,1,0:T(8,128)(2,1)S(1)}, bf16[8,24,448]{2,1,0:T(8,128)(2,1)S(1)}, u32[]{:S(2)}, u32[]{:S(2)}) %collective-permute-start.9) | collective-permute-done | bytes 172064 | tf_op jit(solution)/shard_map/ppermute | solution.py:257
  41.1 1.6 %collective-permute-start.10 = (bf16[4,24,448]{2,1,0:T(8,128)(2,1)S(1)}, bf16[4,24,448]{2,1,0:T(8,128)(2,1)S(1)}, u32[]{:S(2)}, u32[]{:S(2)}) collective-permute-start(bf16[4,24,448]{2,1,0:T(8,128)(2,1)S(1)} %get-tuple-element.48), channel_id=1, source_target_pairs={{0,2},{1,3},{2,0},{3,1},{4,6},{5,7},{6,4},{7,5},{8,10},{9,11},{10,... | collective-permute-start | bytes 258056 | tf_op jit(solution)/shard_map/ppermute | solution.py:257
  42.7 3.3 %collective-permute-done.10.got_ref = bf16[4,24,448]{2,1,0:T(8,128)(2,1)S(1)} collective-permute-done((bf16[4,24,448]{2,1,0:T(8,128)(2,1)S(1)}, bf16[4,24,448]{2,1,0:T(8,128)(2,1)S(1)}, u32[]{:S(2)}, u32[]{:S(2)}) %collective-permute-start.10) | collective-permute-done | bytes 86048 | tf_op jit(solution)/shard_map/ppermute | solution.py:257
  46.1 2.6 %collective-permute-start.11 = (bf16[24,448]{1,0:T(8,128)(2,1)S(1)}, bf16[24,448]{1,0:T(8,128)(2,1)S(1)}, u32[]{:S(2)}, u32[]{:S(2)}) collective-permute-start(bf16[24,448]{1,0:T(8,128)(2,1)S(1)} %get-tuple-element.50), channel_id=1, source_target_pairs={{0,12},{1,13},{2,14},{3,15},{4,8},{5,9},{6,10},{7,11},{8,4},{9,5},... | collective-permute-start | bytes 64520 | tf_op jit(solution)/shard_map/ppermute | solution.py:257
  48.6 0.0 collective-permute-start.12
  48.6 1.9 %collective-permute-start.13 = (bf16[24,448]{1,0:T(8,128)(2,1)S(1)}, bf16[24,448]{1,0:T(8,128)(2,1)S(1)}, u32[]{:S(2)}, u32[]{:S(2)}) collective-permute-start(bf16[24,448]{1,0:T(8,128)(2,1)S(1)} %get-tuple-element.52), channel_id=1, source_target_pairs={{0,4},{1,5},{2,6},{3,7},{4,0},{5,1},{6,2},{7,3},{8,12},{9,13},{10,... | collective-permute-start | bytes 64520 | tf_op jit(solution)/shard_map/ppermute | solution.py:257
  50.5 1.2 %collective-permute-done.11 = bf16[24,448]{1,0:T(8,128)(2,1)S(1)} collective-permute-done((bf16[24,448]{1,0:T(8,128)(2,1)S(1)}, bf16[24,448]{1,0:T(8,128)(2,1)S(1)}, u32[]{:S(2)}, u32[]{:S(2)}) %collective-permute-start.11) | collective-permute-done | bytes 21536 | tf_op jit(solution)/shard_map/ppermute | solution.py:257
  51.7 1.6 %collective-permute-done.12 = bf16[24,448]{1,0:T(8,128)(2,1)S(1)} collective-permute-done((bf16[24,448]{1,0:T(8,128)(2,1)S(1)}, bf16[24,448]{1,0:T(8,128)(2,1)S(1)}, u32[]{:S(2)}, u32[]{:S(2)}) %collective-permute-start.12) | collective-permute-done | bytes 21536 | tf_op jit(solution)/shard_map/ppermute | solution.py:257
  53.3 0.0 collective-permute-done.13
  53.3 0.6 %add_convert_fusion = bf16[24,448]{1,0:T(8,128)(2,1)} fusion(bf16[24,448]{1,0:T(8,128)(2,1)S(1)} %collective-permute-done.13, bf16[24,448]{1,0:T(8,128)(2,1)S(1)} %collective-permute-done.12, f32[24,448]{1,0:T(8,128)S(1)} %get-tuple-element.49, bf16[24,448]{1,0:T(8,128)(2,1)S(1)} %collective-permute-done.11), kind=kLoop, calls=%fused_computation.8 | loop fusion | flops 75264 | bytes 129024 | tf_op jit(solution)/shard_map/convert_element_type | solution.py:317
  (4 shorter events, 0.1 us)
Async XLA Ops:
  0.0 16.5 %collective-permute-start.3 = (bf16[576,512]{1,0:T(8,128)(2,1)}, bf16[576,512]{1,0:T(8,128)(2,1)S(1)}, u32[]{:S(2)}, u32[]{:S(2)}) collective-permute-start(bf16[576,512]{1,0:T(8,128)(2,1)} %bitcast.26), channel_id=1, source_target_pairs={{0,2},{1,3},{2,0},{3,1},{4,6},{5,7},{6,4},{7,5},{8,10},{9,11},{10,... | collective-permute-start | bytes 1769480 | tf_op jit(solution)/shard_map/ppermute | solution.py:257
  3.9 13.0 %collective-permute-start = (bf16[96,576]{1,0:T(8,128)(2,1)S(1)}, bf16[96,576]{1,0:T(8,128)(2,1)S(1)}, u32[]{:S(2)}, u32[]{:S(2)}) collective-permute-start(bf16[96,576]{1,0:T(8,128)(2,1)S(1)} %bitcast.19), channel_id=1, source_target_pairs={{0,4},{1,5},{2,6},{3,7},{4,0},{5,1},{6,2},{7,3},{8,12},{9,13},{10,... | collective-permute-start | bytes 331784 | tf_op jit(solution)/shard_map/ppermute | solution.py:257
  5.6 12.0 %collective-permute-start.1 = (bf16[96,576]{1,0:T(8,128)(2,1)S(1)}, bf16[96,576]{1,0:T(8,128)(2,1)S(1)}, u32[]{:S(2)}, u32[]{:S(2)}) collective-permute-start(bf16[96,576]{1,0:T(8,128)(2,1)S(1)} %bitcast.20), channel_id=1, source_target_pairs={{0,8},{1,9},{2,10},{3,11},{4,12},{5,13},{6,14},{7,15},{8,0},{9,1},... | collective-permute-start | bytes 331784 | tf_op jit(solution)/shard_map/ppermute | solution.py:257
  8.1 9.4 %collective-permute-start.2 = (bf16[96,576]{1,0:T(8,128)(2,1)S(1)}, bf16[96,576]{1,0:T(8,128)(2,1)S(1)}, u32[]{:S(2)}, u32[]{:S(2)}) collective-permute-start(bf16[96,576]{1,0:T(8,128)(2,1)S(1)} %bitcast.21), channel_id=1, source_target_pairs={{0,12},{1,13},{2,14},{3,15},{4,8},{5,9},{6,10},{7,11},{8,4},{9,5},... | collective-permute-start | bytes 331784 | tf_op jit(solution)/shard_map/ppermute | solution.py:257
  8.4 9.2 %collective-permute-start.5 = (bf16[576,512]{1,0:T(8,128)(2,1)}, bf16[576,512]{1,0:T(8,128)(2,1)S(1)}, u32[]{:S(2)}, u32[]{:S(2)}) collective-permute-start(bf16[576,512]{1,0:T(8,128)(2,1)} %bitcast.27), channel_id=1, source_target_pairs={{0,1},{1,0},{2,3},{3,2},{4,5},{5,4},{6,7},{7,6},{8,9},{9,8},{10,11... | collective-permute-start | bytes 1769480 | tf_op jit(solution)/shard_map/ppermute | solution.py:257
  16.5 4.7 %collective-permute-start.4 = (bf16[576,512]{1,0:T(8,128)(2,1)S(1)}, bf16[576,512]{1,0:T(8,128)(2,1)S(1)}, u32[]{:S(2)}, u32[]{:S(2)}) collective-permute-start(bf16[576,512]{1,0:T(8,128)(2,1)S(1)} %collective-permute-done.3.refs_5_), channel_id=1, source_target_pairs={{0,1},{1,0},{2,3},{3,2},{4,5},{5,4},{6,7},{7,6},{8,9},{9,8},{10,11... | collective-permute-start | bytes 1769480 | tf_op jit(solution)/shard_map/ppermute | solution.py:257
  17.6 1.1 %copy-start = (bf16[1,512,576]{1,2,0:T(8,128)(2,1)S(1)}, bf16[1,512,576]{1,2,0:T(8,128)(2,1)}, u32[]{:S(2)}) copy-start(bf16[1,512,576]{1,2,0:T(8,128)(2,1)} %param.8) | copy-start | bytes 1769476
  22.3 7.8 %collective-permute-start.6 = (bf16[104,512]{1,0:T(8,128)(2,1)S(1)}, bf16[104,512]{1,0:T(8,128)(2,1)S(1)}, u32[]{:S(2)}, u32[]{:S(2)}) collective-permute-start(bf16[104,512]{1,0:T(8,128)(2,1)S(1)} %get-tuple-element.35), channel_id=1, source_target_pairs={{0,12},{1,13},{2,14},{3,15},{4,8},{5,9},{6,10},{7,11},{8,4},{9,5},... | collective-permute-start | bytes 319496 | tf_op jit(solution)/shard_map/ppermute | solution.py:257
  25.6 9.6 %collective-permute-start.7 = (bf16[104,512]{1,0:T(8,128)(2,1)S(1)}, bf16[104,512]{1,0:T(8,128)(2,1)S(1)}, u32[]{:S(2)}, u32[]{:S(2)}) collective-permute-start(bf16[104,512]{1,0:T(8,128)(2,1)S(1)} %get-tuple-element.36), channel_id=1, source_target_pairs={{0,8},{1,9},{2,10},{3,11},{4,12},{5,13},{6,14},{7,15},{8,0},{9,1},... | collective-permute-start | bytes 319496 | tf_op jit(solution)/shard_map/ppermute | solution.py:257
  25.7 9.5 %collective-permute-start.8 = (bf16[104,512]{1,0:T(8,128)(2,1)S(1)}, bf16[104,512]{1,0:T(8,128)(2,1)S(1)}, u32[]{:S(2)}, u32[]{:S(2)}) collective-permute-start(bf16[104,512]{1,0:T(8,128)(2,1)S(1)} %get-tuple-element.37), channel_id=1, source_target_pairs={{0,4},{1,5},{2,6},{3,7},{4,0},{5,1},{6,2},{7,3},{8,12},{9,13},{10,... | collective-permute-start | bytes 319496 | tf_op jit(solution)/shard_map/ppermute | solution.py:257
  27.0 1.0 %copy-start.1 = (bf16[4,512,128]{2,1,0:T(8,128)(2,1)S(1)}, bf16[4,512,128]{2,1,0:T(8,128)(2,1)}, u32[]{:S(2)}) copy-start(bf16[4,512,128]{2,1,0:T(8,128)(2,1)} %up_from.1) | copy-start | bytes 1572868
  28.1 0.8 %copy-start.2 = (bf16[1,24,576]{2,1,0:T(8,128)(2,1)S(1)}, bf16[1,24,576]{2,1,0:T(8,128)(2,1)}, u32[]{:S(2)}) copy-start(bf16[1,24,576]{2,1,0:T(8,128)(2,1)} %param.9) | copy-start | bytes 82948
  39.6 1.5 %collective-permute-start.9 = (bf16[8,24,448]{2,1,0:T(8,128)(2,1)S(1)}, bf16[8,24,448]{2,1,0:T(8,128)(2,1)S(1)}, u32[]{:S(2)}, u32[]{:S(2)}) collective-permute-start(bf16[8,24,448]{2,1,0:T(8,128)(2,1)S(1)} %get-tuple-element.46), channel_id=1, source_target_pairs={{0,1},{1,0},{2,3},{3,2},{4,5},{5,4},{6,7},{7,6},{8,9},{9,8},{10,11... | collective-permute-start | bytes 516104 | tf_op jit(solution)/shard_map/ppermute | solution.py:257
  41.1 4.9 %collective-permute-start.10 = (bf16[4,24,448]{2,1,0:T(8,128)(2,1)S(1)}, bf16[4,24,448]{2,1,0:T(8,128)(2,1)S(1)}, u32[]{:S(2)}, u32[]{:S(2)}) collective-permute-start(bf16[4,24,448]{2,1,0:T(8,128)(2,1)S(1)} %get-tuple-element.48), channel_id=1, source_target_pairs={{0,2},{1,3},{2,0},{3,1},{4,6},{5,7},{6,4},{7,5},{8,10},{9,11},{10,... | collective-permute-start | bytes 258056 | tf_op jit(solution)/shard_map/ppermute | solution.py:257
  46.1 5.7 %collective-permute-start.11 = (bf16[24,448]{1,0:T(8,128)(2,1)S(1)}, bf16[24,448]{1,0:T(8,128)(2,1)S(1)}, u32[]{:S(2)}, u32[]{:S(2)}) collective-permute-start(bf16[24,448]{1,0:T(8,128)(2,1)S(1)} %get-tuple-element.50), channel_id=1, source_target_pairs={{0,12},{1,13},{2,14},{3,15},{4,8},{5,9},{6,10},{7,11},{8,4},{9,5},... | collective-permute-start | bytes 64520 | tf_op jit(solution)/shard_map/ppermute | solution.py:257
  48.6 4.7 %collective-permute-start.12 = (bf16[24,448]{1,0:T(8,128)(2,1)S(1)}, bf16[24,448]{1,0:T(8,128)(2,1)S(1)}, u32[]{:S(2)}, u32[]{:S(2)}) collective-permute-start(bf16[24,448]{1,0:T(8,128)(2,1)S(1)} %get-tuple-element.51), channel_id=1, source_target_pairs={{0,8},{1,9},{2,10},{3,11},{4,12},{5,13},{6,14},{7,15},{8,0},{9,1},... | collective-permute-start | bytes 64520 | tf_op jit(solution)/shard_map/ppermute | solution.py:257
  48.6 4.7 %collective-permute-start.13 = (bf16[24,448]{1,0:T(8,128)(2,1)S(1)}, bf16[24,448]{1,0:T(8,128)(2,1)S(1)}, u32[]{:S(2)}, u32[]{:S(2)}) collective-permute-start(bf16[24,448]{1,0:T(8,128)(2,1)S(1)} %get-tuple-element.52), channel_id=1, source_target_pairs={{0,4},{1,5},{2,6},{3,7},{4,0},{5,1},{6,2},{7,3},{8,12},{9,13},{10,... | collective-permute-start | bytes 64520 | tf_op jit(solution)/shard_map/ppermute | solution.py:257
where the time goes:
time: 54.3 us; the launch traced here: 54 us
  waiting for transfers between devices  20.8 us (38%)
  starting transfers between devices  18 us (33%)
  Pallas kernels  8.47 us (16%)
  local copies, waits for them, and re-layouts  3.78 us (7%)
  matrix products  1.41 us (3%)
  other arithmetic  0.79 us (1%)
  between operations  0.76 us (1%)
    ppermute x14, waiting for transfers between devices, swap(): return lax.ppermute(value, 'ctx', [(i, i ^ bits) for i in range(count)])  20.8 us
    ppermute x14, starting transfers between devices, swap(): return lax.ppermute(value, 'ctx', [(i, i ^ bits) for i in range(count)])  18 us
    pallas_call x7, Pallas kernels, call(): pl.pallas_call(kernel, out_shape=outs, in_specs=specs or [pl.BlockSpec()...  8.47 us
    unnamed x6, local copies, waits for them, and re-layouts  2.86 us
    dot_general x3, matrix products, tree_bias(): grown = jnp.dot(reach, reach, preferred_element_type=jnp.float32)  1.41 us
  transfers between devices with their start and end apart: 14, of which 8 were waited for; matrix products, arithmetic and copies ran while one was open for 5% of the time, Pallas kernels for 5%

commit v1 on v0

--- a/solution.py
+++ b/solution.py
@@ -16,19 +16,6 @@
 PACK_ROWS = 8
 
 
-def tree_bias(parents):
-    drafts = parents.shape[0]
-    order = jnp.arange(drafts, dtype=jnp.int32)
-    step = (parents[:, None] == order[None, :]) | (order[:, None] == order[None, :])
-    reach = step.astype(jnp.bfloat16)
-    covered = 1
-    while covered < drafts:
-        grown = jnp.dot(reach, reach, preferred_element_type=jnp.float32)
-        reach = (grown > 0.5).astype(jnp.bfloat16)
-        covered *= 2
-    return jnp.where(reach > 0.5, 0.0, neg_fill).astype(jnp.float32)
-
-
 NT = (((1,), (1,)), ((), ()))
 
 
@@ -37,12 +24,45 @@
     return weights, jnp.sum(weights.astype(jnp.float32), axis=1, keepdims=True)
 
 
-def draft_kernel(q_ref, keys_ref, bias_ref, up_from, numer_ref, top_ref, total_ref, up_ref):
+def as_row(column):
+    count = column.shape[0]
+    eye = lax.broadcasted_iota(jnp.int32, (count, count), 0) == lax.broadcasted_iota(
+        jnp.int32, (count, count), 1
+    )
+    return jnp.sum(jnp.where(eye, column, 0.0), axis=0, keepdims=True)
+
+
+def as_column(row):
+    count = row.shape[1]
+    eye = lax.broadcasted_iota(jnp.int32, (count, count), 0) == lax.broadcasted_iota(
+        jnp.int32, (count, count), 1
+    )
+    return jnp.sum(jnp.where(eye, row, 0.0), axis=1, keepdims=True)
+
+
+def tree_bias(parents):
+    drafts = parents.shape[1]
+    order = lax.broadcasted_iota(jnp.int32, (drafts, drafts), 1)
+    self_order = lax.broadcasted_iota(jnp.int32, (drafts, drafts), 0)
+    parent = as_column(parents.astype(jnp.float32)).astype(jnp.int32)
+    reach = jnp.where((parent == order) | (self_order == order), 1.0, 0.0)
+    covered = 1
+    while covered < drafts:
+        step = reach.astype(jnp.bfloat16)
+        grown = jnp.dot(step, step, preferred_element_type=jnp.float32)
+        reach = jnp.where(grown > 0.5, 1.0, 0.0)
+        covered *= 2
+    return jnp.where(reach > 0.5, 0.0, neg_fill)
+
+
+def draft_kernel(
+    q_ref, keys_ref, parents_ref, up_from, numer_ref, top_ref, total_ref, up_ref
+):
     up_ref[...] = up_from[...]
     latent = numer_ref.shape[1]
     keys = keys_ref[...]
-    repeats = q_ref.shape[0] // bias_ref.shape[0]
-    bias = jnp.concatenate([bias_ref[...]] * repeats, axis=0)
+    repeats = q_ref.shape[0] // keys.shape[0]
+    bias = jnp.concatenate([tree_bias(parents_ref[...])] * repeats, axis=0)
     scores = lax.dot_general(q_ref[...], keys, NT, preferred_element_type=jnp.float32)
     masked = scores * log2_scale + bias
     top = jnp.max(masked, axis=1, keepdims=True)
@@ -96,22 +116,6 @@
     total_ref[...] = total
 
 
-def as_row(column):
-    count = column.shape[0]
-    eye = lax.broadcasted_iota(jnp.int32, (count, count), 0) == lax.broadcasted_iota(
-        jnp.int32, (count, count), 1
-    )
-    return jnp.sum(jnp.where(eye, column, 0.0), axis=0, keepdims=True)
-
-
-def as_column(row):
-    count = row.shape[1]
-    eye = lax.broadcasted_iota(jnp.int32, (count, count), 0) == lax.broadcasted_iota(
-        jnp.int32, (count, count), 1
-    )
-    return jnp.sum(jnp.where(eye, row, 0.0), axis=1, keepdims=True)
-
-
 def pieces(row):
     high = row.astype(jnp.bfloat16).astype(jnp.float32)
     rest = row - high
@@ -143,20 +147,12 @@
 def project_kernel(peers, *refs):
     state_refs, refs = refs[: peers - 1], refs[peers - 1 :]
     full_refs, refs = refs[:6], refs[6:]
-    up_ref, proj_from, keep_ref, send_ref, flat_ref, proj_ref, done = refs
+    up_ref, proj_ref, keep_ref, send_ref, flat_ref = refs
     each = full_refs[0].shape[0]
     heads, _, width = up_ref.shape
     columns = keep_ref.shape[2]
     span = math.lcm(2 * columns, 128)
     blocks = proj_ref.shape[1] // span
-    copies = []
-    for block in range(blocks):
-        strip = (slice(None), pl.ds(block * span, span))
-        copies.append(
-            pltpu.make_async_copy(proj_from.at[strip], proj_ref.at[strip], done.at[block])
-        )
-    for copy in copies:
-        copy.start()
     drafts = each // heads
     numers = [full_refs[0][...], full_refs[3][...]]
     tops = [full_refs[1][...], full_refs[4][...]]
@@ -185,7 +181,6 @@
     flat = flat_ref[...]
     first_core = lax.rem(lax.axis_index("ctx"), 2) == 0
     for block in range(blocks):
-        copies[block].wait()
         part = jnp.dot(
             flat,
             proj_ref[:, block * span : (block + 1) * span],
@@ -222,11 +217,12 @@
     own_ref[...] = both(outer)
 
 
-def call(kernel, outs, values, specs=None, scratch=(), limit=24):
+def call(kernel, outs, values, specs=None, out_specs=None, scratch=(), limit=24):
     return pl.pallas_call(
         kernel,
         out_shape=outs,
         in_specs=specs or [pl.BlockSpec() for _ in values],
+        out_specs=out_specs or [pl.BlockSpec() for _ in outs],
         scratch_shapes=list(scratch),
         compiler_params=pltpu.CompilerParams(vmem_limit_bytes=limit << 20),
     )(*values)
@@ -260,15 +256,22 @@
     keys_across = swap(keys_own, 2)
     keys_core = swap(keys_own, 1)
     own_rows = jnp.transpose(queries[0], (1, 0, 2)).reshape(each, width)
-    rows = [own_rows] + [swap(own_rows, inner * peer) for peer in range(outer - 1, 0, -1)][::-1]
+    rows = {0: own_rows}
+    bit = outer // 2
+    while bit:
+        for peer in list(rows):
+            rows[peer ^ bit] = swap(rows[peer], inner * bit)
+        bit //= 2
+    rows = [rows[peer] for peer in range(outer)]
     keys_far = swap(keys_across, 1)
 
     state_shape = (shaped(outer * each, latent), shaped(outer * each, 1), shaped(outer * each, 1))
     own_shape = (shaped(each, latent), shaped(each, 1), shaped(each, 1))
+    proj_here = jnp.where(lengths[0] > -1, out_proj, jnp.zeros_like(out_proj))
     *drafted, up_here = call(
         draft_kernel,
         own_shape + (shaped(*value_up.shape, dtype=bf16),),
-        (own_rows, draft_latent[0], tree_bias(parents[0]), value_up),
+        (own_rows, draft_latent[0], parents, value_up),
     )
     state = call(
         lambda *refs: first_kernel(outer, *refs),
@@ -291,14 +294,8 @@
     keep, send = call(
         lambda *refs: project_kernel(outer, *refs),
         (shaped(chips, drafts, columns), shaped(chips, drafts, columns, dtype=bf16)),
-        (*got, *whole, *drafted, up_here, out_proj),
-        specs=[pl.BlockSpec()] * (outer + 6) + [pl.BlockSpec(memory_space=pl.ANY)],
-        scratch=[
-            pltpu.VMEM((drafts, heads_here * value_up.shape[2]), bf16),
-            pltpu.VMEM(out_proj.shape, bf16),
-            pltpu.SemaphoreType.DMA((out_proj.shape[1] // math.lcm(2 * columns, 128),)),
-        ],
-        limit=50,
+        (*got, *whole, *drafted, up_here, proj_here),
+        scratch=[pltpu.VMEM((drafts, heads_here * value_up.shape[2]), bf16)],
     )
     stay, send = call(
         pair_kernel,

time: 54.3 us -> 65.3 us (1.20)
  waiting for transfers between devices: 20.8 us -> 33 us
  other arithmetic: 0.79 us -> 4.35 us
  Pallas kernels: 8.47 us -> 6.33 us
  local copies, waits for them, and re-layouts: 3.78 us -> 1.99 us
  matrix products: 1.41 us -> 0 us
  starting transfers between devices: 18 us -> 18.7 us
    ppermute x14, waiting for transfers between devices: 20.8 us -> 33 us  [swap(): return lax.ppermute(value, 'ctx', [(i, i ^ bits) for i in range(count)])]
    select_n x0 -> x1, other arithmetic: none -> 3.56 us  [on_device(): proj_here = jnp.where(lengths[0] > -1, out_proj, jnp.zeros_like(out_proj))]
    pallas_call x7, Pallas kernels: 8.47 us -> 6.33 us  [call(): pl.pallas_call(kernel, out_shape=outs, in_specs=specs or [pl.BlockSpec()...]
    unnamed x6 -> x8, local copies, waits for them, and re-layouts: 2.86 us -> 1.08 us
    dot_general x3 -> x0, matrix products: 1.41 us -> none  [tree_bias(): grown = jnp.dot(reach, reach, preferred_element_type=jnp.float32)]
    ppermute x14, starting transfers between devices: 18 us -> 18.7 us  [swap(): return lax.ppermute(value, 'ctx', [(i, i ^ bits) for i in range(count)])]
  transfers between devices with their start and end apart: 14 -> 14, of which waited for: 8 -> 8; matrix products, arithmetic and copies ran while one was open for 5% -> 7% of each run, Pallas kernels for 5% -> 5%
where the time goes in v1:
time: 65.3 us; the launch traced here: 65.1 us
  waiting for transfers between devices  33 us (51%)
  starting transfers between devices  18.7 us (29%)
  Pallas kernels  6.33 us (10%)
  other arithmetic  4.35 us (7%)
  local copies, waits for them, and re-layouts  1.99 us (3%)
  between operations  0.77 us (1%)
    ppermute x14, waiting for transfers between devices, swap(): return lax.ppermute(value, 'ctx', [(i, i ^ bits) for i in range(count)])  33 us
    ppermute x14, starting transfers between devices, swap(): return lax.ppermute(value, 'ctx', [(i, i ^ bits) for i in range(count)])  18.7 us
    pallas_call x7, Pallas kernels, call(): pl.pallas_call(kernel, out_shape=outs, in_specs=specs or [pl.BlockSpec()...  6.33 us
    select_n x1, other arithmetic, on_device(): proj_here = jnp.where(lengths[0] > -1, out_proj, jnp.zeros_like(out_proj))  3.56 us
  transfers between devices with their start and end apart: 14, of which 8 were waited for; matrix products, arithmetic and copies ran while one was open for 7% of the time, Pallas kernels for 5%

profile of v1, /device:TPU:0, one launch (start us, length us, event | category | flops | bytes accessed | tf_op | source)
XLA Modules:
  0.0 65.1 jit_solution(15839689914961120129)
XLA Ops:
  0.0 3.0 %collective-permute-start.3 = (bf16[576,512]{1,0:T(8,128)(2,1)}, bf16[576,512]{1,0:T(8,128)(2,1)S(1)}, u32[]{:S(2)}, u32[]{:S(2)}) collective-permute-start(bf16[576,512]{1,0:T(8,128)(2,1)} %bitcast.21), channel_id=1, source_target_pairs={{0,2},{1,3},{2,0},{3,1},{4,6},{5,7},{6,4},{7,5},{8,10},{9,11},{10,... | collective-permute-start | bytes 1769480 | tf_op jit(solution)/shard_map/ppermute | solution.py:253
  3.0 0.0 collective-permute-start.5
  3.0 13.5 %collective-permute-done.3.refs_5_ = bf16[576,512]{1,0:T(8,128)(2,1)S(1)} collective-permute-done((bf16[576,512]{1,0:T(8,128)(2,1)}, bf16[576,512]{1,0:T(8,128)(2,1)S(1)}, u32[]{:S(2)}, u32[]{:S(2)}) %collective-permute-start.3) | collective-permute-done | bytes 589856 | tf_op jit(solution)/shard_map/ppermute | solution.py:253
  16.5 0.0 collective-permute-start.4
  16.5 0.9 %copy.8 = bf16[4,24,576]{2,1,0:T(8,128)(2,1)S(1)} copy(bf16[4,24,576]{2,0,1:T(4,128)(2,1)} %bitcast.25) | data formatting | bytes 221184 | tf_op jit(solution)/shard_map/transpose | solution.py:258
  17.5 2.9 %collective-permute-start.1 = (bf16[96,576]{1,0:T(8,128)(2,1)S(1)}, bf16[96,576]{1,0:T(8,128)(2,1)S(1)}, u32[]{:S(2)}, u32[]{:S(2)}) collective-permute-start(bf16[96,576]{1,0:T(8,128)(2,1)S(1)} %bitcast.15), channel_id=1, source_target_pairs={{0,8},{1,9},{2,10},{3,11},{4,12},{5,13},{6,14},{7,15},{8,0},{9,1},... | collective-permute-start | bytes 331784 | tf_op jit(solution)/shard_map/ppermute | solution.py:253
  20.3 1.6 %collective-permute-start = (bf16[96,576]{1,0:T(8,128)(2,1)S(1)}, bf16[96,576]{1,0:T(8,128)(2,1)S(1)}, u32[]{:S(2)}, u32[]{:S(2)}) collective-permute-start(bf16[96,576]{1,0:T(8,128)(2,1)S(1)} %bitcast.16), channel_id=1, source_target_pairs={{0,4},{1,5},{2,6},{3,7},{4,0},{5,1},{6,2},{7,3},{8,12},{9,13},{10,... | collective-permute-start | bytes 331784 | tf_op jit(solution)/shard_map/ppermute | solution.py:253
  22.6 0.1 pad_add_fusion
  22.6 0.1 compare_select_fusion.refs_0_
  22.7 4.3 %collective-permute-done.1.refs_3_ = bf16[96,576]{1,0:T(8,128)(2,1)S(1)} collective-permute-done((bf16[96,576]{1,0:T(8,128)(2,1)S(1)}, bf16[96,576]{1,0:T(8,128)(2,1)S(1)}, u32[]{:S(2)}, u32[]{:S(2)}) %collective-permute-start.1) | collective-permute-done | bytes 110624 | tf_op jit(solution)/shard_map/ppermute | solution.py:253
  27.1 0.6 collective-permute-start.2
  27.7 0.0 collective-permute-done.refs_2_
  27.7 4.3 %collective-permute-done.2.refs_4_ = bf16[96,576]{1,0:T(8,128)(2,1)S(1)} collective-permute-done((bf16[96,576]{1,0:T(8,128)(2,1)S(1)}, bf16[96,576]{1,0:T(8,128)(2,1)S(1)}, u32[]{:S(2)}, u32[]{:S(2)}) %collective-permute-start.2) | collective-permute-done | bytes 110624 | tf_op jit(solution)/shard_map/ppermute | solution.py:253
  32.0 0.0 collective-permute-done.5.refs_6_
  32.0 0.0 copy-start
  32.0 1.1 %copy-done = bf16[1,512,576]{1,2,0:T(8,128)(2,1)S(1)} copy-done((bf16[1,512,576]{1,2,0:T(8,128)(2,1)S(1)}, bf16[1,512,576]{1,2,0:T(8,128)(2,1)}, u32[]{:S(2)}) %copy-start) | copy-done | bytes 589848
  33.1 1.4 %shard_map.73 = (f32[384,512]{1,0:T(8,128)S(1)}, f32[384,1]{1,0:T(8,128)S(1)}, f32[384,1]{1,0:T(8,128)S(1)}) custom-call(f32[2,512]{1,0:T(2,128)S(1)} %compare_select_fusion.refs_0_, bf16[96,576]{1,0:T(8,128)(2,1)S(1)} %bitcast.17, bf16[96,576]{1,0:T(8,128)(2,1)S(1)} %collective-permute-done.refs_2_, bf16[96,576]{1,0:T(8,128)(2,1)S(1)} %collective-permute-done.1.refs_3_, ...), custom_call_target="tpu_custom_call" | custom-call | tf_op jit(solution)/shard_map/pallas_call | solution.py:221
  34.5 1.1 %shard_map.74 = (f32[384,512]{1,0:T(8,128)S(1)}, f32[384,1]{1,0:T(8,128)S(1)}, f32[384,1]{1,0:T(8,128)S(1)}) custom-call(f32[1,512]{1,0:T(1,128)S(1)} %compare_select_fusion.1.refs_0_, bf16[96,576]{1,0:T(8,128)(2,1)S(1)} %bitcast.18, bf16[96,576]{1,0:T(8,128)(2,1)S(1)} %collective-permute-done.refs_2_, bf16[96,576]{1,0:T(8,128)(2,1)S(1)} %collective-permute-done.1.refs_3_, ...), custom_call_target="tpu_custom_call" | custom-call | tf_op jit(solution)/shard_map/pallas_call | solution.py:221
  35.6 0.0 collective-permute-done.4.refs_5_
  35.6 1.1 %shard_map.75 = (f32[96,512]{1,0:T(8,128)S(1)}, f32[96,1]{1,0:T(8,128)S(1)}, f32[96,1]{1,0:T(8,128)S(1)}, bf16[104,512]{1,0:T(8,128)(2,1)S(1)}, bf16[104,512]{1,...) custom-call(f32[1,512]{1,0:T(1,128)S(1)} %compare_select_fusion.2.refs_0_, bf16[96,576]{1,0:T(8,128)(2,1)S(1)} %bitcast.19, ...), custom_call_target="tpu_custom_call" | custom-call | tf_op jit(solution)/shard_map/pallas_call | solution.py:221
  36.7 3.8 %collective-permute-start.6 = (bf16[104,512]{1,0:T(8,128)(2,1)S(1)}, bf16[104,512]{1,0:T(8,128)(2,1)S(1)}, u32[]{:S(2)}, u32[]{:S(2)}) collective-permute-start(bf16[104,512]{1,0:T(8,128)(2,1)S(1)} %get-tuple-element.35), channel_id=1, source_target_pairs={{0,12},{1,13},{2,14},{3,15},{4,8},{5,9},{6,10},{7,11},{8,4},{9,5},... | collective-permute-start | bytes 319496 | tf_op jit(solution)/shard_map/ppermute | solution.py:253
  40.6 0.0 collective-permute-start.7
  40.6 0.0 copy-start.1
  40.6 0.0 copy-start.2
  40.6 0.0 copy-start.3
  40.6 0.6 collective-permute-start.8
  41.2 3.6 %broadcast_select_fusion.refs_10_ = bf16[512,7168]{1,0:T(8,128)(2,1)S(1)} fusion(bf16[512,7168]{1,0:T(8,128)(2,1)} %param.13, pred[]{:T(512)S(6)} %gt.3), kind=kLoop, calls=%fused_computation | loop fusion | flops 3670016 | bytes 14680065 | tf_op jit(solution)/shard_map/jit(_where)/select_n | solution.py:270
  44.8 0.0 copy-done.1
  44.8 0.0 copy-done.2
  44.8 0.0 copy-done.3
  44.8 0.9 %shard_map.76 = (f32[96,512]{1,0:T(8,128)S(1)}, f32[96,1]{1,0:T(8,128)S(1)}, f32[96,1]{1,0:T(8,128)S(1)}, bf16[4,512,128]{2,1,0:T(8,128)(2,1)S(1)}) custom-call(bf16[96,576]{1,0:T(8,128)(2,1)S(1)} %bitcast.20, bf16[24,576]{1,0:T(8,128)(2,1)S(1)} %bitcast.24, s32[1,24]{1,0:T(1,128)S(1)} %copy-done.3, bf16[4,512,128]{2,1,0:T(8,128)(2,1)S(1)} %copy-done.1), custom_call_target="tpu_custom_call" | custom-call | tf_op jit(solution)/shard_map/pallas_call | solution.py:221
  45.8 0.0 collective-permute-done.6.refs_0_
  45.8 3.1 %collective-permute-done.7.refs_1_ = bf16[104,512]{1,0:T(8,128)(2,1)S(1)} collective-permute-done((bf16[104,512]{1,0:T(8,128)(2,1)S(1)}, bf16[104,512]{1,0:T(8,128)(2,1)S(1)}, u32[]{:S(2)}, u32[]{:S(2)}) %collective-permute-start.7) | collective-permute-done | bytes 106528 | tf_op jit(solution)/shard_map/ppermute | solution.py:253
  48.9 0.0 collective-permute-done.8.refs_2_
  48.9 1.7 %shard_map.77 = (f32[8,24,448]{2,1,0:T(8,128)S(1)}, bf16[8,24,448]{2,1,0:T(8,128)(2,1)S(1)}) custom-call(bf16[104,512]{1,0:T(8,128)(2,1)S(1)} %collective-permute-done.6.refs_0_, bf16[104,512]{1,0:T(8,128)(2,1)S(1)} %collective-permute-done.7.refs_1_, bf16[104,512]{1,0:T(8,128)(2,1)S(1)} %collective-permute-done.8.refs_2_, ...), custom_call_target="tpu_custom_call" | custom-call | tf_op jit(solution)/shard_map/pallas_call | solution.py:221
  50.6 0.1 collective-permute-start.9
  50.7 1.4 %collective-permute-done.9.got_ref = bf16[8,24,448]{2,1,0:T(8,128)(2,1)S(1)} collective-permute-done((bf16[8,24,448]{2,1,0:T(8,128)(2,1)S(1)}, bf16[8,24,448]{2,1,0:T(8,128)(2,1)S(1)}, u32[]{:S(2)}, u32[]{:S(2)}) %collective-permute-start.9) | collective-permute-done | bytes 172064 | tf_op jit(solution)/shard_map/ppermute | solution.py:253
  52.1 1.6 %collective-permute-start.10 = (bf16[4,24,448]{2,1,0:T(8,128)(2,1)S(1)}, bf16[4,24,448]{2,1,0:T(8,128)(2,1)S(1)}, u32[]{:S(2)}, u32[]{:S(2)}) collective-permute-start(bf16[4,24,448]{2,1,0:T(8,128)(2,1)S(1)} %get-tuple-element.48), channel_id=1, source_target_pairs={{0,2},{1,3},{2,0},{3,1},{4,6},{5,7},{6,4},{7,5},{8,10},{9,11},{10,... | collective-permute-start | bytes 258056 | tf_op jit(solution)/shard_map/ppermute | solution.py:253
  53.7 3.3 %collective-permute-done.10.got_ref = bf16[4,24,448]{2,1,0:T(8,128)(2,1)S(1)} collective-permute-done((bf16[4,24,448]{2,1,0:T(8,128)(2,1)S(1)}, bf16[4,24,448]{2,1,0:T(8,128)(2,1)S(1)}, u32[]{:S(2)}, u32[]{:S(2)}) %collective-permute-start.10) | collective-permute-done | bytes 86048 | tf_op jit(solution)/shard_map/ppermute | solution.py:253
  57.1 2.7 %collective-permute-start.11 = (bf16[24,448]{1,0:T(8,128)(2,1)S(1)}, bf16[24,448]{1,0:T(8,128)(2,1)S(1)}, u32[]{:S(2)}, u32[]{:S(2)}) collective-permute-start(bf16[24,448]{1,0:T(8,128)(2,1)S(1)} %get-tuple-element.50), channel_id=1, source_target_pairs={{0,12},{1,13},{2,14},{3,15},{4,8},{5,9},{6,10},{7,11},{8,4},{9,5},... | collective-permute-start | bytes 64520 | tf_op jit(solution)/shard_map/ppermute | solution.py:253
  59.8 0.0 collective-permute-start.12
  59.8 1.7 %collective-permute-start.13 = (bf16[24,448]{1,0:T(8,128)(2,1)S(1)}, bf16[24,448]{1,0:T(8,128)(2,1)S(1)}, u32[]{:S(2)}, u32[]{:S(2)}) collective-permute-start(bf16[24,448]{1,0:T(8,128)(2,1)S(1)} %get-tuple-element.52), channel_id=1, source_target_pairs={{0,4},{1,5},{2,6},{3,7},{4,0},{5,1},{6,2},{7,3},{8,12},{9,13},{10,... | collective-permute-start | bytes 64520 | tf_op jit(solution)/shard_map/ppermute | solution.py:253
  61.5 1.3 %collective-permute-done.11 = bf16[24,448]{1,0:T(8,128)(2,1)S(1)} collective-permute-done((bf16[24,448]{1,0:T(8,128)(2,1)S(1)}, bf16[24,448]{1,0:T(8,128)(2,1)S(1)}, u32[]{:S(2)}, u32[]{:S(2)}) %collective-permute-start.11) | collective-permute-done | bytes 21536 | tf_op jit(solution)/shard_map/ppermute | solution.py:253
  62.8 1.7 %collective-permute-done.12 = bf16[24,448]{1,0:T(8,128)(2,1)S(1)} collective-permute-done((bf16[24,448]{1,0:T(8,128)(2,1)S(1)}, bf16[24,448]{1,0:T(8,128)(2,1)S(1)}, u32[]{:S(2)}, u32[]{:S(2)}) %collective-permute-start.12) | collective-permute-done | bytes 21536 | tf_op jit(solution)/shard_map/ppermute | solution.py:253
  64.5 0.0 collective-permute-done.13
  64.5 0.6 add_convert_fusion
  (4 shorter events, 0.1 us)
Async XLA Ops:
  0.0 16.5 %collective-permute-start.3 = (bf16[576,512]{1,0:T(8,128)(2,1)}, bf16[576,512]{1,0:T(8,128)(2,1)S(1)}, u32[]{:S(2)}, u32[]{:S(2)}) collective-permute-start(bf16[576,512]{1,0:T(8,128)(2,1)} %bitcast.21), channel_id=1, source_target_pairs={{0,2},{1,3},{2,0},{3,1},{4,6},{5,7},{6,4},{7,5},{8,10},{9,11},{10,... | collective-permute-start | bytes 1769480 | tf_op jit(solution)/shard_map/ppermute | solution.py:253
  3.0 29.0 %collective-permute-start.5 = (bf16[576,512]{1,0:T(8,128)(2,1)}, bf16[576,512]{1,0:T(8,128)(2,1)S(1)}, u32[]{:S(2)}, u32[]{:S(2)}) collective-permute-start(bf16[576,512]{1,0:T(8,128)(2,1)} %bitcast.22), channel_id=1, source_target_pairs={{0,1},{1,0},{2,3},{3,2},{4,5},{5,4},{6,7},{7,6},{8,9},{9,8},{10,11... | collective-permute-start | bytes 1769480 | tf_op jit(solution)/shard_map/ppermute | solution.py:253
  16.5 19.1 %collective-permute-start.4 = (bf16[576,512]{1,0:T(8,128)(2,1)S(1)}, bf16[576,512]{1,0:T(8,128)(2,1)S(1)}, u32[]{:S(2)}, u32[]{:S(2)}) collective-permute-start(bf16[576,512]{1,0:T(8,128)(2,1)S(1)} %collective-permute-done.3.refs_5_), channel_id=1, source_target_pairs={{0,1},{1,0},{2,3},{3,2},{4,5},{5,4},{6,7},{7,6},{8,9},{9,8},{10,11... | collective-permute-start | bytes 1769480 | tf_op jit(solution)/shard_map/ppermute | solution.py:253
  17.5 9.6 %collective-permute-start.1 = (bf16[96,576]{1,0:T(8,128)(2,1)S(1)}, bf16[96,576]{1,0:T(8,128)(2,1)S(1)}, u32[]{:S(2)}, u32[]{:S(2)}) collective-permute-start(bf16[96,576]{1,0:T(8,128)(2,1)S(1)} %bitcast.15), channel_id=1, source_target_pairs={{0,8},{1,9},{2,10},{3,11},{4,12},{5,13},{6,14},{7,15},{8,0},{9,1},... | collective-permute-start | bytes 331784 | tf_op jit(solution)/shard_map/ppermute | solution.py:253
  20.3 7.4 %collective-permute-start = (bf16[96,576]{1,0:T(8,128)(2,1)S(1)}, bf16[96,576]{1,0:T(8,128)(2,1)S(1)}, u32[]{:S(2)}, u32[]{:S(2)}) collective-permute-start(bf16[96,576]{1,0:T(8,128)(2,1)S(1)} %bitcast.16), channel_id=1, source_target_pairs={{0,4},{1,5},{2,6},{3,7},{4,0},{5,1},{6,2},{7,3},{8,12},{9,13},{10,... | collective-permute-start | bytes 331784 | tf_op jit(solution)/shard_map/ppermute | solution.py:253
  27.1 5.0 %collective-permute-start.2 = (bf16[96,576]{1,0:T(8,128)(2,1)S(1)}, bf16[96,576]{1,0:T(8,128)(2,1)S(1)}, u32[]{:S(2)}, u32[]{:S(2)}) collective-permute-start(bf16[96,576]{1,0:T(8,128)(2,1)S(1)} %collective-permute-done.1.refs_3_), channel_id=1, source_target_pairs={{0,4},{1,5},{2,6},{3,7},{4,0},{5,1},{6,2},{7,3},{8,12},{9,13},{10,... | collective-permute-start | bytes 331784 | tf_op jit(solution)/shard_map/ppermute | solution.py:253
  32.0 1.1 %copy-start = (bf16[1,512,576]{1,2,0:T(8,128)(2,1)S(1)}, bf16[1,512,576]{1,2,0:T(8,128)(2,1)}, u32[]{:S(2)}) copy-start(bf16[1,512,576]{1,2,0:T(8,128)(2,1)} %param.8) | copy-start | bytes 1769476
  36.7 9.0 %collective-permute-start.6 = (bf16[104,512]{1,0:T(8,128)(2,1)S(1)}, bf16[104,512]{1,0:T(8,128)(2,1)S(1)}, u32[]{:S(2)}, u32[]{:S(2)}) collective-permute-start(bf16[104,512]{1,0:T(8,128)(2,1)S(1)} %get-tuple-element.35), channel_id=1, source_target_pairs={{0,12},{1,13},{2,14},{3,15},{4,8},{5,9},{6,10},{7,11},{8,4},{9,5},... | collective-permute-start | bytes 319496 | tf_op jit(solution)/shard_map/ppermute | solution.py:253
  40.6 8.3 %collective-permute-start.7 = (bf16[104,512]{1,0:T(8,128)(2,1)S(1)}, bf16[104,512]{1,0:T(8,128)(2,1)S(1)}, u32[]{:S(2)}, u32[]{:S(2)}) collective-permute-start(bf16[104,512]{1,0:T(8,128)(2,1)S(1)} %get-tuple-element.36), channel_id=1, source_target_pairs={{0,8},{1,9},{2,10},{3,11},{4,12},{5,13},{6,14},{7,15},{8,0},{9,1},... | collective-permute-start | bytes 319496 | tf_op jit(solution)/shard_map/ppermute | solution.py:253
  40.6 4.2 %copy-start.1 = (bf16[4,512,128]{2,1,0:T(8,128)(2,1)S(1)}, bf16[4,512,128]{2,1,0:T(8,128)(2,1)}, u32[]{:S(2)}) copy-start(bf16[4,512,128]{2,1,0:T(8,128)(2,1)} %up_from.1) | copy-start | bytes 1572868
  40.6 4.2 %copy-start.2 = (bf16[1,24,576]{2,1,0:T(8,128)(2,1)S(1)}, bf16[1,24,576]{2,1,0:T(8,128)(2,1)}, u32[]{:S(2)}) copy-start(bf16[1,24,576]{2,1,0:T(8,128)(2,1)} %param.9) | copy-start | bytes 82948
  40.6 4.2 %copy-start.3 = (s32[1,24]{1,0:T(1,128)S(1)}, s32[1,24]{1,0:T(1,128)}, u32[]{:S(2)}) copy-start(s32[1,24]{1,0:T(1,128)} %parents_ref.1) | copy-start | bytes 292
  40.6 8.3 %collective-permute-start.8 = (bf16[104,512]{1,0:T(8,128)(2,1)S(1)}, bf16[104,512]{1,0:T(8,128)(2,1)S(1)}, u32[]{:S(2)}, u32[]{:S(2)}) collective-permute-start(bf16[104,512]{1,0:T(8,128)(2,1)S(1)} %get-tuple-element.37), channel_id=1, source_target_pairs={{0,4},{1,5},{2,6},{3,7},{4,0},{5,1},{6,2},{7,3},{8,12},{9,13},{10,... | collective-permute-start | bytes 319496 | tf_op jit(solution)/shard_map/ppermute | solution.py:253
  50.6 1.5 %collective-permute-start.9 = (bf16[8,24,448]{2,1,0:T(8,128)(2,1)S(1)}, bf16[8,24,448]{2,1,0:T(8,128)(2,1)S(1)}, u32[]{:S(2)}, u32[]{:S(2)}) collective-permute-start(bf16[8,24,448]{2,1,0:T(8,128)(2,1)S(1)} %get-tuple-element.46), channel_id=1, source_target_pairs={{0,1},{1,0},{2,3},{3,2},{4,5},{5,4},{6,7},{7,6},{8,9},{9,8},{10,11... | collective-permute-start | bytes 516104 | tf_op jit(solution)/shard_map/ppermute | solution.py:253
  52.1 4.9 %collective-permute-start.10 = (bf16[4,24,448]{2,1,0:T(8,128)(2,1)S(1)}, bf16[4,24,448]{2,1,0:T(8,128)(2,1)S(1)}, u32[]{:S(2)}, u32[]{:S(2)}) collective-permute-start(bf16[4,24,448]{2,1,0:T(8,128)(2,1)S(1)} %get-tuple-element.48), channel_id=1, source_target_pairs={{0,2},{1,3},{2,0},{3,1},{4,6},{5,7},{6,4},{7,5},{8,10},{9,11},{10,... | collective-permute-start | bytes 258056 | tf_op jit(solution)/shard_map/ppermute | solution.py:253
  57.1 5.7 %collective-permute-start.11 = (bf16[24,448]{1,0:T(8,128)(2,1)S(1)}, bf16[24,448]{1,0:T(8,128)(2,1)S(1)}, u32[]{:S(2)}, u32[]{:S(2)}) collective-permute-start(bf16[24,448]{1,0:T(8,128)(2,1)S(1)} %get-tuple-element.50), channel_id=1, source_target_pairs={{0,12},{1,13},{2,14},{3,15},{4,8},{5,9},{6,10},{7,11},{8,4},{9,5},... | collective-permute-start | bytes 64520 | tf_op jit(solution)/shard_map/ppermute | solution.py:253
  59.8 4.7 %collective-permute-start.12 = (bf16[24,448]{1,0:T(8,128)(2,1)S(1)}, bf16[24,448]{1,0:T(8,128)(2,1)S(1)}, u32[]{:S(2)}, u32[]{:S(2)}) collective-permute-start(bf16[24,448]{1,0:T(8,128)(2,1)S(1)} %get-tuple-element.51), channel_id=1, source_target_pairs={{0,8},{1,9},{2,10},{3,11},{4,12},{5,13},{6,14},{7,15},{8,0},{9,1},... | collective-permute-start | bytes 64520 | tf_op jit(solution)/shard_map/ppermute | solution.py:253
  59.8 4.7 %collective-permute-start.13 = (bf16[24,448]{1,0:T(8,128)(2,1)S(1)}, bf16[24,448]{1,0:T(8,128)(2,1)S(1)}, u32[]{:S(2)}, u32[]{:S(2)}) collective-permute-start(bf16[24,448]{1,0:T(8,128)(2,1)S(1)} %get-tuple-element.52), channel_id=1, source_target_pairs={{0,4},{1,5},{2,6},{3,7},{4,0},{5,1},{6,2},{7,3},{8,12},{9,13},{10,... | collective-permute-start | bytes 64520 | tf_op jit(solution)/shard_map/ppermute | solution.py:253

commit v2 on v1

--- a/solution.py
+++ b/solution.py
@@ -74,9 +74,11 @@
 
 def fold(rows, key_refs, bias_ref, carry, latent):
     blocks, tops = [], []
-    for spot, key_ref in enumerate(key_refs):
+    at = 0
+    for key_ref in key_refs:
         scores = jnp.dot(rows, key_ref[...], preferred_element_type=jnp.float32)
-        masked = scores * log2_scale + bias_ref[spot : spot + 1, :]
+        masked = scores * log2_scale + bias_ref[:, at : at + key_ref.shape[1]]
+        at += key_ref.shape[1]
         blocks.append(masked)
         tops.append(jnp.max(masked, axis=1, keepdims=True))
     top = carry[1] if carry is not None else jnp.full_like(tops[0], low_top)
@@ -108,12 +110,12 @@
 
 
 def middle_kernel(peers, bias_ref, *refs):
-    q_refs, (key_ref, *carry_refs, numer_ref, top_ref, total_ref) = refs[:peers], refs[peers:]
+    q_refs, refs = refs[:peers], refs[peers:]
+    key_refs, carry_refs, out_refs = refs[:-6], refs[-6:-3], refs[-3:]
     carry = tuple(ref[...] for ref in carry_refs)
-    numer, top, total = fold(join_rows(q_refs), [key_ref], bias_ref, carry, numer_ref.shape[1])
-    numer_ref[...] = numer
-    top_ref[...] = top
-    total_ref[...] = total
+    state = fold(join_rows(q_refs), key_refs, bias_ref, carry, out_refs[0].shape[1])
+    for out_ref, value in zip(out_refs, state):
+        out_ref[...] = value
 
 
 def pieces(row):
@@ -244,26 +246,36 @@
     bf16 = jnp.bfloat16
     myself = lax.axis_index("ctx")
 
-    def bias_of(*bits):
-        firsts = jnp.stack([lax.bitwise_xor(myself, bit) * block_len for bit in bits])
-        spots = firsts[:, None] + jnp.arange(block_len, dtype=jnp.int32)[None, :]
-        return jnp.where(spots < lengths[0], 0.0, neg_fill).astype(jnp.float32)
+    half = block_len // 2
+
+    def bias_of(*spans):
+        spots = [
+            lax.bitwise_xor(myself, bit) * block_len + jnp.arange(low, high, dtype=jnp.int32)
+            for bit, low, high in spans
+        ]
+        live = jnp.concatenate(spots)[None, :] < lengths[0]
+        return jnp.where(live, 0.0, neg_fill).astype(jnp.float32)
 
     def swap(value, bits):
         return lax.ppermute(value, "ctx", [(i, i ^ bits) for i in range(count)])
 
     keys_own = jnp.transpose(cache[0])
-    keys_across = swap(keys_own, 2)
+    own_low, own_high = keys_own[:, :half], keys_own[:, half:]
+    across_low = swap(own_low, 2)
+    across_high = swap(own_high, 2)
     keys_core = swap(keys_own, 1)
-    own_rows = jnp.transpose(queries[0], (1, 0, 2)).reshape(each, width)
-    rows = {0: own_rows}
+    sent = {0: queries[0]}
     bit = outer // 2
     while bit:
-        for peer in list(rows):
-            rows[peer ^ bit] = swap(rows[peer], inner * bit)
+        for peer in list(sent):
+            sent[peer ^ bit] = swap(sent[peer], inner * bit)
         bit //= 2
-    rows = [rows[peer] for peer in range(outer)]
-    keys_far = swap(keys_across, 1)
+    rows = [
+        jnp.transpose(sent[peer], (1, 0, 2)).reshape(each, width) for peer in range(outer)
+    ]
+    own_rows = rows[0]
+    far_low = swap(across_low, 1)
+    far_high = swap(across_high, 1)
 
     state_shape = (shaped(outer * each, latent), shaped(outer * each, 1), shaped(outer * each, 1))
     own_shape = (shaped(each, latent), shaped(each, 1), shaped(each, 1))
@@ -273,21 +285,27 @@
         own_shape + (shaped(*value_up.shape, dtype=bf16),),
         (own_rows, draft_latent[0], parents, value_up),
     )
+    low, high = (0, half), (half, block_len)
     state = call(
         lambda *refs: first_kernel(outer, *refs),
         state_shape,
-        (bias_of(0, 1), *rows, keys_own, keys_core),
+        (bias_of((0, *low), (0, *high), (1, 0, block_len)), *rows, own_low, own_high, keys_core),
     )
     state = call(
         lambda *refs: middle_kernel(outer, *refs),
         state_shape,
-        (bias_of(2), *rows, keys_across, *state),
+        (bias_of((2, *low), (3, *low)), *rows, across_low, far_low, *state),
+    )
+    state = call(
+        lambda *refs: middle_kernel(outer, *refs),
+        state_shape,
+        (bias_of((2, *high)), *rows, across_high, *state),
     )
     done = call(
         lambda *refs: last_kernel(outer, *refs),
         own_shape
         + tuple(shaped(each + PACK_ROWS, latent, dtype=bf16) for _ in range(outer - 1)),
-        (bias_of(3), *rows, keys_far, *state),
+        (bias_of((3, *high)), *rows, far_high, *state),
     )
     whole, states = done[:3], done[3:]
     got = [swap(states[peer - 1], inner * peer) for peer in range(outer - 1, 0, -1)]

time: 65.3 us -> 59.6 us (0.913)
  waiting for transfers between devices: 33 us -> 26.4 us
  Pallas kernels: 6.33 us -> 7.04 us
    ppermute x14 -> x16, waiting for transfers between devices: 33 us -> 26.4 us  [swap(): return lax.ppermute(value, 'ctx', [(i, i ^ bits) for i in range(count)])]
    slice x0 -> x1, local copies, waits for them, and re-layouts: none -> 1.09 us  [on_device(): own_low, own_high = (keys_own[:, :half], keys_own[:, half:])]
    unnamed x8 -> x6, local copies, waits for them, and re-layouts: 1.08 us -> 0.01 us
    pallas_call x7 -> x8, Pallas kernels: 6.33 us -> 7.04 us  [call(): pl.pallas_call(kernel, out_shape=outs, in_specs=specs or [pl.BlockSpec()...]
    ppermute x14 -> x16, starting transfers between devices: 18.7 us -> 18.8 us  [swap(): return lax.ppermute(value, 'ctx', [(i, i ^ bits) for i in range(count)])]
  transfers between devices with their start and end apart: 14 -> 16, of which waited for: 8 -> 9; matrix products, arithmetic and copies ran while one was open for 7% -> 10% of each run, Pallas kernels for 5% -> 7%
where the time goes in v2:
time: 59.6 us; the launch traced here: 59.4 us
  waiting for transfers between devices  26.4 us (44%)
  starting transfers between devices  18.8 us (32%)
  Pallas kernels  7.04 us (12%)
  other arithmetic  4.23 us (7%)
  local copies, waits for them, and re-layouts  2.07 us (3%)
  between operations  0.84 us (1%)
    ppermute x16, waiting for transfers between devices, swap(): return lax.ppermute(value, 'ctx', [(i, i ^ bits) for i in range(count)])  26.4 us
    ppermute x16, starting transfers between devices, swap(): return lax.ppermute(value, 'ctx', [(i, i ^ bits) for i in range(count)])  18.8 us
    pallas_call x8, Pallas kernels, call(): pl.pallas_call(kernel, out_shape=outs, in_specs=specs or [pl.BlockSpec()...  7.04 us
    select_n x1, other arithmetic, on_device(): proj_here = jnp.where(lengths[0] > -1, out_proj, jnp.zeros_like(out_proj))  3.56 us
  transfers between devices with their start and end apart: 16, of which 9 were waited for; matrix products, arithmetic and copies ran while one was open for 10% of the time, Pallas kernels for 7%

profile of v2, /device:TPU:0, one launch (start us, length us, event | category | flops | bytes accessed | tf_op | source)
XLA Modules:
  0.0 59.4 jit_solution(780831709843917106)
XLA Ops:
  0.0 3.1 %collective-permute-start = (bf16[24,4,576]{2,1,0:T(4,128)(2,1)}, bf16[24,4,576]{2,1,0:T(4,128)(2,1)S(1)}, u32[]{:S(2)}, u32[]{:S(2)}) collective-permute-start(bf16[24,4,576]{2,1,0:T(4,128)(2,1)} %bitcast.45), channel_id=1, source_target_pairs={{0,4},{1,5},{2,6},{3,7},{4,0},{5,1},{6,2},{7,3},{8,12},{9,13},{10,... | collective-permute-start | bytes 331784 | tf_op jit(solution)/shard_map/ppermute | solution.py:260
  3.1 2.6 %collective-permute-start.1 = (bf16[24,4,576]{2,1,0:T(4,128)(2,1)}, bf16[24,4,576]{2,1,0:T(4,128)(2,1)S(1)}, u32[]{:S(2)}, u32[]{:S(2)}) collective-permute-start(bf16[24,4,576]{2,1,0:T(4,128)(2,1)} %bitcast.46), channel_id=1, source_target_pairs={{0,8},{1,9},{2,10},{3,11},{4,12},{5,13},{6,14},{7,15},{8,0},{9,1},... | collective-permute-start | bytes 331784 | tf_op jit(solution)/shard_map/ppermute | solution.py:260
  5.6 0.0 collective-permute-start.7
  5.6 1.1 %fusion = (bf16[576,256]{1,0:T(8,128)(2,1)S(1)}, bf16[576,256]{1,0:T(8,128)(2,1)S(1)}) fusion(bf16[576,512]{1,0:T(8,128)(2,1)} %bitcast.44), kind=kLoop, calls=%fused_computation.12 | loop fusion | bytes 1179648 | tf_op jit(solution)/shard_map/slice | solution.py:263
  6.7 1.6 %collective-permute-start.5 = (bf16[576,256]{1,0:T(8,128)(2,1)S(1)}, bf16[576,256]{1,0:T(8,128)(2,1)S(1)}, u32[]{:S(2)}, u32[]{:S(2)}) collective-permute-start(bf16[576,256]{1,0:T(8,128)(2,1)S(1)} %get-tuple-element.59.refs_5_), channel_id=1, source_target_pairs={{0,2},{1,3},{2,0},{3,1},{4,6},{5,7},{6,4},{7,5},{8,10},{9,11},{10,... | collective-permute-start | bytes 884744 | tf_op jit(solution)/shard_map/ppermute | solution.py:260
  8.3 0.5 collective-permute-start.3
  9.5 0.9 %copy.8 = bf16[4,24,576]{2,1,0:T(8,128)(2,1)S(1)} copy(bf16[4,24,576]{2,0,1:T(4,128)(2,1)} %bitcast.47) | data formatting | bytes 221184 | tf_op jit(solution)/shard_map/transpose | solution.py:274
  10.5 6.2 %collective-permute-done.5.refs_5_ = bf16[576,256]{1,0:T(8,128)(2,1)S(1)} collective-permute-done((bf16[576,256]{1,0:T(8,128)(2,1)S(1)}, bf16[576,256]{1,0:T(8,128)(2,1)S(1)}, u32[]{:S(2)}, u32[]{:S(2)}) %collective-permute-start.5) | collective-permute-done | bytes 294944 | tf_op jit(solution)/shard_map/ppermute | solution.py:260
  16.7 0.0 collective-permute-start.6
  16.7 5.9 %collective-permute-done.3.refs_5_ = bf16[576,256]{1,0:T(8,128)(2,1)S(1)} collective-permute-done((bf16[576,256]{1,0:T(8,128)(2,1)S(1)}, bf16[576,256]{1,0:T(8,128)(2,1)S(1)}, u32[]{:S(2)}, u32[]{:S(2)}) %collective-permute-start.3) | collective-permute-done | bytes 294944 | tf_op jit(solution)/shard_map/ppermute | solution.py:260
  22.5 0.0 collective-permute-start.4
  22.6 0.0 collective-permute-done.1
  22.6 0.5 collective-permute-start.2
  23.1 0.0 collective-permute-done
  23.1 5.2 %collective-permute-done.2 = bf16[24,4,576]{2,1,0:T(4,128)(2,1)S(1)} collective-permute-done((bf16[24,4,576]{2,1,0:T(4,128)(2,1)S(1)}, bf16[24,4,576]{2,1,0:T(4,128)(2,1)S(1)}, u32[]{:S(2)}, u32[]{:S(2)}) %collective-permute-start.2) | collective-permute-done | bytes 110624 | tf_op jit(solution)/shard_map/ppermute | solution.py:260
  28.4 0.0 collective-permute-done.7.refs_7_
  28.4 1.4 %shard_map.73 = (f32[384,512]{1,0:T(8,128)S(1)}, f32[384,1]{1,0:T(8,128)S(1)}, f32[384,1]{1,0:T(8,128)S(1)}) custom-call(f32[1,1024]{1,0:T(1,128)S(1)} %compare_select_fusion.refs_0_, bf16[96,576]{1,0:T(8,128)(2,1)S(1)} %bitcast.25, bf16[96,576]{1,0:T(8,128)(2,1)S(1)} %bitcast.30, bf16[96,576]{1,0:T(8,128)(2,1)S(1)} %bitcast.34, ...), custom_call_target="tpu_custom_call" | custom-call | tf_op jit(solution)/shard_map/pallas_call | solution.py:223
  29.8 0.0 collective-permute-done.6.refs_6_
  29.8 1.1 %shard_map.74 = (f32[384,512]{1,0:T(8,128)S(1)}, f32[384,1]{1,0:T(8,128)S(1)}, f32[384,1]{1,0:T(8,128)S(1)}) custom-call(f32[1,512]{1,0:T(1,128)S(1)} %compare_select_fusion.1.refs_0_, bf16[96,576]{1,0:T(8,128)(2,1)S(1)} %bitcast.26, bf16[96,576]{1,0:T(8,128)(2,1)S(1)} %bitcast.31, bf16[96,576]{1,0:T(8,128)(2,1)S(1)} %bitcast.35, ...), custom_call_target="tpu_custom_call" | custom-call | tf_op jit(solution)/shard_map/pallas_call | solution.py:223
  30.9 0.9 %shard_map.75 = (f32[384,512]{1,0:T(8,128)S(1)}, f32[384,1]{1,0:T(8,128)S(1)}, f32[384,1]{1,0:T(8,128)S(1)}) custom-call(f32[1,256]{1,0:T(1,128)S(1)} %compare_select_fusion.2.refs_0_, bf16[96,576]{1,0:T(8,128)(2,1)S(1)} %bitcast.27, bf16[96,576]{1,0:T(8,128)(2,1)S(1)} %bitcast.32, bf16[96,576]{1,0:T(8,128)(2,1)S(1)} %bitcast.36, ...), custom_call_target="tpu_custom_call" | custom-call | tf_op jit(solution)/shard_map/pallas_call | solution.py:223
  31.8 0.0 collective-permute-done.4.refs_5_
  31.9 0.9 %shard_map.76 = (f32[96,512]{1,0:T(8,128)S(1)}, f32[96,1]{1,0:T(8,128)S(1)}, f32[96,1]{1,0:T(8,128)S(1)}, bf16[104,512]{1,0:T(8,128)(2,1)S(1)}, bf16[104,512]{1,...) custom-call(f32[1,256]{1,0:T(1,128)S(1)} %compare_select_fusion.3.refs_0_, bf16[96,576]{1,0:T(8,128)(2,1)S(1)} %bitcast.28, ...), custom_call_target="tpu_custom_call" | custom-call | tf_op jit(solution)/shard_map/pallas_call | solution.py:223
  32.8 0.1 collective-permute-start.8
  32.9 1.8 %collective-permute-start.9 = (bf16[104,512]{1,0:T(8,128)(2,1)S(1)}, bf16[104,512]{1,0:T(8,128)(2,1)S(1)}, u32[]{:S(2)}, u32[]{:S(2)}) collective-permute-start(bf16[104,512]{1,0:T(8,128)(2,1)S(1)} %get-tuple-element.42), channel_id=1, source_target_pairs={{0,8},{1,9},{2,10},{3,11},{4,12},{5,13},{6,14},{7,15},{8,0},{9,1},... | collective-permute-start | bytes 319496 | tf_op jit(solution)/shard_map/ppermute | solution.py:260
  34.8 0.0 copy-start
  34.8 0.0 copy-start.1
  34.8 0.0 copy-start.2
  34.8 2.5 %collective-permute-start.10 = (bf16[104,512]{1,0:T(8,128)(2,1)S(1)}, bf16[104,512]{1,0:T(8,128)(2,1)S(1)}, u32[]{:S(2)}, u32[]{:S(2)}) collective-permute-start(bf16[104,512]{1,0:T(8,128)(2,1)S(1)} %get-tuple-element.43), channel_id=1, source_target_pairs={{0,4},{1,5},{2,6},{3,7},{4,0},{5,1},{6,2},{7,3},{8,12},{9,13},{10,... | collective-permute-start | bytes 319496 | tf_op jit(solution)/shard_map/ppermute | solution.py:260
  37.2 3.6 %broadcast_select_fusion.refs_10_ = bf16[512,7168]{1,0:T(8,128)(2,1)S(1)} fusion(bf16[512,7168]{1,0:T(8,128)(2,1)} %param.13, pred[]{:T(512)S(6)} %gt.3), kind=kLoop, calls=%fused_computation | loop fusion | flops 3670016 | bytes 14680065 | tf_op jit(solution)/shard_map/jit(_where)/select_n | solution.py:282
  40.8 0.0 copy-done
  40.8 0.0 copy-done.1
  40.8 0.0 copy-done.2
  40.8 0.9 %shard_map.77 = (f32[96,512]{1,0:T(8,128)S(1)}, f32[96,1]{1,0:T(8,128)S(1)}, f32[96,1]{1,0:T(8,128)S(1)}, bf16[4,512,128]{2,1,0:T(8,128)(2,1)S(1)}) custom-call(bf16[96,576]{1,0:T(8,128)(2,1)S(1)} %bitcast.29, bf16[24,576]{1,0:T(8,128)(2,1)S(1)} %bitcast.42, s32[1,24]{1,0:T(1,128)S(1)} %copy-done.2, bf16[4,512,128]{2,1,0:T(8,128)(2,1)S(1)} %copy-done), custom_call_target="tpu_custom_call" | custom-call | tf_op jit(solution)/shard_map/pallas_call | solution.py:223
  41.8 0.0 collective-permute-done.8.refs_0_
  41.8 2.3 %collective-permute-done.9.refs_1_ = bf16[104,512]{1,0:T(8,128)(2,1)S(1)} collective-permute-done((bf16[104,512]{1,0:T(8,128)(2,1)S(1)}, bf16[104,512]{1,0:T(8,128)(2,1)S(1)}, u32[]{:S(2)}, u32[]{:S(2)}) %collective-permute-start.9) | collective-permute-done | bytes 106528 | tf_op jit(solution)/shard_map/ppermute | solution.py:260
  44.1 0.0 collective-permute-done.10.refs_2_
  44.1 1.7 %shard_map.78 = (f32[8,24,448]{2,1,0:T(8,128)S(1)}, bf16[8,24,448]{2,1,0:T(8,128)(2,1)S(1)}) custom-call(bf16[104,512]{1,0:T(8,128)(2,1)S(1)} %collective-permute-done.8.refs_0_, bf16[104,512]{1,0:T(8,128)(2,1)S(1)} %collective-permute-done.9.refs_1_, bf16[104,512]{1,0:T(8,128)(2,1)S(1)} %collective-permute-done.10.refs_2_, ...), custom_call_target="tpu_custom_call" | custom-call | tf_op jit(solution)/shard_map/pallas_call | solution.py:223
  45.8 0.1 collective-permute-start.11
  45.9 1.4 %collective-permute-done.11.got_ref = bf16[8,24,448]{2,1,0:T(8,128)(2,1)S(1)} collective-permute-done((bf16[8,24,448]{2,1,0:T(8,128)(2,1)S(1)}, bf16[8,24,448]{2,1,0:T(8,128)(2,1)S(1)}, u32[]{:S(2)}, u32[]{:S(2)}) %collective-permute-start.11) | collective-permute-done | bytes 172064 | tf_op jit(solution)/shard_map/ppermute | solution.py:260
  47.4 1.6 %collective-permute-start.12 = (bf16[4,24,448]{2,1,0:T(8,128)(2,1)S(1)}, bf16[4,24,448]{2,1,0:T(8,128)(2,1)S(1)}, u32[]{:S(2)}, u32[]{:S(2)}) collective-permute-start(bf16[4,24,448]{2,1,0:T(8,128)(2,1)S(1)} %get-tuple-element.54), channel_id=1, source_target_pairs={{0,2},{1,3},{2,0},{3,1},{4,6},{5,7},{6,4},{7,5},{8,10},{9,11},{10,... | collective-permute-start | bytes 258056 | tf_op jit(solution)/shard_map/ppermute | solution.py:260
  49.0 3.3 %collective-permute-done.12.got_ref = bf16[4,24,448]{2,1,0:T(8,128)(2,1)S(1)} collective-permute-done((bf16[4,24,448]{2,1,0:T(8,128)(2,1)S(1)}, bf16[4,24,448]{2,1,0:T(8,128)(2,1)S(1)}, u32[]{:S(2)}, u32[]{:S(2)}) %collective-permute-start.12) | collective-permute-done | bytes 86048 | tf_op jit(solution)/shard_map/ppermute | solution.py:260
  52.3 1.4 %collective-permute-start.13 = (bf16[24,448]{1,0:T(8,128)(2,1)S(1)}, bf16[24,448]{1,0:T(8,128)(2,1)S(1)}, u32[]{:S(2)}, u32[]{:S(2)}) collective-permute-start(bf16[24,448]{1,0:T(8,128)(2,1)S(1)} %get-tuple-element.56), channel_id=1, source_target_pairs={{0,12},{1,13},{2,14},{3,15},{4,8},{5,9},{6,10},{7,11},{8,4},{9,5},... | collective-permute-start | bytes 64520 | tf_op jit(solution)/shard_map/ppermute | solution.py:260
  53.7 0.0 collective-permute-start.14
  53.7 3.0 %collective-permute-start.15 = (bf16[24,448]{1,0:T(8,128)(2,1)S(1)}, bf16[24,448]{1,0:T(8,128)(2,1)S(1)}, u32[]{:S(2)}, u32[]{:S(2)}) collective-permute-start(bf16[24,448]{1,0:T(8,128)(2,1)S(1)} %get-tuple-element.58), channel_id=1, source_target_pairs={{0,4},{1,5},{2,6},{3,7},{4,0},{5,1},{6,2},{7,3},{8,12},{9,13},{10,... | collective-permute-start | bytes 64520 | tf_op jit(solution)/shard_map/ppermute | solution.py:260
  56.8 1.2 %collective-permute-done.13 = bf16[24,448]{1,0:T(8,128)(2,1)S(1)} collective-permute-done((bf16[24,448]{1,0:T(8,128)(2,1)S(1)}, bf16[24,448]{1,0:T(8,128)(2,1)S(1)}, u32[]{:S(2)}, u32[]{:S(2)}) %collective-permute-start.13) | collective-permute-done | bytes 21536 | tf_op jit(solution)/shard_map/ppermute | solution.py:260
  58.0 0.5 collective-permute-done.14
  58.6 0.2 collective-permute-done.15
  58.8 0.6 %add_convert_fusion = bf16[24,448]{1,0:T(8,128)(2,1)} fusion(bf16[24,448]{1,0:T(8,128)(2,1)S(1)} %collective-permute-done.15, bf16[24,448]{1,0:T(8,128)(2,1)S(1)} %collective-permute-done.14, f32[24,448]{1,0:T(8,128)S(1)} %get-tuple-element.55, bf16[24,448]{1,0:T(8,128)(2,1)S(1)} %collective-permute-done.13), kind=kLoop, calls=%fused_computation.1 | loop fusion | flops 75264 | bytes 129024 | tf_op jit(solution)/shard_map/convert_element_type | solution.py:332
  (13 shorter events, 0.2 us)
Async XLA Ops:
  0.0 23.1 %collective-permute-start = (bf16[24,4,576]{2,1,0:T(4,128)(2,1)}, bf16[24,4,576]{2,1,0:T(4,128)(2,1)S(1)}, u32[]{:S(2)}, u32[]{:S(2)}) collective-permute-start(bf16[24,4,576]{2,1,0:T(4,128)(2,1)} %bitcast.45), channel_id=1, source_target_pairs={{0,4},{1,5},{2,6},{3,7},{4,0},{5,1},{6,2},{7,3},{8,12},{9,13},{10,... | collective-permute-start | bytes 331784 | tf_op jit(solution)/shard_map/ppermute | solution.py:260
  3.1 19.5 %collective-permute-start.1 = (bf16[24,4,576]{2,1,0:T(4,128)(2,1)}, bf16[24,4,576]{2,1,0:T(4,128)(2,1)S(1)}, u32[]{:S(2)}, u32[]{:S(2)}) collective-permute-start(bf16[24,4,576]{2,1,0:T(4,128)(2,1)} %bitcast.46), channel_id=1, source_target_pairs={{0,8},{1,9},{2,10},{3,11},{4,12},{5,13},{6,14},{7,15},{8,0},{9,1},... | collective-permute-start | bytes 331784 | tf_op jit(solution)/shard_map/ppermute | solution.py:260
  5.6 22.8 %collective-permute-start.7 = (bf16[576,512]{1,0:T(8,128)(2,1)}, bf16[576,512]{1,0:T(8,128)(2,1)S(1)}, u32[]{:S(2)}, u32[]{:S(2)}) collective-permute-start(bf16[576,512]{1,0:T(8,128)(2,1)} %bitcast.43), channel_id=1, source_target_pairs={{0,1},{1,0},{2,3},{3,2},{4,5},{5,4},{6,7},{7,6},{8,9},{9,8},{10,11... | collective-permute-start | bytes 1769480 | tf_op jit(solution)/shard_map/ppermute | solution.py:260
  6.7 9.9 %collective-permute-start.5 = (bf16[576,256]{1,0:T(8,128)(2,1)S(1)}, bf16[576,256]{1,0:T(8,128)(2,1)S(1)}, u32[]{:S(2)}, u32[]{:S(2)}) collective-permute-start(bf16[576,256]{1,0:T(8,128)(2,1)S(1)} %get-tuple-element.59.refs_5_), channel_id=1, source_target_pairs={{0,2},{1,3},{2,0},{3,1},{4,6},{5,7},{6,4},{7,5},{8,10},{9,11},{10,... | collective-permute-start | bytes 884744 | tf_op jit(solution)/shard_map/ppermute | solution.py:260
  8.3 14.2 %collective-permute-start.3 = (bf16[576,256]{1,0:T(8,128)(2,1)S(1)}, bf16[576,256]{1,0:T(8,128)(2,1)S(1)}, u32[]{:S(2)}, u32[]{:S(2)}) collective-permute-start(bf16[576,256]{1,0:T(8,128)(2,1)S(1)} %get-tuple-element.60.refs_6_), channel_id=1, source_target_pairs={{0,2},{1,3},{2,0},{3,1},{4,6},{5,7},{6,4},{7,5},{8,10},{9,11},{10,... | collective-permute-start | bytes 884744 | tf_op jit(solution)/shard_map/ppermute | solution.py:260
  16.7 13.1 %collective-permute-start.6 = (bf16[576,256]{1,0:T(8,128)(2,1)S(1)}, bf16[576,256]{1,0:T(8,128)(2,1)S(1)}, u32[]{:S(2)}, u32[]{:S(2)}) collective-permute-start(bf16[576,256]{1,0:T(8,128)(2,1)S(1)} %collective-permute-done.5.refs_5_), channel_id=1, source_target_pairs={{0,1},{1,0},{2,3},{3,2},{4,5},{5,4},{6,7},{7,6},{8,9},{9,8},{10,11... | collective-permute-start | bytes 884744 | tf_op jit(solution)/shard_map/ppermute | solution.py:260
  22.5 9.3 %collective-permute-start.4 = (bf16[576,256]{1,0:T(8,128)(2,1)S(1)}, bf16[576,256]{1,0:T(8,128)(2,1)S(1)}, u32[]{:S(2)}, u32[]{:S(2)}) collective-permute-start(bf16[576,256]{1,0:T(8,128)(2,1)S(1)} %collective-permute-done.3.refs_5_), channel_id=1, source_target_pairs={{0,1},{1,0},{2,3},{3,2},{4,5},{5,4},{6,7},{7,6},{8,9},{9,8},{10,11... | collective-permute-start | bytes 884744 | tf_op jit(solution)/shard_map/ppermute | solution.py:260
  22.6 5.8 %collective-permute-start.2 = (bf16[24,4,576]{2,1,0:T(4,128)(2,1)S(1)}, bf16[24,4,576]{2,1,0:T(4,128)(2,1)S(1)}, u32[]{:S(2)}, u32[]{:S(2)}) collective-permute-start(bf16[24,4,576]{2,1,0:T(4,128)(2,1)S(1)} %collective-permute-done.1), channel_id=1, source_target_pairs={{0,4},{1,5},{2,6},{3,7},{4,0},{5,1},{6,2},{7,3},{8,12},{9,13},{10,... | collective-permute-start | bytes 331784 | tf_op jit(solution)/shard_map/ppermute | solution.py:260
  32.8 9.0 %collective-permute-start.8 = (bf16[104,512]{1,0:T(8,128)(2,1)S(1)}, bf16[104,512]{1,0:T(8,128)(2,1)S(1)}, u32[]{:S(2)}, u32[]{:S(2)}) collective-permute-start(bf16[104,512]{1,0:T(8,128)(2,1)S(1)} %get-tuple-element.41), channel_id=1, source_target_pairs={{0,12},{1,13},{2,14},{3,15},{4,8},{5,9},{6,10},{7,11},{8,4},{9,5},... | collective-permute-start | bytes 319496 | tf_op jit(solution)/shard_map/ppermute | solution.py:260
  32.9 11.2 %collective-permute-start.9 = (bf16[104,512]{1,0:T(8,128)(2,1)S(1)}, bf16[104,512]{1,0:T(8,128)(2,1)S(1)}, u32[]{:S(2)}, u32[]{:S(2)}) collective-permute-start(bf16[104,512]{1,0:T(8,128)(2,1)S(1)} %get-tuple-element.42), channel_id=1, source_target_pairs={{0,8},{1,9},{2,10},{3,11},{4,12},{5,13},{6,14},{7,15},{8,0},{9,1},... | collective-permute-start | bytes 319496 | tf_op jit(solution)/shard_map/ppermute | solution.py:260
  34.8 6.0 %copy-start = (bf16[4,512,128]{2,1,0:T(8,128)(2,1)S(1)}, bf16[4,512,128]{2,1,0:T(8,128)(2,1)}, u32[]{:S(2)}) copy-start(bf16[4,512,128]{2,1,0:T(8,128)(2,1)} %up_from.1) | copy-start | bytes 1572868
  34.8 6.1 %copy-start.1 = (bf16[1,24,576]{2,1,0:T(8,128)(2,1)S(1)}, bf16[1,24,576]{2,1,0:T(8,128)(2,1)}, u32[]{:S(2)}) copy-start(bf16[1,24,576]{2,1,0:T(8,128)(2,1)} %param.9) | copy-start | bytes 82948
  34.8 6.1 %copy-start.2 = (s32[1,24]{1,0:T(1,128)S(1)}, s32[1,24]{1,0:T(1,128)}, u32[]{:S(2)}) copy-start(s32[1,24]{1,0:T(1,128)} %parents_ref.1) | copy-start | bytes 292
  34.8 9.4 %collective-permute-start.10 = (bf16[104,512]{1,0:T(8,128)(2,1)S(1)}, bf16[104,512]{1,0:T(8,128)(2,1)S(1)}, u32[]{:S(2)}, u32[]{:S(2)}) collective-permute-start(bf16[104,512]{1,0:T(8,128)(2,1)S(1)} %get-tuple-element.43), channel_id=1, source_target_pairs={{0,4},{1,5},{2,6},{3,7},{4,0},{5,1},{6,2},{7,3},{8,12},{9,13},{10,... | collective-permute-start | bytes 319496 | tf_op jit(solution)/shard_map/ppermute | solution.py:260
  45.8 1.5 %collective-permute-start.11 = (bf16[8,24,448]{2,1,0:T(8,128)(2,1)S(1)}, bf16[8,24,448]{2,1,0:T(8,128)(2,1)S(1)}, u32[]{:S(2)}, u32[]{:S(2)}) collective-permute-start(bf16[8,24,448]{2,1,0:T(8,128)(2,1)S(1)} %get-tuple-element.52), channel_id=1, source_target_pairs={{0,1},{1,0},{2,3},{3,2},{4,5},{5,4},{6,7},{7,6},{8,9},{9,8},{10,11... | collective-permute-start | bytes 516104 | tf_op jit(solution)/shard_map/ppermute | solution.py:260
  47.4 4.9 %collective-permute-start.12 = (bf16[4,24,448]{2,1,0:T(8,128)(2,1)S(1)}, bf16[4,24,448]{2,1,0:T(8,128)(2,1)S(1)}, u32[]{:S(2)}, u32[]{:S(2)}) collective-permute-start(bf16[4,24,448]{2,1,0:T(8,128)(2,1)S(1)} %get-tuple-element.54), channel_id=1, source_target_pairs={{0,2},{1,3},{2,0},{3,1},{4,6},{5,7},{6,4},{7,5},{8,10},{9,11},{10,... | collective-permute-start | bytes 258056 | tf_op jit(solution)/shard_map/ppermute | solution.py:260
  52.3 5.7 %collective-permute-start.13 = (bf16[24,448]{1,0:T(8,128)(2,1)S(1)}, bf16[24,448]{1,0:T(8,128)(2,1)S(1)}, u32[]{:S(2)}, u32[]{:S(2)}) collective-permute-start(bf16[24,448]{1,0:T(8,128)(2,1)S(1)} %get-tuple-element.56), channel_id=1, source_target_pairs={{0,12},{1,13},{2,14},{3,15},{4,8},{5,9},{6,10},{7,11},{8,4},{9,5},... | collective-permute-start | bytes 64520 | tf_op jit(solution)/shard_map/ppermute | solution.py:260
  53.7 4.8 %collective-permute-start.14 = (bf16[24,448]{1,0:T(8,128)(2,1)S(1)}, bf16[24,448]{1,0:T(8,128)(2,1)S(1)}, u32[]{:S(2)}, u32[]{:S(2)}) collective-permute-start(bf16[24,448]{1,0:T(8,128)(2,1)S(1)} %get-tuple-element.57), channel_id=1, source_target_pairs={{0,8},{1,9},{2,10},{3,11},{4,12},{5,13},{6,14},{7,15},{8,0},{9,1},... | collective-permute-start | bytes 64520 | tf_op jit(solution)/shard_map/ppermute | solution.py:260
  53.7 5.1 %collective-permute-start.15 = (bf16[24,448]{1,0:T(8,128)(2,1)S(1)}, bf16[24,448]{1,0:T(8,128)(2,1)S(1)}, u32[]{:S(2)}, u32[]{:S(2)}) collective-permute-start(bf16[24,448]{1,0:T(8,128)(2,1)S(1)} %get-tuple-element.58), channel_id=1, source_target_pairs={{0,4},{1,5},{2,6},{3,7},{4,0},{5,1},{6,2},{7,3},{8,12},{9,13},{10,... | collective-permute-start | bytes 64520 | tf_op jit(solution)/shard_map/ppermute | solution.py:260

commit v3 on v2

--- a/solution.py
+++ b/solution.py
@@ -101,19 +101,16 @@
 
 
 def first_kernel(peers, bias_ref, *refs):
-    q_refs, refs = refs[:peers], refs[peers:]
-    key_refs, (numer_ref, top_ref, total_ref) = refs[:-3], refs[-3:]
-    numer, top, total = fold(join_rows(q_refs), key_refs, bias_ref, None, numer_ref.shape[1])
-    numer_ref[...] = numer
-    top_ref[...] = top
-    total_ref[...] = total
+    q_refs, key_refs, out_refs = refs[:peers], refs[peers:-3], refs[-3:]
+    state = fold(join_rows(q_refs), key_refs, bias_ref, None, out_refs[0].shape[1])
+    for out_ref, value in zip(out_refs, state):
+        out_ref[...] = value
 
 
 def middle_kernel(peers, bias_ref, *refs):
-    q_refs, refs = refs[:peers], refs[peers:]
-    key_refs, carry_refs, out_refs = refs[:-6], refs[-6:-3], refs[-3:]
-    carry = tuple(ref[...] for ref in carry_refs)
-    state = fold(join_rows(q_refs), key_refs, bias_ref, carry, out_refs[0].shape[1])
+    q_refs, (key_ref, *carry_refs), out_refs = refs[:peers], refs[peers:-3], refs[-3:]
+    carry = tuple(join_rows(carry_refs[part::3]) for part in range(3))
+    state = fold(join_rows(q_refs), [key_ref], bias_ref, carry, out_refs[0].shape[1])
     for out_ref, value in zip(out_refs, state):
         out_ref[...] = value
 
@@ -246,12 +243,10 @@
     bf16 = jnp.bfloat16
     myself = lax.axis_index("ctx")
 
-    half = block_len // 2
-
-    def bias_of(*spans):
+    def bias_of(*bits):
         spots = [
-            lax.bitwise_xor(myself, bit) * block_len + jnp.arange(low, high, dtype=jnp.int32)
-            for bit, low, high in spans
+            lax.bitwise_xor(myself, bit) * block_len + jnp.arange(block_len, dtype=jnp.int32)
+            for bit in bits
         ]
         live = jnp.concatenate(spots)[None, :] < lengths[0]
         return jnp.where(live, 0.0, neg_fill).astype(jnp.float32)
@@ -259,56 +254,54 @@
     def swap(value, bits):
         return lax.ppermute(value, "ctx", [(i, i ^ bits) for i in range(count)])
 
+    def on_chip(value):
+        return jnp.where(lengths[0] > -1, value, jnp.zeros_like(value))
+
     keys_own = jnp.transpose(cache[0])
-    own_low, own_high = keys_own[:, :half], keys_own[:, half:]
-    across_low = swap(own_low, 2)
-    across_high = swap(own_high, 2)
+    keys_across = swap(keys_own, 2)
     keys_core = swap(keys_own, 1)
+    keys_far = swap(keys_across, 1)
     sent = {0: queries[0]}
     bit = outer // 2
     while bit:
         for peer in list(sent):
             sent[peer ^ bit] = swap(sent[peer], inner * bit)
         bit //= 2
-    rows = [
-        jnp.transpose(sent[peer], (1, 0, 2)).reshape(each, width) for peer in range(outer)
-    ]
+    peers = [*range(0, outer, 2), *range(1, outer, 2)]
+    rows = [jnp.transpose(sent[peer], (1, 0, 2)).reshape(each, width) for peer in peers]
     own_rows = rows[0]
-    far_low = swap(across_low, 1)
-    far_high = swap(across_high, 1)
-
-    state_shape = (shaped(outer * each, latent), shaped(outer * each, 1), shaped(outer * each, 1))
-    own_shape = (shaped(each, latent), shaped(each, 1), shaped(each, 1))
-    proj_here = jnp.where(lengths[0] > -1, out_proj, jnp.zeros_like(out_proj))
+
+    def state_of(blocks):
+        return tuple(shaped(blocks * each, size) for size in (latent, 1, 1))
+
+    own_shape = state_of(1)
+    proj_here = on_chip(out_proj)
     *drafted, up_here = call(
         draft_kernel,
         own_shape + (shaped(*value_up.shape, dtype=bf16),),
         (own_rows, draft_latent[0], parents, value_up),
     )
-    low, high = (0, half), (half, block_len)
-    state = call(
-        lambda *refs: first_kernel(outer, *refs),
-        state_shape,
-        (bias_of((0, *low), (0, *high), (1, 0, block_len)), *rows, own_low, own_high, keys_core),
-    )
+    keys_here = on_chip(keys_own)
+    parts = []
+    for some in (rows[: outer // 2], rows[outer // 2 :]):
+        parts += call(
+            lambda *refs: first_kernel(outer // 2, *refs),
+            state_of(outer // 2),
+            (bias_of(0, 1), *some, keys_here, keys_core),
+        )
     state = call(
         lambda *refs: middle_kernel(outer, *refs),
-        state_shape,
-        (bias_of((2, *low), (3, *low)), *rows, across_low, far_low, *state),
-    )
-    state = call(
-        lambda *refs: middle_kernel(outer, *refs),
-        state_shape,
-        (bias_of((2, *high)), *rows, across_high, *state),
+        state_of(outer),
+        (bias_of(2), *rows, keys_across, *parts),
     )
     done = call(
         lambda *refs: last_kernel(outer, *refs),
         own_shape
         + tuple(shaped(each + PACK_ROWS, latent, dtype=bf16) for _ in range(outer - 1)),
-        (bias_of((3, *high)), *rows, far_high, *state),
-    )
-    whole, states = done[:3], done[3:]
-    got = [swap(states[peer - 1], inner * peer) for peer in range(outer - 1, 0, -1)]
+        (bias_of(3), *rows, keys_far, *state),
+    )
+    whole, states = done[:3], dict(zip(peers[1:], done[3:]))
+    got = [swap(states[peer], inner * peer) for peer in range(outer - 1, 0, -1)]
     keep, send = call(
         lambda *refs: project_kernel(outer, *refs),
         (shaped(chips, drafts, columns), shaped(chips, drafts, columns, dtype=bf16)),

time: 59.6 us -> 56.7 us (0.951)
  waiting for transfers between devices: 26.4 us -> 22.8 us
  other arithmetic: 4.23 us -> 5.32 us
  local copies, waits for them, and re-layouts: 2.07 us -> 0.98 us
  starting transfers between devices: 18.8 us -> 19.6 us
    ppermute x16 -> x14, waiting for transfers between devices: 26.4 us -> 22.8 us  [swap(): return lax.ppermute(value, 'ctx', [(i, i ^ bits) for i in range(count)])]
    select_n x1 -> x2, other arithmetic: 3.56 us -> 4.67 us  [on_chip(): return jnp.where(lengths[0] > -1, value, jnp.zeros_like(value))]
    slice x1 -> x0, local copies, waits for them, and re-layouts: 1.09 us -> none  [on_device(): own_low, own_high = (keys_own[:, :half], keys_own[:, half:])]
    ppermute x16 -> x14, starting transfers between devices: 18.8 us -> 19.6 us  [swap(): return lax.ppermute(value, 'ctx', [(i, i ^ bits) for i in range(count)])]
  transfers between devices with their start and end apart: 16 -> 14, of which waited for: 9 -> 7; matrix products, arithmetic and copies ran while one was open for 10% -> 10% of each run, Pallas kernels for 7% -> 7%
where the time goes in v3:
time: 56.7 us; the launch traced here: 56.5 us
  waiting for transfers between devices  22.8 us (40%)
  starting transfers between devices  19.6 us (35%)
  Pallas kernels  6.86 us (12%)
  other arithmetic  5.32 us (9%)
  local copies, waits for them, and re-layouts  0.98 us (2%)
  between operations  0.83 us (1%)
    ppermute x14, waiting for transfers between devices, swap(): return lax.ppermute(value, 'ctx', [(i, i ^ bits) for i in range(count)])  22.8 us
    ppermute x14, starting transfers between devices, swap(): return lax.ppermute(value, 'ctx', [(i, i ^ bits) for i in range(count)])  19.6 us
    pallas_call x8, Pallas kernels, call(): pl.pallas_call(kernel, out_shape=outs, in_specs=specs or [pl.BlockSpec()...  6.86 us
    select_n x2, other arithmetic, on_chip(): return jnp.where(lengths[0] > -1, value, jnp.zeros_like(value))  4.67 us
  transfers between devices with their start and end apart: 14, of which 7 were waited for; matrix products, arithmetic and copies ran while one was open for 10% of the time, Pallas kernels for 7%

profile of v3, /device:TPU:0, one launch (start us, length us, event | category | flops | bytes accessed | tf_op | source)
XLA Modules:
  0.0 56.5 jit_solution(6677665781923922939)
XLA Ops:
  0.0 3.0 %collective-permute-start.3 = (bf16[576,512]{1,0:T(8,128)(2,1)}, bf16[576,512]{1,0:T(8,128)(2,1)S(1)}, u32[]{:S(2)}, u32[]{:S(2)}) collective-permute-start(bf16[576,512]{1,0:T(8,128)(2,1)} %bitcast.36), channel_id=1, source_target_pairs={{0,2},{1,3},{2,0},{3,1},{4,6},{5,7},{6,4},{7,5},{8,10},{9,11},{10,... | collective-permute-start | bytes 1769480 | tf_op jit(solution)/shard_map/ppermute | solution.py:255
  3.0 2.6 %collective-permute-start = (bf16[24,4,576]{2,1,0:T(4,128)(2,1)}, bf16[24,4,576]{2,1,0:T(4,128)(2,1)S(1)}, u32[]{:S(2)}, u32[]{:S(2)}) collective-permute-start(bf16[24,4,576]{2,1,0:T(4,128)(2,1)} %bitcast.38), channel_id=1, source_target_pairs={{0,8},{1,9},{2,10},{3,11},{4,12},{5,13},{6,14},{7,15},{8,0},{9,1},... | collective-permute-start | bytes 331784 | tf_op jit(solution)/shard_map/ppermute | solution.py:255
  5.6 1.6 %collective-permute-start.1 = (bf16[24,4,576]{2,1,0:T(4,128)(2,1)}, bf16[24,4,576]{2,1,0:T(4,128)(2,1)S(1)}, u32[]{:S(2)}, u32[]{:S(2)}) collective-permute-start(bf16[24,4,576]{2,1,0:T(4,128)(2,1)} %bitcast.39), channel_id=1, source_target_pairs={{0,4},{1,5},{2,6},{3,7},{4,0},{5,1},{6,2},{7,3},{8,12},{9,13},{10,... | collective-permute-start | bytes 331784 | tf_op jit(solution)/shard_map/ppermute | solution.py:255
  7.2 0.0 collective-permute-start.5
  7.8 0.9 %copy.8 = bf16[4,24,576]{2,1,0:T(8,128)(2,1)S(1)} copy(bf16[4,24,576]{2,0,1:T(4,128)(2,1)} %bitcast.40) | data formatting | bytes 221184 | tf_op jit(solution)/shard_map/transpose | solution.py:271
  8.8 7.8 %collective-permute-done.3.refs_5_ = bf16[576,512]{1,0:T(8,128)(2,1)S(1)} collective-permute-done((bf16[576,512]{1,0:T(8,128)(2,1)}, bf16[576,512]{1,0:T(8,128)(2,1)S(1)}, u32[]{:S(2)}, u32[]{:S(2)}) %collective-permute-start.3) | collective-permute-done | bytes 589856 | tf_op jit(solution)/shard_map/ppermute | solution.py:255
  16.5 0.0 collective-permute-start.4
  16.5 1.1 %broadcast_select_fusion.1.refs_3_ = bf16[576,512]{1,0:T(8,128)(2,1)S(1)} fusion(pred[]{:T(512)S(6)} %gt.4, bf16[1,512,576]{1,2,0:T(8,128)(2,1)} %param.8), kind=kLoop, calls=%fused_computation.1 | loop fusion | flops 294912 | bytes 1179649 | tf_op jit(solution)/shard_map/jit(_where)/select_n | solution.py:258
  17.7 0.0 collective-permute-done
  17.7 1.9 %collective-permute-start.2 = (bf16[24,4,576]{2,1,0:T(4,128)(2,1)S(1)}, bf16[24,4,576]{2,1,0:T(4,128)(2,1)S(1)}, u32[]{:S(2)}, u32[]{:S(2)}) collective-permute-start(bf16[24,4,576]{2,1,0:T(4,128)(2,1)S(1)} %collective-permute-done), channel_id=1, source_target_pairs={{0,4},{1,5},{2,6},{3,7},{4,0},{5,1},{6,2},{7,3},{8,12},{9,13},{10,... | collective-permute-start | bytes 331784 | tf_op jit(solution)/shard_map/ppermute | solution.py:255
  19.6 0.0 collective-permute-done.1
  19.6 3.9 %collective-permute-done.2 = bf16[24,4,576]{2,1,0:T(4,128)(2,1)S(1)} collective-permute-done((bf16[24,4,576]{2,1,0:T(4,128)(2,1)S(1)}, bf16[24,4,576]{2,1,0:T(4,128)(2,1)S(1)}, u32[]{:S(2)}, u32[]{:S(2)}) %collective-permute-start.2) | collective-permute-done | bytes 110624 | tf_op jit(solution)/shard_map/ppermute | solution.py:255
  23.6 0.0 collective-permute-done.5.refs_4_
  23.6 1.0 %shard_map.74 = (f32[192,512]{1,0:T(8,128)S(1)}, f32[192,1]{1,0:T(8,128)S(1)}, f32[192,1]{1,0:T(8,128)S(1)}) custom-call(f32[1,1024]{1,0:T(1,128)S(1)} %compare_select_fusion.refs_0_, bf16[96,576]{1,0:T(8,128)(2,1)S(1)} %bitcast.29, bf16[96,576]{1,0:T(8,128)(2,1)S(1)} %bitcast.32, bf16[576,512]{1,0:T(8,128)(2,1)S(1)} %broadcast_select_fusion.1.refs_3_, ...), custom_call_target="tpu_custom_call" | custom-call | tf_op jit(solution)/shard_map/pallas_call | solution.py:220
  24.5 1.0 %shard_map.73 = (f32[192,512]{1,0:T(8,128)S(1)}, f32[192,1]{1,0:T(8,128)S(1)}, f32[192,1]{1,0:T(8,128)S(1)}) custom-call(f32[1,1024]{1,0:T(1,128)S(1)} %compare_select_fusion.refs_0_, bf16[96,576]{1,0:T(8,128)(2,1)S(1)} %bitcast.22, bf16[96,576]{1,0:T(8,128)(2,1)S(1)} %bitcast.26, bf16[576,512]{1,0:T(8,128)(2,1)S(1)} %broadcast_select_fusion.1.refs_3_, ...), custom_call_target="tpu_custom_call" | custom-call | tf_op jit(solution)/shard_map/pallas_call | solution.py:220
  25.5 1.1 %shard_map.75 = (f32[384,512]{1,0:T(8,128)S(1)}, f32[384,1]{1,0:T(8,128)S(1)}, f32[384,1]{1,0:T(8,128)S(1)}) custom-call(f32[1,512]{1,0:T(1,128)S(1)} %compare_select_fusion.1.refs_0_, bf16[96,576]{1,0:T(8,128)(2,1)S(1)} %bitcast.23, bf16[96,576]{1,0:T(8,128)(2,1)S(1)} %bitcast.27, bf16[96,576]{1,0:T(8,128)(2,1)S(1)} %bitcast.30, ...), custom_call_target="tpu_custom_call" | custom-call | tf_op jit(solution)/shard_map/pallas_call | solution.py:220
  26.6 0.0 collective-permute-done.4.refs_5_
  26.6 1.1 %shard_map.76 = (f32[96,512]{1,0:T(8,128)S(1)}, f32[96,1]{1,0:T(8,128)S(1)}, f32[96,1]{1,0:T(8,128)S(1)}, bf16[104,512]{1,0:T(8,128)(2,1)S(1)}, bf16[104,512]{1,...) custom-call(f32[1,512]{1,0:T(1,128)S(1)} %compare_select_fusion.2.refs_0_, bf16[96,576]{1,0:T(8,128)(2,1)S(1)} %bitcast.24, ...), custom_call_target="tpu_custom_call" | custom-call | tf_op jit(solution)/shard_map/pallas_call | solution.py:220
  27.7 3.8 %collective-permute-start.6 = (bf16[104,512]{1,0:T(8,128)(2,1)S(1)}, bf16[104,512]{1,0:T(8,128)(2,1)S(1)}, u32[]{:S(2)}, u32[]{:S(2)}) collective-permute-start(bf16[104,512]{1,0:T(8,128)(2,1)S(1)} %get-tuple-element.41), channel_id=1, source_target_pairs={{0,12},{1,13},{2,14},{3,15},{4,8},{5,9},{6,10},{7,11},{8,4},{9,5},... | collective-permute-start | bytes 319496 | tf_op jit(solution)/shard_map/ppermute | solution.py:255
  31.6 0.0 collective-permute-start.7
  31.6 0.0 copy-start
  31.6 0.0 copy-start.1
  31.6 0.0 copy-start.2
  31.6 0.6 %collective-permute-start.8 = (bf16[104,512]{1,0:T(8,128)(2,1)S(1)}, bf16[104,512]{1,0:T(8,128)(2,1)S(1)}, u32[]{:S(2)}, u32[]{:S(2)}) collective-permute-start(bf16[104,512]{1,0:T(8,128)(2,1)S(1)} %get-tuple-element.43), channel_id=1, source_target_pairs={{0,4},{1,5},{2,6},{3,7},{4,0},{5,1},{6,2},{7,3},{8,12},{9,13},{10,... | collective-permute-start | bytes 319496 | tf_op jit(solution)/shard_map/ppermute | solution.py:255
  32.2 3.6 %broadcast_select_fusion.refs_10_ = bf16[512,7168]{1,0:T(8,128)(2,1)S(1)} fusion(bf16[512,7168]{1,0:T(8,128)(2,1)} %param.13, pred[]{:T(512)S(6)} %gt.4), kind=kLoop, calls=%fused_computation | loop fusion | flops 3670016 | bytes 14680065 | tf_op jit(solution)/shard_map/jit(_where)/select_n | solution.py:258
  35.8 0.0 copy-done
  35.8 0.0 copy-done.1
  35.8 0.0 copy-done.2
  35.8 0.9 %shard_map.77 = (f32[96,512]{1,0:T(8,128)S(1)}, f32[96,1]{1,0:T(8,128)S(1)}, f32[96,1]{1,0:T(8,128)S(1)}, bf16[4,512,128]{2,1,0:T(8,128)(2,1)S(1)}) custom-call(bf16[96,576]{1,0:T(8,128)(2,1)S(1)} %bitcast.25, bf16[24,576]{1,0:T(8,128)(2,1)S(1)} %bitcast.35, s32[1,24]{1,0:T(1,128)S(1)} %copy-done.2, bf16[4,512,128]{2,1,0:T(8,128)(2,1)S(1)} %copy-done), custom_call_target="tpu_custom_call" | custom-call | tf_op jit(solution)/shard_map/pallas_call | solution.py:220
  36.8 0.0 collective-permute-done.6.refs_0_
  36.8 3.6 %collective-permute-done.7.refs_1_ = bf16[104,512]{1,0:T(8,128)(2,1)S(1)} collective-permute-done((bf16[104,512]{1,0:T(8,128)(2,1)S(1)}, bf16[104,512]{1,0:T(8,128)(2,1)S(1)}, u32[]{:S(2)}, u32[]{:S(2)}) %collective-permute-start.7) | collective-permute-done | bytes 106528 | tf_op jit(solution)/shard_map/ppermute | solution.py:255
  40.4 0.0 collective-permute-done.8.refs_2_
  40.4 1.7 %shard_map.78 = (f32[8,24,448]{2,1,0:T(8,128)S(1)}, bf16[8,24,448]{2,1,0:T(8,128)(2,1)S(1)}) custom-call(bf16[104,512]{1,0:T(8,128)(2,1)S(1)} %collective-permute-done.6.refs_0_, bf16[104,512]{1,0:T(8,128)(2,1)S(1)} %collective-permute-done.7.refs_1_, bf16[104,512]{1,0:T(8,128)(2,1)S(1)} %collective-permute-done.8.refs_2_, ...), custom_call_target="tpu_custom_call" | custom-call | tf_op jit(solution)/shard_map/pallas_call | solution.py:220
  42.1 0.1 collective-permute-start.9
  42.2 1.4 %collective-permute-done.9.got_ref = bf16[8,24,448]{2,1,0:T(8,128)(2,1)S(1)} collective-permute-done((bf16[8,24,448]{2,1,0:T(8,128)(2,1)S(1)}, bf16[8,24,448]{2,1,0:T(8,128)(2,1)S(1)}, u32[]{:S(2)}, u32[]{:S(2)}) %collective-permute-start.9) | collective-permute-done | bytes 172064 | tf_op jit(solution)/shard_map/ppermute | solution.py:255
  43.6 1.6 %collective-permute-start.10 = (bf16[4,24,448]{2,1,0:T(8,128)(2,1)S(1)}, bf16[4,24,448]{2,1,0:T(8,128)(2,1)S(1)}, u32[]{:S(2)}, u32[]{:S(2)}) collective-permute-start(bf16[4,24,448]{2,1,0:T(8,128)(2,1)S(1)} %get-tuple-element.54), channel_id=1, source_target_pairs={{0,2},{1,3},{2,0},{3,1},{4,6},{5,7},{6,4},{7,5},{8,10},{9,11},{10,... | collective-permute-start | bytes 258056 | tf_op jit(solution)/shard_map/ppermute | solution.py:255
  45.2 3.3 %collective-permute-done.10.got_ref = bf16[4,24,448]{2,1,0:T(8,128)(2,1)S(1)} collective-permute-done((bf16[4,24,448]{2,1,0:T(8,128)(2,1)S(1)}, bf16[4,24,448]{2,1,0:T(8,128)(2,1)S(1)}, u32[]{:S(2)}, u32[]{:S(2)}) %collective-permute-start.10) | collective-permute-done | bytes 86048 | tf_op jit(solution)/shard_map/ppermute | solution.py:255
  48.5 2.5 %collective-permute-start.11 = (bf16[24,448]{1,0:T(8,128)(2,1)S(1)}, bf16[24,448]{1,0:T(8,128)(2,1)S(1)}, u32[]{:S(2)}, u32[]{:S(2)}) collective-permute-start(bf16[24,448]{1,0:T(8,128)(2,1)S(1)} %get-tuple-element.56), channel_id=1, source_target_pairs={{0,12},{1,13},{2,14},{3,15},{4,8},{5,9},{6,10},{7,11},{8,4},{9,5},... | collective-permute-start | bytes 64520 | tf_op jit(solution)/shard_map/ppermute | solution.py:255
  51.1 0.0 collective-permute-start.12
  51.1 1.9 %collective-permute-start.13 = (bf16[24,448]{1,0:T(8,128)(2,1)S(1)}, bf16[24,448]{1,0:T(8,128)(2,1)S(1)}, u32[]{:S(2)}, u32[]{:S(2)}) collective-permute-start(bf16[24,448]{1,0:T(8,128)(2,1)S(1)} %get-tuple-element.58), channel_id=1, source_target_pairs={{0,4},{1,5},{2,6},{3,7},{4,0},{5,1},{6,2},{7,3},{8,12},{9,13},{10,... | collective-permute-start | bytes 64520 | tf_op jit(solution)/shard_map/ppermute | solution.py:255
  53.0 1.2 %collective-permute-done.11 = bf16[24,448]{1,0:T(8,128)(2,1)S(1)} collective-permute-done((bf16[24,448]{1,0:T(8,128)(2,1)S(1)}, bf16[24,448]{1,0:T(8,128)(2,1)S(1)}, u32[]{:S(2)}, u32[]{:S(2)}) %collective-permute-start.11) | collective-permute-done | bytes 21536 | tf_op jit(solution)/shard_map/ppermute | solution.py:255
  54.2 1.6 %collective-permute-done.12 = bf16[24,448]{1,0:T(8,128)(2,1)S(1)} collective-permute-done((bf16[24,448]{1,0:T(8,128)(2,1)S(1)}, bf16[24,448]{1,0:T(8,128)(2,1)S(1)}, u32[]{:S(2)}, u32[]{:S(2)}) %collective-permute-start.12) | collective-permute-done | bytes 21536 | tf_op jit(solution)/shard_map/ppermute | solution.py:255
  55.8 0.0 collective-permute-done.13
  55.8 0.6 %add_convert_fusion = bf16[24,448]{1,0:T(8,128)(2,1)} fusion(bf16[24,448]{1,0:T(8,128)(2,1)S(1)} %collective-permute-done.13, bf16[24,448]{1,0:T(8,128)(2,1)S(1)} %collective-permute-done.12, f32[24,448]{1,0:T(8,128)S(1)} %get-tuple-element.55, bf16[24,448]{1,0:T(8,128)(2,1)S(1)} %collective-permute-done.11), kind=kLoop, calls=%fused_computation.2 | loop fusion | flops 75264 | bytes 129024 | tf_op jit(solution)/shard_map/convert_element_type | solution.py:325
  (10 shorter events, 0.1 us)
Async XLA Ops:
  0.0 16.5 %collective-permute-start.3 = (bf16[576,512]{1,0:T(8,128)(2,1)}, bf16[576,512]{1,0:T(8,128)(2,1)S(1)}, u32[]{:S(2)}, u32[]{:S(2)}) collective-permute-start(bf16[576,512]{1,0:T(8,128)(2,1)} %bitcast.36), channel_id=1, source_target_pairs={{0,2},{1,3},{2,0},{3,1},{4,6},{5,7},{6,4},{7,5},{8,10},{9,11},{10,... | collective-permute-start | bytes 1769480 | tf_op jit(solution)/shard_map/ppermute | solution.py:255
  3.0 14.7 %collective-permute-start = (bf16[24,4,576]{2,1,0:T(4,128)(2,1)}, bf16[24,4,576]{2,1,0:T(4,128)(2,1)S(1)}, u32[]{:S(2)}, u32[]{:S(2)}) collective-permute-start(bf16[24,4,576]{2,1,0:T(4,128)(2,1)} %bitcast.38), channel_id=1, source_target_pairs={{0,8},{1,9},{2,10},{3,11},{4,12},{5,13},{6,14},{7,15},{8,0},{9,1},... | collective-permute-start | bytes 331784 | tf_op jit(solution)/shard_map/ppermute | solution.py:255
  5.6 14.0 %collective-permute-start.1 = (bf16[24,4,576]{2,1,0:T(4,128)(2,1)}, bf16[24,4,576]{2,1,0:T(4,128)(2,1)S(1)}, u32[]{:S(2)}, u32[]{:S(2)}) collective-permute-start(bf16[24,4,576]{2,1,0:T(4,128)(2,1)} %bitcast.39), channel_id=1, source_target_pairs={{0,4},{1,5},{2,6},{3,7},{4,0},{5,1},{6,2},{7,3},{8,12},{9,13},{10,... | collective-permute-start | bytes 331784 | tf_op jit(solution)/shard_map/ppermute | solution.py:255
  7.2 16.4 %collective-permute-start.5 = (bf16[576,512]{1,0:T(8,128)(2,1)}, bf16[576,512]{1,0:T(8,128)(2,1)S(1)}, u32[]{:S(2)}, u32[]{:S(2)}) collective-permute-start(bf16[576,512]{1,0:T(8,128)(2,1)} %bitcast.37), channel_id=1, source_target_pairs={{0,1},{1,0},{2,3},{3,2},{4,5},{5,4},{6,7},{7,6},{8,9},{9,8},{10,11... | collective-permute-start | bytes 1769480 | tf_op jit(solution)/shard_map/ppermute | solution.py:255
  16.5 10.1 %collective-permute-start.4 = (bf16[576,512]{1,0:T(8,128)(2,1)S(1)}, bf16[576,512]{1,0:T(8,128)(2,1)S(1)}, u32[]{:S(2)}, u32[]{:S(2)}) collective-permute-start(bf16[576,512]{1,0:T(8,128)(2,1)S(1)} %collective-permute-done.3.refs_5_), channel_id=1, source_target_pairs={{0,1},{1,0},{2,3},{3,2},{4,5},{5,4},{6,7},{7,6},{8,9},{9,8},{10,11... | collective-permute-start | bytes 1769480 | tf_op jit(solution)/shard_map/ppermute | solution.py:255
  17.7 5.9 %collective-permute-start.2 = (bf16[24,4,576]{2,1,0:T(4,128)(2,1)S(1)}, bf16[24,4,576]{2,1,0:T(4,128)(2,1)S(1)}, u32[]{:S(2)}, u32[]{:S(2)}) collective-permute-start(bf16[24,4,576]{2,1,0:T(4,128)(2,1)S(1)} %collective-permute-done), channel_id=1, source_target_pairs={{0,4},{1,5},{2,6},{3,7},{4,0},{5,1},{6,2},{7,3},{8,12},{9,13},{10,... | collective-permute-start | bytes 331784 | tf_op jit(solution)/shard_map/ppermute | solution.py:255
  27.7 9.0 %collective-permute-start.6 = (bf16[104,512]{1,0:T(8,128)(2,1)S(1)}, bf16[104,512]{1,0:T(8,128)(2,1)S(1)}, u32[]{:S(2)}, u32[]{:S(2)}) collective-permute-start(bf16[104,512]{1,0:T(8,128)(2,1)S(1)} %get-tuple-element.41), channel_id=1, source_target_pairs={{0,12},{1,13},{2,14},{3,15},{4,8},{5,9},{6,10},{7,11},{8,4},{9,5},... | collective-permute-start | bytes 319496 | tf_op jit(solution)/shard_map/ppermute | solution.py:255
  31.6 8.8 %collective-permute-start.7 = (bf16[104,512]{1,0:T(8,128)(2,1)S(1)}, bf16[104,512]{1,0:T(8,128)(2,1)S(1)}, u32[]{:S(2)}, u32[]{:S(2)}) collective-permute-start(bf16[104,512]{1,0:T(8,128)(2,1)S(1)} %get-tuple-element.42), channel_id=1, source_target_pairs={{0,8},{1,9},{2,10},{3,11},{4,12},{5,13},{6,14},{7,15},{8,0},{9,1},... | collective-permute-start | bytes 319496 | tf_op jit(solution)/shard_map/ppermute | solution.py:255
  31.6 4.2 %copy-start = (bf16[4,512,128]{2,1,0:T(8,128)(2,1)S(1)}, bf16[4,512,128]{2,1,0:T(8,128)(2,1)}, u32[]{:S(2)}) copy-start(bf16[4,512,128]{2,1,0:T(8,128)(2,1)} %up_from.1) | copy-start | bytes 1572868
  31.6 4.2 %copy-start.1 = (bf16[1,24,576]{2,1,0:T(8,128)(2,1)S(1)}, bf16[1,24,576]{2,1,0:T(8,128)(2,1)}, u32[]{:S(2)}) copy-start(bf16[1,24,576]{2,1,0:T(8,128)(2,1)} %param.9) | copy-start | bytes 82948
  31.6 4.2 %copy-start.2 = (s32[1,24]{1,0:T(1,128)S(1)}, s32[1,24]{1,0:T(1,128)}, u32[]{:S(2)}) copy-start(s32[1,24]{1,0:T(1,128)} %parents_ref.1) | copy-start | bytes 292
  31.6 8.8 %collective-permute-start.8 = (bf16[104,512]{1,0:T(8,128)(2,1)S(1)}, bf16[104,512]{1,0:T(8,128)(2,1)S(1)}, u32[]{:S(2)}, u32[]{:S(2)}) collective-permute-start(bf16[104,512]{1,0:T(8,128)(2,1)S(1)} %get-tuple-element.43), channel_id=1, source_target_pairs={{0,4},{1,5},{2,6},{3,7},{4,0},{5,1},{6,2},{7,3},{8,12},{9,13},{10,... | collective-permute-start | bytes 319496 | tf_op jit(solution)/shard_map/ppermute | solution.py:255
  42.1 1.5 %collective-permute-start.9 = (bf16[8,24,448]{2,1,0:T(8,128)(2,1)S(1)}, bf16[8,24,448]{2,1,0:T(8,128)(2,1)S(1)}, u32[]{:S(2)}, u32[]{:S(2)}) collective-permute-start(bf16[8,24,448]{2,1,0:T(8,128)(2,1)S(1)} %get-tuple-element.52), channel_id=1, source_target_pairs={{0,1},{1,0},{2,3},{3,2},{4,5},{5,4},{6,7},{7,6},{8,9},{9,8},{10,11... | collective-permute-start | bytes 516104 | tf_op jit(solution)/shard_map/ppermute | solution.py:255
  43.6 4.9 %collective-permute-start.10 = (bf16[4,24,448]{2,1,0:T(8,128)(2,1)S(1)}, bf16[4,24,448]{2,1,0:T(8,128)(2,1)S(1)}, u32[]{:S(2)}, u32[]{:S(2)}) collective-permute-start(bf16[4,24,448]{2,1,0:T(8,128)(2,1)S(1)} %get-tuple-element.54), channel_id=1, source_target_pairs={{0,2},{1,3},{2,0},{3,1},{4,6},{5,7},{6,4},{7,5},{8,10},{9,11},{10,... | collective-permute-start | bytes 258056 | tf_op jit(solution)/shard_map/ppermute | solution.py:255
  48.5 5.7 %collective-permute-start.11 = (bf16[24,448]{1,0:T(8,128)(2,1)S(1)}, bf16[24,448]{1,0:T(8,128)(2,1)S(1)}, u32[]{:S(2)}, u32[]{:S(2)}) collective-permute-start(bf16[24,448]{1,0:T(8,128)(2,1)S(1)} %get-tuple-element.56), channel_id=1, source_target_pairs={{0,12},{1,13},{2,14},{3,15},{4,8},{5,9},{6,10},{7,11},{8,4},{9,5},... | collective-permute-start | bytes 64520 | tf_op jit(solution)/shard_map/ppermute | solution.py:255
  51.1 4.7 %collective-permute-start.12 = (bf16[24,448]{1,0:T(8,128)(2,1)S(1)}, bf16[24,448]{1,0:T(8,128)(2,1)S(1)}, u32[]{:S(2)}, u32[]{:S(2)}) collective-permute-start(bf16[24,448]{1,0:T(8,128)(2,1)S(1)} %get-tuple-element.57), channel_id=1, source_target_pairs={{0,8},{1,9},{2,10},{3,11},{4,12},{5,13},{6,14},{7,15},{8,0},{9,1},... | collective-permute-start | bytes 64520 | tf_op jit(solution)/shard_map/ppermute | solution.py:255
  51.1 4.7 %collective-permute-start.13 = (bf16[24,448]{1,0:T(8,128)(2,1)S(1)}, bf16[24,448]{1,0:T(8,128)(2,1)S(1)}, u32[]{:S(2)}, u32[]{:S(2)}) collective-permute-start(bf16[24,448]{1,0:T(8,128)(2,1)S(1)} %get-tuple-element.58), channel_id=1, source_target_pairs={{0,4},{1,5},{2,6},{3,7},{4,0},{5,1},{6,2},{7,3},{8,12},{9,13},{10,... | collective-permute-start | bytes 64520 | tf_op jit(solution)/shard_map/ppermute | solution.py:255

commit v4 on v3

--- a/solution.py
+++ b/solution.py
@@ -55,11 +55,22 @@
     return jnp.where(reach > 0.5, 0.0, neg_fill)
 
 
-def draft_kernel(
-    q_ref, keys_ref, parents_ref, up_from, numer_ref, top_ref, total_ref, up_ref
-):
+def merge(states):
+    best = states[0][1]
+    for state in states[1:]:
+        best = jnp.maximum(best, state[1])
+    numer = total = 0.0
+    for part, top, count in states:
+        factor = jnp.exp2(top - best)
+        numer = numer + part * factor
+        total = total + count * factor
+    return numer, best, total
+
+
+def draft_kernel(q_ref, keys_ref, parents_ref, up_from, *refs):
+    own_refs, out_refs, up_ref = refs[:3], refs[3:6], refs[6]
     up_ref[...] = up_from[...]
-    latent = numer_ref.shape[1]
+    latent = own_refs[0].shape[1]
     keys = keys_ref[...]
     repeats = q_ref.shape[0] // keys.shape[0]
     bias = jnp.concatenate([tree_bias(parents_ref[...])] * repeats, axis=0)
@@ -67,9 +78,8 @@
     masked = scores * log2_scale + bias
     top = jnp.max(masked, axis=1, keepdims=True)
     weights, total = weights_of(masked, top)
-    numer_ref[...] = jnp.dot(weights, keys[:, :latent], preferred_element_type=jnp.float32)
-    top_ref[...] = top
-    total_ref[...] = total
+    numer = jnp.dot(weights, keys[:, :latent], preferred_element_type=jnp.float32)
+    put(merge([(numer, top, total), tuple(ref[...] for ref in own_refs)]), out_refs)
 
 
 def fold(rows, key_refs, bias_ref, carry, latent):
@@ -100,19 +110,28 @@
     return jnp.concatenate([q[...] for q in q_refs], axis=0)
 
 
+def put(state, refs):
+    blocks = len(refs) // 3
+    each = refs[0].shape[0]
+    for block in range(blocks):
+        for part in range(3):
+            refs[3 * block + part][...] = state[part][block * each : (block + 1) * each]
+
+
 def first_kernel(peers, bias_ref, *refs):
-    q_refs, key_refs, out_refs = refs[:peers], refs[peers:-3], refs[-3:]
-    state = fold(join_rows(q_refs), key_refs, bias_ref, None, out_refs[0].shape[1])
-    for out_ref, value in zip(out_refs, state):
-        out_ref[...] = value
+    q_refs, key_refs, out_refs = refs[:peers], refs[peers : -3 * peers], refs[-3 * peers :]
+    put(fold(join_rows(q_refs), key_refs, bias_ref, None, out_refs[0].shape[1]), out_refs)
+
+
+def carried(refs):
+    return tuple(join_rows(refs[part::3]) for part in range(3))
 
 
 def middle_kernel(peers, bias_ref, *refs):
-    q_refs, (key_ref, *carry_refs), out_refs = refs[:peers], refs[peers:-3], refs[-3:]
-    carry = tuple(join_rows(carry_refs[part::3]) for part in range(3))
-    state = fold(join_rows(q_refs), [key_ref], bias_ref, carry, out_refs[0].shape[1])
-    for out_ref, value in zip(out_refs, state):
-        out_ref[...] = value
+    q_refs, (key_ref, *refs) = refs[:peers], refs[peers:]
+    carry_refs, out_refs = refs[: 3 * peers], refs[3 * peers :]
+    latent = out_refs[0].shape[1]
+    put(fold(join_rows(q_refs), [key_ref], bias_ref, carried(carry_refs), latent), out_refs)
 
 
 def pieces(row):
@@ -122,53 +141,51 @@
     return [high, middle, rest - middle]
 
 
-def last_kernel(peers, bias_ref, *refs):
-    q_refs, (key_ref, *rest) = refs[:peers], refs[peers:]
-    numer_ref, top_ref, total_ref, own_refs, out_refs = *rest[:3], rest[3:6], rest[6:]
-    carry = (numer_ref[...], top_ref[...], total_ref[...])
-    latent = numer_ref.shape[1]
-    numer, top, total = fold(join_rows(q_refs), [key_ref], bias_ref, carry, latent)
+def pack(numer, top, total, out_ref):
+    each, latent = numer.shape
+    lanes = out_ref.shape[1]
+    for group in range(latent // lanes):
+        strip = numer[:, group * lanes : (group + 1) * lanes]
+        out_ref[group * each : (group + 1) * each, :] = strip.astype(jnp.bfloat16)
+    lines = pieces(as_row(top)) + pieces(as_row(total))
+    lines += [jnp.zeros_like(lines[0])] * (PACK_ROWS - len(lines))
+    packed = jnp.concatenate(lines, axis=0)
+    if lanes > each:
+        packed = jnp.concatenate(
+            [packed, jnp.zeros((PACK_ROWS, lanes - each), jnp.float32)], axis=1
+        )
+    out_ref[out_ref.shape[0] - PACK_ROWS :, :] = packed.astype(jnp.bfloat16)
+
+
+def unpack(state_ref, each):
+    bottom = state_ref.shape[0] - PACK_ROWS
+    lines = state_ref[bottom:, :each].astype(jnp.float32)
+    top = as_column(lines[0:1] + lines[1:2] + lines[2:3])
+    total = as_column(lines[3:4] + lines[4:5] + lines[5:6])
+    strips = [state_ref[at : at + each, :] for at in range(0, bottom, each)]
+    return jnp.concatenate(strips, axis=1).astype(jnp.float32), top, total
+
+
+def last_kernel(peers, plain, bias_ref, *refs):
+    q_refs, (key_ref, *refs) = refs[:peers], refs[peers:]
+    carry_refs, out_refs = refs[: 3 * peers], refs[3 * peers :]
+    latent = carry_refs[0].shape[1]
+    state = fold(join_rows(q_refs), [key_ref], bias_ref, carried(carry_refs), latent)
     each = q_refs[0].shape[0]
-    for own_ref, value in zip(own_refs, (numer, top, total)):
-        own_ref[...] = value[:each]
-    for peer, out_ref in enumerate(out_refs, 1):
-        here = slice(peer * each, (peer + 1) * each)
-        out_ref[:each, :] = numer[here].astype(jnp.bfloat16)
-        lines = pieces(as_row(top[here])) + pieces(as_row(total[here]))
-        lines += [jnp.zeros_like(lines[0])] * (PACK_ROWS - len(lines))
-        packed = jnp.concatenate(lines, axis=0)
-        packed = jnp.concatenate(
-            [packed, jnp.zeros((PACK_ROWS, latent - each), jnp.float32)], axis=1
-        )
-        out_ref[each:, :] = packed.astype(jnp.bfloat16)
-
-
-def project_kernel(peers, *refs):
-    state_refs, refs = refs[: peers - 1], refs[peers - 1 :]
-    full_refs, refs = refs[:6], refs[6:]
-    up_ref, proj_ref, keep_ref, send_ref, flat_ref = refs
-    each = full_refs[0].shape[0]
+    if plain:
+        put([value[:each] for value in state], out_refs[:3])
+        out_refs = out_refs[3:]
+    for peer, out_ref in enumerate(out_refs, 1 if plain else 0):
+        pack(*(value[peer * each : (peer + 1) * each] for value in state), out_ref)
+
+
+def values_of(peers, refs, flat_ref):
+    state_refs, own_refs, up_ref = refs[: peers - 1], refs[peers - 1 : peers + 2], refs[peers + 2]
+    each = own_refs[0].shape[0]
     heads, _, width = up_ref.shape
-    columns = keep_ref.shape[2]
-    span = math.lcm(2 * columns, 128)
-    blocks = proj_ref.shape[1] // span
     drafts = each // heads
-    numers = [full_refs[0][...], full_refs[3][...]]
-    tops = [full_refs[1][...], full_refs[4][...]]
-    totals = [full_refs[2][...], full_refs[5][...]]
-    for state in state_refs:
-        lines = state[each:, :each].astype(jnp.float32)
-        numers.append(state[:each, :].astype(jnp.float32))
-        tops.append(as_column(lines[0:1] + lines[1:2] + lines[2:3]))
-        totals.append(as_column(lines[3:4] + lines[4:5] + lines[5:6]))
-    best = tops[0]
-    for other in tops[1:]:
-        best = jnp.maximum(best, other)
-    numer = total = 0.0
-    for part, top, count in zip(numers, tops, totals):
-        factor = jnp.exp2(top - best)
-        numer = numer + part * factor
-        total = total + count * factor
+    states = [unpack(state, each) for state in state_refs]
+    numer, _, total = merge([tuple(ref[...] for ref in own_refs)] + states)
     latent_out = (numer / total).astype(jnp.bfloat16)
     for head in range(heads):
         value = jnp.dot(
@@ -177,23 +194,59 @@
             preferred_element_type=jnp.float32,
         )
         flat_ref[:, head * width : (head + 1) * width] = value.astype(jnp.bfloat16)
+
+
+def share(part, pair, spot, keep_ref, send_ref):
+    columns = keep_ref.shape[2]
+    first_core = lax.rem(lax.axis_index("ctx"), 2) == 0
+    halves = []
+    for side in range(2):
+        shift = (2 * pair + side) * columns
+        moved = part if shift == 0 else pltpu.roll(part, part.shape[1] - shift, 1)
+        halves.append(moved[:, :columns])
+    keep_ref[spot] = jnp.where(first_core, halves[0], halves[1])
+    send_ref[spot] = jnp.where(first_core, halves[1], halves[0]).astype(jnp.bfloat16)
+
+
+def project_kernel(across, flat, proj_ref, keep_ref, send_ref):
+    side = lax.rem(lax.div(lax.axis_index("ctx"), 2), 2)
+    side = 1 - side if across else side
+    span = 2 * keep_ref.shape[2]
+    for spot in range(keep_ref.shape[0]):
+        at = pl.multiple_of((2 * spot + side) * span, span)
+        part = jnp.dot(flat, proj_ref[:, pl.ds(at, span)], preferred_element_type=jnp.float32)
+        share(part, 0, spot, keep_ref, send_ref)
+
+
+def leaving_kernel(peers, *refs):
+    proj_ref, flat_ref, keep_ref, send_ref = refs[-4:]
+    values_of(peers, refs, flat_ref)
+    project_kernel(1, flat_ref[...], proj_ref, keep_ref, send_ref)
+
+
+def staying_kernel(flat_ref, proj_ref, keep_ref, send_ref):
+    project_kernel(0, flat_ref[...], proj_ref, keep_ref, send_ref)
+
+
+def add_kernel(keep_ref, got_ref, out_ref):
+    out_ref[...] = (keep_ref[...] + got_ref[...].astype(jnp.float32)).astype(out_ref.dtype)
+
+
+def whole_kernel(peers, *refs):
+    proj_ref, flat_ref, keep_ref, send_ref = refs[-4:]
+    values_of(peers, refs, flat_ref)
     flat = flat_ref[...]
-    first_core = lax.rem(lax.axis_index("ctx"), 2) == 0
-    for block in range(blocks):
+    columns = keep_ref.shape[2]
+    span = math.lcm(2 * columns, 128)
+    pairs = span // (2 * columns)
+    for block in range(proj_ref.shape[1] // span):
         part = jnp.dot(
             flat,
             proj_ref[:, block * span : (block + 1) * span],
             preferred_element_type=jnp.float32,
         )
-        for pair in range(span // (2 * columns)):
-            halves = []
-            for side in range(2):
-                shift = (2 * pair + side) * columns
-                moved = part if shift == 0 else pltpu.roll(part, span - shift, 1)
-                halves.append(moved[:, :columns])
-            spot = block * (span // (2 * columns)) + pair
-            keep_ref[spot] = jnp.where(first_core, halves[0], halves[1])
-            send_ref[spot] = jnp.where(first_core, halves[1], halves[0]).astype(jnp.bfloat16)
+        for pair in range(pairs):
+            share(part, pair, block * pairs + pair, keep_ref, send_ref)
 
 
 def pair_kernel(keep_ref, got_ref, stay_ref, send_ref):
@@ -267,52 +320,80 @@
         for peer in list(sent):
             sent[peer ^ bit] = swap(sent[peer], inner * bit)
         bit //= 2
-    peers = [*range(0, outer, 2), *range(1, outer, 2)]
-    rows = [jnp.transpose(sent[peer], (1, 0, 2)).reshape(each, width) for peer in peers]
+    rows = {
+        peer: jnp.transpose(value, (1, 0, 2)).reshape(each, width) for peer, value in sent.items()
+    }
     own_rows = rows[0]
+    everyone = list(range(outer))
+
+    def pick(table, peers):
+        return [table[peer] for peer in peers]
 
     def state_of(blocks):
-        return tuple(shaped(blocks * each, size) for size in (latent, 1, 1))
+        return tuple(shaped(each, size) for size in (latent, 1, 1)) * blocks
 
     own_shape = state_of(1)
     proj_here = on_chip(out_proj)
-    *drafted, up_here = call(
+    keys_here = on_chip(keys_own)
+    state = {}
+
+    def save(peers, values):
+        for spot, peer in enumerate(peers):
+            state[peer] = list(values[3 * spot : 3 * spot + 3])
+
+    for part in range(2):
+        peers = everyone[part::2]
+        values = call(
+            lambda *refs: first_kernel(outer // 2, *refs),
+            state_of(outer // 2),
+            (bias_of(0, 1), *pick(rows, peers), keys_here, keys_core),
+        )
+        save(peers, values)
+    values = call(
+        lambda *refs: middle_kernel(outer, *refs),
+        state_of(outer),
+        (bias_of(2), *pick(rows, everyone), keys_across, *sum(pick(state, everyone), [])),
+    )
+    save(everyone, values)
+    lanes = math.gcd(latent, 128)
+    packed = shaped(each * latent // lanes + PACK_ROWS, lanes, dtype=bf16)
+    got = []
+    for near in (False, True):
+        peers = everyone[: outer // 2] if near else everyone[outer // 2 :]
+        values = call(
+            lambda *refs, near=near: last_kernel(outer // 2, near, *refs),
+            (own_shape if near else ()) + (packed,) * (len(peers) - near),
+            (bias_of(3), *pick(rows, peers), keys_far, *sum(pick(state, peers), [])),
+        )
+        if near:
+            whole, values, peers = values[:3], values[3:], peers[1:]
+        got += [swap(value, inner * peer) for peer, value in zip(peers, values)]
+    proj_here = on_chip(out_proj)
+    *whole, up_here = call(
         draft_kernel,
         own_shape + (shaped(*value_up.shape, dtype=bf16),),
-        (own_rows, draft_latent[0], parents, value_up),
-    )
-    keys_here = on_chip(keys_own)
-    parts = []
-    for some in (rows[: outer // 2], rows[outer // 2 :]):
-        parts += call(
-            lambda *refs: first_kernel(outer // 2, *refs),
-            state_of(outer // 2),
-            (bias_of(0, 1), *some, keys_here, keys_core),
-        )
-    state = call(
-        lambda *refs: middle_kernel(outer, *refs),
-        state_of(outer),
-        (bias_of(2), *rows, keys_across, *parts),
-    )
-    done = call(
-        lambda *refs: last_kernel(outer, *refs),
-        own_shape
-        + tuple(shaped(each + PACK_ROWS, latent, dtype=bf16) for _ in range(outer - 1)),
-        (bias_of(3), *rows, keys_far, *state),
-    )
-    whole, states = done[:3], dict(zip(peers[1:], done[3:]))
-    got = [swap(states[peer], inner * peer) for peer in range(outer - 1, 0, -1)]
-    keep, send = call(
-        lambda *refs: project_kernel(outer, *refs),
-        (shaped(chips, drafts, columns), shaped(chips, drafts, columns, dtype=bf16)),
-        (*got, *whole, *drafted, up_here, proj_here),
-        scratch=[pltpu.VMEM((drafts, heads_here * value_up.shape[2]), bf16)],
-    )
-    stay, send = call(
-        pair_kernel,
-        (shaped(chips // 2, drafts, columns), shaped(chips // 2, drafts, columns, dtype=bf16)),
-        (keep, swap(send, 1)),
-    )
+        (own_rows, draft_latent[0], parents, value_up, *whole),
+    )
+    inputs = (*got, *whole, up_here, proj_here)
+    flat_shape = shaped(drafts, heads_here * value_up.shape[2], dtype=bf16)
+
+    def halves_of(chips):
+        return shaped(chips, drafts, columns), shaped(chips, drafts, columns, dtype=bf16)
+
+    if 2 * columns % 128 == 0:
+        flat, keep, send = call(
+            lambda *refs: leaving_kernel(outer, *refs), (flat_shape, *halves_of(chips // 2)), inputs
+        )
+        got_leaving = swap(send, 1)
+        stay, stay_send = call(staying_kernel, halves_of(chips // 2), (flat, proj_here))
+        send = call(add_kernel, (halves_of(chips // 2)[1],), (keep, got_leaving))[0]
+        got_staying = swap(stay_send, 1)
+        stay = call(add_kernel, (halves_of(chips // 2)[0],), (stay, got_staying))[0]
+    else:
+        flat, keep, send = call(
+            lambda *refs: whole_kernel(outer, *refs), (flat_shape, *halves_of(chips)), inputs
+        )
+        stay, send = call(pair_kernel, halves_of(chips // 2), (keep, swap(send, 1)))
     own, *parts = call(
         quad_kernel,
         (shaped(drafts, columns),)

time: 56.7 us -> 55.4 us (0.977)
  waiting for transfers between devices: 22.8 us -> 20.3 us
  Pallas kernels: 6.86 us -> 7.52 us
  starting transfers between devices: 19.6 us -> 20.2 us
    ppermute x14 -> x15, waiting for transfers between devices: 22.8 us -> 20.3 us  [swap(): return lax.ppermute(value, 'ctx', [(i, i ^ bits) for i in range(count)])]
    pallas_call x8 -> x11, Pallas kernels: 6.86 us -> 7.52 us  [call(): pl.pallas_call(kernel, out_shape=outs, in_specs=specs or [pl.BlockSpec()...]
    ppermute x14 -> x15, starting transfers between devices: 19.6 us -> 20.2 us  [swap(): return lax.ppermute(value, 'ctx', [(i, i ^ bits) for i in range(count)])]
  transfers between devices with their start and end apart: 14 -> 15, of which waited for: 7 -> 7; matrix products, arithmetic and copies ran while one was open for 10% -> 10% of each run, Pallas kernels for 7% -> 10%
where the time goes in v4:
time: 55.4 us; the launch traced here: 55.2 us
  waiting for transfers between devices  20.3 us (37%)
  starting transfers between devices  20.2 us (36%)
  Pallas kernels  7.52 us (14%)
  other arithmetic  5.32 us (10%)
  local copies, waits for them, and re-layouts  0.99 us (2%)
  between operations  0.87 us (2%)
    ppermute x15, waiting for transfers between devices, swap(): return lax.ppermute(value, 'ctx', [(i, i ^ bits) for i in range(count)])  20.3 us
    ppermute x15, starting transfers between devices, swap(): return lax.ppermute(value, 'ctx', [(i, i ^ bits) for i in range(count)])  20.2 us
    pallas_call x11, Pallas kernels, call(): pl.pallas_call(kernel, out_shape=outs, in_specs=specs or [pl.BlockSpec()...  7.52 us
    select_n x2, other arithmetic, on_chip(): return jnp.where(lengths[0] > -1, value, jnp.zeros_like(value))  4.67 us
  transfers between devices with their start and end apart: 15, of which 7 were waited for; matrix products, arithmetic and copies ran while one was open for 10% of the time, Pallas kernels for 10%

profile of v4, /device:TPU:0, one launch (start us, length us, event | category | flops | bytes accessed | tf_op | source)
XLA Modules:
  0.0 55.2 jit_solution(17940305938082995098)
XLA Ops:
  0.0 3.0 %collective-permute-start.2 = (bf16[576,512]{1,0:T(8,128)(2,1)}, bf16[576,512]{1,0:T(8,128)(2,1)S(1)}, u32[]{:S(2)}, u32[]{:S(2)}) collective-permute-start(bf16[576,512]{1,0:T(8,128)(2,1)} %bitcast.36), channel_id=1, source_target_pairs={{0,2},{1,3},{2,0},{3,1},{4,6},{5,7},{6,4},{7,5},{8,10},{9,11},{10,... | collective-permute-start | bytes 1769480 | tf_op jit(solution)/shard_map/ppermute | solution.py:308
  3.0 1.6 %collective-permute-start.4 = (bf16[24,4,576]{2,1,0:T(4,128)(2,1)}, bf16[24,4,576]{2,1,0:T(4,128)(2,1)S(1)}, u32[]{:S(2)}, u32[]{:S(2)}) collective-permute-start(bf16[24,4,576]{2,1,0:T(4,128)(2,1)} %bitcast.38), channel_id=1, source_target_pairs={{0,4},{1,5},{2,6},{3,7},{4,0},{5,1},{6,2},{7,3},{8,12},{9,13},{10,... | collective-permute-start | bytes 331784 | tf_op jit(solution)/shard_map/ppermute | solution.py:308
  4.6 2.6 %collective-permute-start = (bf16[24,4,576]{2,1,0:T(4,128)(2,1)}, bf16[24,4,576]{2,1,0:T(4,128)(2,1)S(1)}, u32[]{:S(2)}, u32[]{:S(2)}) collective-permute-start(bf16[24,4,576]{2,1,0:T(4,128)(2,1)} %bitcast.39), channel_id=1, source_target_pairs={{0,8},{1,9},{2,10},{3,11},{4,12},{5,13},{6,14},{7,15},{8,0},{9,1},... | collective-permute-start | bytes 331784 | tf_op jit(solution)/shard_map/ppermute | solution.py:308
  7.2 0.0 collective-permute-start.5
  7.8 0.9 %copy.10 = bf16[4,24,576]{2,1,0:T(8,128)(2,1)S(1)} copy(bf16[4,24,576]{2,0,1:T(4,128)(2,1)} %bitcast.40) | data formatting | bytes 221184 | tf_op jit(solution)/shard_map/transpose | solution.py:324
  8.8 7.8 %collective-permute-done.2.refs_5_ = bf16[576,512]{1,0:T(8,128)(2,1)S(1)} collective-permute-done((bf16[576,512]{1,0:T(8,128)(2,1)}, bf16[576,512]{1,0:T(8,128)(2,1)S(1)}, u32[]{:S(2)}, u32[]{:S(2)}) %collective-permute-start.2) | collective-permute-done | bytes 589856 | tf_op jit(solution)/shard_map/ppermute | solution.py:308
  16.5 0.0 collective-permute-start.3
  16.5 1.1 %broadcast_select_fusion.1.refs_3_ = bf16[576,512]{1,0:T(8,128)(2,1)S(1)} fusion(pred[]{:T(512)S(6)} %gt.4, bf16[1,512,576]{1,2,0:T(8,128)(2,1)} %param.8), kind=kLoop, calls=%fused_computation.1 | loop fusion | flops 294912 | bytes 1179649 | tf_op jit(solution)/shard_map/jit(_where)/select_n | solution.py:311
  17.7 0.0 collective-permute-done
  17.7 1.9 %collective-permute-start.1 = (bf16[24,4,576]{2,1,0:T(4,128)(2,1)S(1)}, bf16[24,4,576]{2,1,0:T(4,128)(2,1)S(1)}, u32[]{:S(2)}, u32[]{:S(2)}) collective-permute-start(bf16[24,4,576]{2,1,0:T(4,128)(2,1)S(1)} %collective-permute-done), channel_id=1, source_target_pairs={{0,4},{1,5},{2,6},{3,7},{4,0},{5,1},{6,2},{7,3},{8,12},{9,13},{10,... | collective-permute-start | bytes 331784 | tf_op jit(solution)/shard_map/ppermute | solution.py:308
  19.6 0.0 collective-permute-done.4
  19.6 3.9 %collective-permute-done.1 = bf16[24,4,576]{2,1,0:T(4,128)(2,1)S(1)} collective-permute-done((bf16[24,4,576]{2,1,0:T(4,128)(2,1)S(1)}, bf16[24,4,576]{2,1,0:T(4,128)(2,1)S(1)}, u32[]{:S(2)}, u32[]{:S(2)}) %collective-permute-start.1) | collective-permute-done | bytes 110624 | tf_op jit(solution)/shard_map/ppermute | solution.py:308
  23.6 0.0 collective-permute-done.5.refs_4_
  23.6 1.0 %shard_map.74 = (f32[96,512]{1,0:T(8,128)S(1)}, f32[96,1]{1,0:T(8,128)S(1)}, f32[96,1]{1,0:T(8,128)S(1)}, f32[96,512]{1,0:T(8,128)S(1)}, f32[96,1]{1,0:T(8,128)S(1)}, /*index=5*/f32[96,1]{1,0:T(8,128)S(1)}) custom-call(f32[1,1024]{1,0:T(1,128)S(1)} %compare_select_fusion.refs_0_, bf16[96,576]{1,0:T(8,128)(2,1)S(1)} %bitcast.26, ...), custom_call_target="tpu_custom_call" | custom-call | tf_op jit(solution)/shard_map/pallas_call | solution.py:273
  24.5 1.0 %shard_map.73 = (f32[96,512]{1,0:T(8,128)S(1)}, f32[96,1]{1,0:T(8,128)S(1)}, f32[96,1]{1,0:T(8,128)S(1)}, f32[96,512]{1,0:T(8,128)S(1)}, f32[96,1]{1,0:T(8,128)S(1)}, /*index=5*/f32[96,1]{1,0:T(8,128)S(1)}) custom-call(f32[1,1024]{1,0:T(1,128)S(1)} %compare_select_fusion.refs_0_, bf16[96,576]{1,0:T(8,128)(2,1)S(1)} %bitcast.22, ...), custom_call_target="tpu_custom_call" | custom-call | tf_op jit(solution)/shard_map/pallas_call | solution.py:273
  25.5 1.1 %shard_map.75 = (f32[96,512]{1,0:T(8,128)S(1)}, f32[96,1]{1,0:T(8,128)S(1)}, f32[96,1]{1,0:T(8,128)S(1)}, f32[96,512]{1,0:T(8,128)S(1)}, f32[96,1]{1,0:T(8,128)S...) custom-call(f32[1,512]{1,0:T(1,128)S(1)} %compare_select_fusion.1.re, ...), custom_call_target="tpu_custom_call" | custom-call | tf_op jit(solution)/shard_map/pallas_call | solution.py:273
  26.6 0.0 collective-permute-done.3.refs_3_
  26.6 0.8 %shard_map.76 = (bf16[392,128]{1,0:T(8,128)(2,1)S(1)}, bf16[392,128]{1,0:T(8,128)(2,1)S(1)}) custom-call(f32[1,512]{1,0:T(1,128)S(1)} %compare_select_fusion.2.refs_0_, bf16[96,576]{1,0:T(8,128)(2,1)S(1)} %bitcast.31, bf16[96,576]{1,0:T(8,128)(2,1)S(1)} %bitcast.34, bf16[576,512]{1,0:T(8,128)(2,1)S(1)} %collective-permute-done.3.refs_3_, ...), custom_call_target="tpu_custom_call" | custom-call | tf_op jit(solution)/shard_map/pallas_call | solution.py:273
  27.4 2.8 %collective-permute-start.6 = (bf16[392,128]{1,0:T(8,128)(2,1)S(1)}, bf16[392,128]{1,0:T(8,128)(2,1)S(1)}, u32[]{:S(2)}, u32[]{:S(2)}) collective-permute-start(bf16[392,128]{1,0:T(8,128)(2,1)S(1)} %get-tuple-element.66), channel_id=1, source_target_pairs={{0,8},{1,9},{2,10},{3,11},{4,12},{5,13},{6,14},{7,15},{8,0},{9,1},... | collective-permute-start | bytes 301064 | tf_op jit(solution)/shard_map/ppermute | solution.py:308
  30.2 1.3 %collective-permute-start.7 = (bf16[392,128]{1,0:T(8,128)(2,1)S(1)}, bf16[392,128]{1,0:T(8,128)(2,1)S(1)}, u32[]{:S(2)}, u32[]{:S(2)}) collective-permute-start(bf16[392,128]{1,0:T(8,128)(2,1)S(1)} %get-tuple-element.67), channel_id=1, source_target_pairs={{0,12},{1,13},{2,14},{3,15},{4,8},{5,9},{6,10},{7,11},{8,4},{9,5},... | collective-permute-start | bytes 301064 | tf_op jit(solution)/shard_map/ppermute | solution.py:308
  31.6 0.8 %shard_map.77 = (f32[96,512]{1,0:T(8,128)S(1)}, f32[96,1]{1,0:T(8,128)S(1)}, f32[96,1]{1,0:T(8,128)S(1)}, bf16[392,128]{1,0:T(8,128)(2,1)S(1)}) custom-call(f32[1,512]{1,0:T(1,128)S(1)} %compare_select_fusion.2.refs_0_, bf16[96,576]{1,0:T(8,128)(2,1)S(1)} %bitcast.24, bf16[96,576]{1,0:T(8,128)(2,1)S(1)} %bitcast.28, ...), custom_call_target="tpu_custom_call" | custom-call | tf_op jit(solution)/shard_map/pallas_call | solution.py:273
  32.3 0.0 copy-start
  32.3 0.0 copy-start.1
  32.4 0.0 copy-start.2
  32.4 0.3 collective-permute-start.8
  32.7 3.6 %broadcast_select_fusion.refs_7_.proj_ref = bf16[512,7168]{1,0:T(8,128)(2,1)S(1)} fusion(bf16[512,7168]{1,0:T(8,128)(2,1)} %param.13, pred[]{:T(512)S(6)} %gt.4), kind=kLoop, calls=%fused_computation | loop fusion | flops 3670016 | bytes 14680065 | tf_op jit(solution)/shard_map/jit(_where)/select_n | solution.py:311
  36.2 0.0 copy-done
  36.2 0.0 copy-done.1
  36.2 0.0 copy-done.2
  36.3 1.0 %shard_map.78 = (f32[96,512]{1,0:T(8,128)S(1)}, f32[96,1]{1,0:T(8,128)S(1)}, f32[96,1]{1,0:T(8,128)S(1)}, bf16[4,512,128]{2,1,0:T(8,128)(2,1)S(1)}) custom-call(bf16[96,576]{1,0:T(8,128)(2,1)S(1)} %bitcast.25, bf16[24,576]{1,0:T(8,128)(2,1)S(1)} %bitcast.35, s32[1,24]{1,0:T(1,128)S(1)} %copy-done.2, bf16[4,512,128]{2,1,0:T(8,128)(2,1)S(1)} %copy-done, ...), custom_call_target="tpu_custom_call" | custom-call | tf_op jit(solution)/shard_map/pallas_call | solution.py:273
  37.2 0.8 %collective-permute-done.6.refs_0_ = bf16[392,128]{1,0:T(8,128)(2,1)S(1)} collective-permute-done((bf16[392,128]{1,0:T(8,128)(2,1)S(1)}, bf16[392,128]{1,0:T(8,128)(2,1)S(1)}, u32[]{:S(2)}, u32[]{:S(2)}) %collective-permute-start.6) | collective-permute-done | bytes 100384 | tf_op jit(solution)/shard_map/ppermute | solution.py:308
  38.0 0.0 collective-permute-done.7.refs_1_
  38.0 1.2 %collective-permute-done.8.refs_2_ = bf16[392,128]{1,0:T(8,128)(2,1)S(1)} collective-permute-done((bf16[392,128]{1,0:T(8,128)(2,1)S(1)}, bf16[392,128]{1,0:T(8,128)(2,1)S(1)}, u32[]{:S(2)}, u32[]{:S(2)}) %collective-permute-start.8) | collective-permute-done | bytes 100384 | tf_op jit(solution)/shard_map/ppermute | solution.py:308
  39.2 1.1 %shard_map.79 = (bf16[24,512]{1,0:T(8,128)(2,1)S(1)}, f32[4,24,448]{2,1,0:T(8,128)S(1)}, bf16[4,24,448]{2,1,0:T(8,128)(2,1)S(1)}) custom-call(bf16[392,128]{1,0:T(8,128)(2,1)S(1)} %collective-permute-done.6.refs_0_, bf16[392,128]{1,0:T(8,128)(2,1)S(1)} %collective-permute-done.7.refs_1_, bf16[392,128]{1,0:T(8,128)(2,1)S(1)} %collective-permute-done.8.refs_2_, ...), custom_call_target="tpu_custom_call" | custom-call | tf_op jit(solution)/shard_map/pallas_call | solution.py:273
  40.3 0.1 collective-permute-start.10
  40.4 0.8 %shard_map.80 = (f32[4,24,448]{2,1,0:T(8,128)S(1)}, bf16[4,24,448]{2,1,0:T(8,128)(2,1)S(1)}) custom-call(bf16[24,512]{1,0:T(8,128)(2,1)S(1)} %get-tuple-element.82.flat_ref, bf16[512,7168]{1,0:T(8,128)(2,1)S(1)} %broadcast_select_fusion.refs_7_.proj_ref), custom_call_target="tpu_custom_call" | custom-call | tf_op jit(solution)/shard_map/pallas_call | solution.py:273
  41.2 0.5 collective-permute-start.9
  41.8 0.0 collective-permute-done.10.got_ref
  41.8 1.6 %collective-permute-start.11 = (bf16[4,24,448]{2,1,0:T(8,128)(2,1)S(1)}, bf16[4,24,448]{2,1,0:T(8,128)(2,1)S(1)}, u32[]{:S(2)}, u32[]{:S(2)}) collective-permute-start(bf16[4,24,448]{2,1,0:T(8,128)(2,1)S(1)} %shard_map.82), channel_id=1, source_target_pairs={{0,2},{1,3},{2,0},{3,1},{4,6},{5,7},{6,4},{7,5},{8,10},{9,11},{10,... | collective-permute-start | bytes 258056 | tf_op jit(solution)/shard_map/ppermute | solution.py:308
  43.4 0.0 collective-permute-done.9.got_ref
  43.5 3.2 %collective-permute-done.11.got_ref = bf16[4,24,448]{2,1,0:T(8,128)(2,1)S(1)} collective-permute-done((bf16[4,24,448]{2,1,0:T(8,128)(2,1)S(1)}, bf16[4,24,448]{2,1,0:T(8,128)(2,1)S(1)}, u32[]{:S(2)}, u32[]{:S(2)}) %collective-permute-start.11) | collective-permute-done | bytes 86048 | tf_op jit(solution)/shard_map/ppermute | solution.py:308
  46.7 3.1 %collective-permute-start.12 = (bf16[24,448]{1,0:T(8,128)(2,1)S(1)}, bf16[24,448]{1,0:T(8,128)(2,1)S(1)}, u32[]{:S(2)}, u32[]{:S(2)}) collective-permute-start(bf16[24,448]{1,0:T(8,128)(2,1)S(1)} %get-tuple-element.88), channel_id=1, source_target_pairs={{0,12},{1,13},{2,14},{3,15},{4,8},{5,9},{6,10},{7,11},{8,4},{9,5},... | collective-permute-start | bytes 64520 | tf_op jit(solution)/shard_map/ppermute | solution.py:308
  49.8 0.0 collective-permute-start.13
  49.8 1.3 %collective-permute-start.14 = (bf16[24,448]{1,0:T(8,128)(2,1)S(1)}, bf16[24,448]{1,0:T(8,128)(2,1)S(1)}, u32[]{:S(2)}, u32[]{:S(2)}) collective-permute-start(bf16[24,448]{1,0:T(8,128)(2,1)S(1)} %get-tuple-element.90), channel_id=1, source_target_pairs={{0,4},{1,5},{2,6},{3,7},{4,0},{5,1},{6,2},{7,3},{8,12},{9,13},{10,... | collective-permute-start | bytes 64520 | tf_op jit(solution)/shard_map/ppermute | solution.py:308
  51.1 1.4 %collective-permute-done.12 = bf16[24,448]{1,0:T(8,128)(2,1)S(1)} collective-permute-done((bf16[24,448]{1,0:T(8,128)(2,1)S(1)}, bf16[24,448]{1,0:T(8,128)(2,1)S(1)}, u32[]{:S(2)}, u32[]{:S(2)}) %collective-permute-start.12) | collective-permute-done | bytes 21536 | tf_op jit(solution)/shard_map/ppermute | solution.py:308
  52.5 2.0 %collective-permute-done.13 = bf16[24,448]{1,0:T(8,128)(2,1)S(1)} collective-permute-done((bf16[24,448]{1,0:T(8,128)(2,1)S(1)}, bf16[24,448]{1,0:T(8,128)(2,1)S(1)}, u32[]{:S(2)}, u32[]{:S(2)}) %collective-permute-start.13) | collective-permute-done | bytes 21536 | tf_op jit(solution)/shard_map/ppermute | solution.py:308
  54.6 0.0 collective-permute-done.14
  54.6 0.6 %add_convert_fusion = bf16[24,448]{1,0:T(8,128)(2,1)} fusion(bf16[24,448]{1,0:T(8,128)(2,1)S(1)} %collective-permute-done.14, bf16[24,448]{1,0:T(8,128)(2,1)S(1)} %collective-permute-done.13, f32[24,448]{1,0:T(8,128)S(1)} %get-tuple-element.87, bf16[24,448]{1,0:T(8,128)(2,1)S(1)} %collective-permute-done.12), kind=kLoop, calls=%fused_computation.2 | loop fusion | flops 75264 | bytes 129024 | tf_op jit(solution)/shard_map/convert_element_type | solution.py:406
  (11 shorter events, 0.1 us)
Async XLA Ops:
  0.0 16.5 %collective-permute-start.2 = (bf16[576,512]{1,0:T(8,128)(2,1)}, bf16[576,512]{1,0:T(8,128)(2,1)S(1)}, u32[]{:S(2)}, u32[]{:S(2)}) collective-permute-start(bf16[576,512]{1,0:T(8,128)(2,1)} %bitcast.36), channel_id=1, source_target_pairs={{0,2},{1,3},{2,0},{3,1},{4,6},{5,7},{6,4},{7,5},{8,10},{9,11},{10,... | collective-permute-start | bytes 1769480 | tf_op jit(solution)/shard_map/ppermute | solution.py:308
  3.0 16.6 %collective-permute-start.4 = (bf16[24,4,576]{2,1,0:T(4,128)(2,1)}, bf16[24,4,576]{2,1,0:T(4,128)(2,1)S(1)}, u32[]{:S(2)}, u32[]{:S(2)}) collective-permute-start(bf16[24,4,576]{2,1,0:T(4,128)(2,1)} %bitcast.38), channel_id=1, source_target_pairs={{0,4},{1,5},{2,6},{3,7},{4,0},{5,1},{6,2},{7,3},{8,12},{9,13},{10,... | collective-permute-start | bytes 331784 | tf_op jit(solution)/shard_map/ppermute | solution.py:308
  4.6 13.1 %collective-permute-start = (bf16[24,4,576]{2,1,0:T(4,128)(2,1)}, bf16[24,4,576]{2,1,0:T(4,128)(2,1)S(1)}, u32[]{:S(2)}, u32[]{:S(2)}) collective-permute-start(bf16[24,4,576]{2,1,0:T(4,128)(2,1)} %bitcast.39), channel_id=1, source_target_pairs={{0,8},{1,9},{2,10},{3,11},{4,12},{5,13},{6,14},{7,15},{8,0},{9,1},... | collective-permute-start | bytes 331784 | tf_op jit(solution)/shard_map/ppermute | solution.py:308
  7.2 16.4 %collective-permute-start.5 = (bf16[576,512]{1,0:T(8,128)(2,1)}, bf16[576,512]{1,0:T(8,128)(2,1)S(1)}, u32[]{:S(2)}, u32[]{:S(2)}) collective-permute-start(bf16[576,512]{1,0:T(8,128)(2,1)} %bitcast.37), channel_id=1, source_target_pairs={{0,1},{1,0},{2,3},{3,2},{4,5},{5,4},{6,7},{7,6},{8,9},{9,8},{10,11... | collective-permute-start | bytes 1769480 | tf_op jit(solution)/shard_map/ppermute | solution.py:308
  16.5 10.1 %collective-permute-start.3 = (bf16[576,512]{1,0:T(8,128)(2,1)S(1)}, bf16[576,512]{1,0:T(8,128)(2,1)S(1)}, u32[]{:S(2)}, u32[]{:S(2)}) collective-permute-start(bf16[576,512]{1,0:T(8,128)(2,1)S(1)} %collective-permute-done.2.refs_5_), channel_id=1, source_target_pairs={{0,1},{1,0},{2,3},{3,2},{4,5},{5,4},{6,7},{7,6},{8,9},{9,8},{10,11... | collective-permute-start | bytes 1769480 | tf_op jit(solution)/shard_map/ppermute | solution.py:308
  17.7 5.9 %collective-permute-start.1 = (bf16[24,4,576]{2,1,0:T(4,128)(2,1)S(1)}, bf16[24,4,576]{2,1,0:T(4,128)(2,1)S(1)}, u32[]{:S(2)}, u32[]{:S(2)}) collective-permute-start(bf16[24,4,576]{2,1,0:T(4,128)(2,1)S(1)} %collective-permute-done), channel_id=1, source_target_pairs={{0,4},{1,5},{2,6},{3,7},{4,0},{5,1},{6,2},{7,3},{8,12},{9,13},{10,... | collective-permute-start | bytes 331784 | tf_op jit(solution)/shard_map/ppermute | solution.py:308
  27.4 10.6 %collective-permute-start.6 = (bf16[392,128]{1,0:T(8,128)(2,1)S(1)}, bf16[392,128]{1,0:T(8,128)(2,1)S(1)}, u32[]{:S(2)}, u32[]{:S(2)}) collective-permute-start(bf16[392,128]{1,0:T(8,128)(2,1)S(1)} %get-tuple-element.66), channel_id=1, source_target_pairs={{0,8},{1,9},{2,10},{3,11},{4,12},{5,13},{6,14},{7,15},{8,0},{9,1},... | collective-permute-start | bytes 301064 | tf_op jit(solution)/shard_map/ppermute | solution.py:308
  30.2 7.8 %collective-permute-start.7 = (bf16[392,128]{1,0:T(8,128)(2,1)S(1)}, bf16[392,128]{1,0:T(8,128)(2,1)S(1)}, u32[]{:S(2)}, u32[]{:S(2)}) collective-permute-start(bf16[392,128]{1,0:T(8,128)(2,1)S(1)} %get-tuple-element.67), channel_id=1, source_target_pairs={{0,12},{1,13},{2,14},{3,15},{4,8},{5,9},{6,10},{7,11},{8,4},{9,5},... | collective-permute-start | bytes 301064 | tf_op jit(solution)/shard_map/ppermute | solution.py:308
  32.3 3.9 %copy-start = (bf16[4,512,128]{2,1,0:T(8,128)(2,1)S(1)}, bf16[4,512,128]{2,1,0:T(8,128)(2,1)}, u32[]{:S(2)}) copy-start(bf16[4,512,128]{2,1,0:T(8,128)(2,1)} %up_from.1) | copy-start | bytes 1572868
  32.3 3.9 %copy-start.1 = (bf16[1,24,576]{2,1,0:T(8,128)(2,1)S(1)}, bf16[1,24,576]{2,1,0:T(8,128)(2,1)}, u32[]{:S(2)}) copy-start(bf16[1,24,576]{2,1,0:T(8,128)(2,1)} %param.9) | copy-start | bytes 82948
  32.4 3.9 %copy-start.2 = (s32[1,24]{1,0:T(1,128)S(1)}, s32[1,24]{1,0:T(1,128)}, u32[]{:S(2)}) copy-start(s32[1,24]{1,0:T(1,128)} %parents_ref.1) | copy-start | bytes 292
  32.4 6.8 %collective-permute-start.8 = (bf16[392,128]{1,0:T(8,128)(2,1)S(1)}, bf16[392,128]{1,0:T(8,128)(2,1)S(1)}, u32[]{:S(2)}, u32[]{:S(2)}) collective-permute-start(bf16[392,128]{1,0:T(8,128)(2,1)S(1)} %get-tuple-element.74), channel_id=1, source_target_pairs={{0,4},{1,5},{2,6},{3,7},{4,0},{5,1},{6,2},{7,3},{8,12},{9,13},{10,... | collective-permute-start | bytes 301064 | tf_op jit(solution)/shard_map/ppermute | solution.py:308
  40.3 1.4 %collective-permute-start.10 = (bf16[4,24,448]{2,1,0:T(8,128)(2,1)S(1)}, bf16[4,24,448]{2,1,0:T(8,128)(2,1)S(1)}, u32[]{:S(2)}, u32[]{:S(2)}) collective-permute-start(bf16[4,24,448]{2,1,0:T(8,128)(2,1)S(1)} %get-tuple-element.86), channel_id=1, source_target_pairs={{0,1},{1,0},{2,3},{3,2},{4,5},{5,4},{6,7},{7,6},{8,9},{9,8},{10,11... | collective-permute-start | bytes 258056 | tf_op jit(solution)/shard_map/ppermute | solution.py:308
  41.2 2.2 %collective-permute-start.9 = (bf16[4,24,448]{2,1,0:T(8,128)(2,1)S(1)}, bf16[4,24,448]{2,1,0:T(8,128)(2,1)S(1)}, u32[]{:S(2)}, u32[]{:S(2)}) collective-permute-start(bf16[4,24,448]{2,1,0:T(8,128)(2,1)S(1)} %get-tuple-element.84), channel_id=1, source_target_pairs={{0,1},{1,0},{2,3},{3,2},{4,5},{5,4},{6,7},{7,6},{8,9},{9,8},{10,11... | collective-permute-start | bytes 258056 | tf_op jit(solution)/shard_map/ppermute | solution.py:308
  41.8 4.8 %collective-permute-start.11 = (bf16[4,24,448]{2,1,0:T(8,128)(2,1)S(1)}, bf16[4,24,448]{2,1,0:T(8,128)(2,1)S(1)}, u32[]{:S(2)}, u32[]{:S(2)}) collective-permute-start(bf16[4,24,448]{2,1,0:T(8,128)(2,1)S(1)} %shard_map.82), channel_id=1, source_target_pairs={{0,2},{1,3},{2,0},{3,1},{4,6},{5,7},{6,4},{7,5},{8,10},{9,11},{10,... | collective-permute-start | bytes 258056 | tf_op jit(solution)/shard_map/ppermute | solution.py:308
  46.7 5.9 %collective-permute-start.12 = (bf16[24,448]{1,0:T(8,128)(2,1)S(1)}, bf16[24,448]{1,0:T(8,128)(2,1)S(1)}, u32[]{:S(2)}, u32[]{:S(2)}) collective-permute-start(bf16[24,448]{1,0:T(8,128)(2,1)S(1)} %get-tuple-element.88), channel_id=1, source_target_pairs={{0,12},{1,13},{2,14},{3,15},{4,8},{5,9},{6,10},{7,11},{8,4},{9,5},... | collective-permute-start | bytes 64520 | tf_op jit(solution)/shard_map/ppermute | solution.py:308
  49.8 4.8 %collective-permute-start.13 = (bf16[24,448]{1,0:T(8,128)(2,1)S(1)}, bf16[24,448]{1,0:T(8,128)(2,1)S(1)}, u32[]{:S(2)}, u32[]{:S(2)}) collective-permute-start(bf16[24,448]{1,0:T(8,128)(2,1)S(1)} %get-tuple-element.89), channel_id=1, source_target_pairs={{0,8},{1,9},{2,10},{3,11},{4,12},{5,13},{6,14},{7,15},{8,0},{9,1},... | collective-permute-start | bytes 64520 | tf_op jit(solution)/shard_map/ppermute | solution.py:308
  49.8 4.8 %collective-permute-start.14 = (bf16[24,448]{1,0:T(8,128)(2,1)S(1)}, bf16[24,448]{1,0:T(8,128)(2,1)S(1)}, u32[]{:S(2)}, u32[]{:S(2)}) collective-permute-start(bf16[24,448]{1,0:T(8,128)(2,1)S(1)} %get-tuple-element.90), channel_id=1, source_target_pairs={{0,4},{1,5},{2,6},{3,7},{4,0},{5,1},{6,2},{7,3},{8,12},{9,13},{10,... | collective-permute-start | bytes 64520 | tf_op jit(solution)/shard_map/ppermute | solution.py:308

commit v5 on v4

--- a/solution.py
+++ b/solution.py
@@ -196,9 +196,9 @@
         flat_ref[:, head * width : (head + 1) * width] = value.astype(jnp.bfloat16)
 
 
-def share(part, pair, spot, keep_ref, send_ref):
+def share(part, pair, spot, keep_ref, send_ref, cross=0):
     columns = keep_ref.shape[2]
-    first_core = lax.rem(lax.axis_index("ctx"), 2) == 0
+    first_core = lax.rem(lax.axis_index("ctx") + cross, 2) == 0
     halves = []
     for side in range(2):
         shift = (2 * pair + side) * columns
@@ -211,11 +211,13 @@
 def project_kernel(across, flat, proj_ref, keep_ref, send_ref):
     side = lax.rem(lax.div(lax.axis_index("ctx"), 2), 2)
     side = 1 - side if across else side
+    outer = lax.div(lax.axis_index("ctx"), 4)
     span = 2 * keep_ref.shape[2]
     for spot in range(keep_ref.shape[0]):
         at = pl.multiple_of((2 * spot + side) * span, span)
         part = jnp.dot(flat, proj_ref[:, pl.ds(at, span)], preferred_element_type=jnp.float32)
-        share(part, 0, spot, keep_ref, send_ref)
+        elsewhere = jnp.where(outer == spot, 0, 1)
+        share(part, 0, spot, keep_ref, send_ref, elsewhere + across)
 
 
 def leaving_kernel(peers, *refs):
@@ -311,14 +313,15 @@
         return jnp.where(lengths[0] > -1, value, jnp.zeros_like(value))
 
     keys_own = jnp.transpose(cache[0])
-    keys_across = swap(keys_own, 2)
+    keys_across = swap(keys_own, 3)
     keys_core = swap(keys_own, 1)
     keys_far = swap(keys_across, 1)
     sent = {0: queries[0]}
     bit = outer // 2
     while bit:
         for peer in list(sent):
-            sent[peer ^ bit] = swap(sent[peer], inner * bit)
+            cross = 0 if peer else 1
+            sent[peer ^ bit] = swap(sent[peer], inner * bit + cross)
         bit //= 2
     rows = {
         peer: jnp.transpose(value, (1, 0, 2)).reshape(each, width) for peer, value in sent.items()
@@ -352,7 +355,7 @@
     values = call(
         lambda *refs: middle_kernel(outer, *refs),
         state_of(outer),
-        (bias_of(2), *pick(rows, everyone), keys_across, *sum(pick(state, everyone), [])),
+        (bias_of(3), *pick(rows, everyone), keys_across, *sum(pick(state, everyone), [])),
     )
     save(everyone, values)
     lanes = math.gcd(latent, 128)
@@ -363,11 +366,11 @@
         values = call(
             lambda *refs, near=near: last_kernel(outer // 2, near, *refs),
             (own_shape if near else ()) + (packed,) * (len(peers) - near),
-            (bias_of(3), *pick(rows, peers), keys_far, *sum(pick(state, peers), [])),
+            (bias_of(2), *pick(rows, peers), keys_far, *sum(pick(state, peers), [])),
         )
         if near:
             whole, values, peers = values[:3], values[3:], peers[1:]
-        got += [swap(value, inner * peer) for peer, value in zip(peers, values)]
+        got += [swap(value, inner * peer + 1) for peer, value in zip(peers, values)]
     proj_here = on_chip(out_proj)
     *whole, up_here = call(
         draft_kernel,
@@ -380,7 +383,8 @@
     def halves_of(chips):
         return shaped(chips, drafts, columns), shaped(chips, drafts, columns, dtype=bf16)
 
-    if 2 * columns % 128 == 0:
+    cross = int(2 * columns % 128 == 0)
+    if cross:
         flat, keep, send = call(
             lambda *refs: leaving_kernel(outer, *refs), (flat_shape, *halves_of(chips // 2)), inputs
         )
@@ -398,11 +402,11 @@
         quad_kernel,
         (shaped(drafts, columns),)
         + tuple(shaped(drafts, columns, dtype=bf16) for _ in range(outer - 1)),
-        (stay, swap(send, 2)),
+        (stay, swap(send, 2 + cross)),
     )
     result = own
     for peer in range(outer - 1, 0, -1):
-        result = result + swap(parts[peer - 1], inner * peer).astype(jnp.float32)
+        result = result + swap(parts[peer - 1], inner * peer + cross).astype(jnp.float32)
     return result.astype(bf16)
 
 

time: 55.4 us -> 56.1 us (1.013)
  waiting for transfers between devices: 20.3 us -> 21.5 us
    ppermute x15, waiting for transfers between devices: 20.3 us -> 21.5 us  [swap(): return lax.ppermute(value, 'ctx', [(i, i ^ bits) for i in range(count)])]
where the time goes in v5:
time: 56.1 us; the launch traced here: 55.9 us
  waiting for transfers between devices  21.5 us (38%)
  starting transfers between devices  19.8 us (35%)
  Pallas kernels  7.51 us (13%)
  other arithmetic  5.32 us (9%)
  local copies, waits for them, and re-layouts  0.99 us (2%)
  between operations  0.86 us (2%)
    ppermute x15, waiting for transfers between devices, swap(): return lax.ppermute(value, 'ctx', [(i, i ^ bits) for i in range(count)])  21.5 us
    ppermute x15, starting transfers between devices, swap(): return lax.ppermute(value, 'ctx', [(i, i ^ bits) for i in range(count)])  19.8 us
    pallas_call x11, Pallas kernels, call(): pl.pallas_call(kernel, out_shape=outs, in_specs=specs or [pl.BlockSpec()...  7.51 us
    select_n x2, other arithmetic, on_chip(): return jnp.where(lengths[0] > -1, value, jnp.zeros_like(value))  4.66 us
  transfers between devices with their start and end apart: 15, of which 7 were waited for; matrix products, arithmetic and copies ran while one was open for 10% of the time, Pallas kernels for 10%

profile of v5, /device:TPU:0, one launch (start us, length us, event | category | flops | bytes accessed | tf_op | source)
XLA Modules:
  0.0 55.9 jit_solution(4051645412687338772)
XLA Ops:
  0.0 2.4 %collective-permute-start.2 = (bf16[576,512]{1,0:T(8,128)(2,1)}, bf16[576,512]{1,0:T(8,128)(2,1)S(1)}, u32[]{:S(2)}, u32[]{:S(2)}) collective-permute-start(bf16[576,512]{1,0:T(8,128)(2,1)} %bitcast.36), channel_id=1, source_target_pairs={{0,3},{1,2},{2,1},{3,0},{4,7},{5,6},{6,5},{7,4},{8,11},{9,10},{10,... | collective-permute-start | bytes 1769480 | tf_op jit(solution)/shard_map/ppermute | solution.py:310
  2.4 1.9 %collective-permute-start.4 = (bf16[24,4,576]{2,1,0:T(4,128)(2,1)}, bf16[24,4,576]{2,1,0:T(4,128)(2,1)S(1)}, u32[]{:S(2)}, u32[]{:S(2)}) collective-permute-start(bf16[24,4,576]{2,1,0:T(4,128)(2,1)} %bitcast.38), channel_id=1, source_target_pairs={{0,5},{1,4},{2,7},{3,6},{4,1},{5,0},{6,3},{7,2},{8,13},{9,12},{10,... | collective-permute-start | bytes 331784 | tf_op jit(solution)/shard_map/ppermute | solution.py:310
  4.3 2.0 %collective-permute-start = (bf16[24,4,576]{2,1,0:T(4,128)(2,1)}, bf16[24,4,576]{2,1,0:T(4,128)(2,1)S(1)}, u32[]{:S(2)}, u32[]{:S(2)}) collective-permute-start(bf16[24,4,576]{2,1,0:T(4,128)(2,1)} %bitcast.39), channel_id=1, source_target_pairs={{0,9},{1,8},{2,11},{3,10},{4,13},{5,12},{6,15},{7,14},{8,1},{9,0},... | collective-permute-start | bytes 331784 | tf_op jit(solution)/shard_map/ppermute | solution.py:310
  6.3 0.7 %collective-permute-start.5 = (bf16[576,512]{1,0:T(8,128)(2,1)}, bf16[576,512]{1,0:T(8,128)(2,1)S(1)}, u32[]{:S(2)}, u32[]{:S(2)}) collective-permute-start(bf16[576,512]{1,0:T(8,128)(2,1)} %bitcast.37), channel_id=1, source_target_pairs={{0,1},{1,0},{2,3},{3,2},{4,5},{5,4},{6,7},{7,6},{8,9},{9,8},{10,11... | collective-permute-start | bytes 1769480 | tf_op jit(solution)/shard_map/ppermute | solution.py:310
  7.7 0.9 %copy.10 = bf16[4,24,576]{2,1,0:T(8,128)(2,1)S(1)} copy(bf16[4,24,576]{2,0,1:T(4,128)(2,1)} %bitcast.40) | data formatting | bytes 221184 | tf_op jit(solution)/shard_map/transpose | solution.py:327
  8.6 7.9 %collective-permute-done.2.refs_5_ = bf16[576,512]{1,0:T(8,128)(2,1)S(1)} collective-permute-done((bf16[576,512]{1,0:T(8,128)(2,1)}, bf16[576,512]{1,0:T(8,128)(2,1)S(1)}, u32[]{:S(2)}, u32[]{:S(2)}) %collective-permute-start.2) | collective-permute-done | bytes 589856 | tf_op jit(solution)/shard_map/ppermute | solution.py:310
  16.5 0.1 collective-permute-start.3
  16.6 1.1 %broadcast_select_fusion.1.refs_3_ = bf16[576,512]{1,0:T(8,128)(2,1)S(1)} fusion(pred[]{:T(512)S(6)} %gt.4, bf16[1,512,576]{1,2,0:T(8,128)(2,1)} %param.8), kind=kLoop, calls=%fused_computation.1 | loop fusion | flops 294912 | bytes 1179649 | tf_op jit(solution)/shard_map/jit(_where)/select_n | solution.py:313
  17.7 0.0 collective-permute-done
  17.7 2.4 %collective-permute-start.1 = (bf16[24,4,576]{2,1,0:T(4,128)(2,1)S(1)}, bf16[24,4,576]{2,1,0:T(4,128)(2,1)S(1)}, u32[]{:S(2)}, u32[]{:S(2)}) collective-permute-start(bf16[24,4,576]{2,1,0:T(4,128)(2,1)S(1)} %collective-permute-done), channel_id=1, source_target_pairs={{0,4},{1,5},{2,6},{3,7},{4,0},{5,1},{6,2},{7,3},{8,12},{9,13},{10,... | collective-permute-start | bytes 331784 | tf_op jit(solution)/shard_map/ppermute | solution.py:310
  20.1 0.0 collective-permute-done.4
  20.2 3.8 %collective-permute-done.1 = bf16[24,4,576]{2,1,0:T(4,128)(2,1)S(1)} collective-permute-done((bf16[24,4,576]{2,1,0:T(4,128)(2,1)S(1)}, bf16[24,4,576]{2,1,0:T(4,128)(2,1)S(1)}, u32[]{:S(2)}, u32[]{:S(2)}) %collective-permute-start.1) | collective-permute-done | bytes 110624 | tf_op jit(solution)/shard_map/ppermute | solution.py:310
  24.0 0.0 collective-permute-done.5.refs_4_
  24.1 1.0 %shard_map.74 = (f32[96,512]{1,0:T(8,128)S(1)}, f32[96,1]{1,0:T(8,128)S(1)}, f32[96,1]{1,0:T(8,128)S(1)}, f32[96,512]{1,0:T(8,128)S(1)}, f32[96,1]{1,0:T(8,128)S(1)}, /*index=5*/f32[96,1]{1,0:T(8,128)S(1)}) custom-call(f32[1,1024]{1,0:T(1,128)S(1)} %compare_select_fusion.refs_0_, bf16[96,576]{1,0:T(8,128)(2,1)S(1)} %bitcast.26, ...), custom_call_target="tpu_custom_call" | custom-call | tf_op jit(solution)/shard_map/pallas_call | solution.py:275
  25.0 1.0 %shard_map.73 = (f32[96,512]{1,0:T(8,128)S(1)}, f32[96,1]{1,0:T(8,128)S(1)}, f32[96,1]{1,0:T(8,128)S(1)}, f32[96,512]{1,0:T(8,128)S(1)}, f32[96,1]{1,0:T(8,128)S(1)}, /*index=5*/f32[96,1]{1,0:T(8,128)S(1)}) custom-call(f32[1,1024]{1,0:T(1,128)S(1)} %compare_select_fusion.refs_0_, bf16[96,576]{1,0:T(8,128)(2,1)S(1)} %bitcast.22, ...), custom_call_target="tpu_custom_call" | custom-call | tf_op jit(solution)/shard_map/pallas_call | solution.py:275
  26.0 1.1 %shard_map.75 = (f32[96,512]{1,0:T(8,128)S(1)}, f32[96,1]{1,0:T(8,128)S(1)}, f32[96,1]{1,0:T(8,128)S(1)}, f32[96,512]{1,0:T(8,128)S(1)}, f32[96,1]{1,0:T(8,128)S...) custom-call(f32[1,512]{1,0:T(1,128)S(1)} %compare_select_fusion.1.re, ...), custom_call_target="tpu_custom_call" | custom-call | tf_op jit(solution)/shard_map/pallas_call | solution.py:275
  27.1 0.0 collective-permute-done.3.refs_3_
  27.1 0.8 %shard_map.76 = (bf16[392,128]{1,0:T(8,128)(2,1)S(1)}, bf16[392,128]{1,0:T(8,128)(2,1)S(1)}) custom-call(f32[1,512]{1,0:T(1,128)S(1)} %compare_select_fusion.2.refs_0_, bf16[96,576]{1,0:T(8,128)(2,1)S(1)} %bitcast.31, bf16[96,576]{1,0:T(8,128)(2,1)S(1)} %bitcast.34, bf16[576,512]{1,0:T(8,128)(2,1)S(1)} %collective-permute-done.3.refs_3_, ...), custom_call_target="tpu_custom_call" | custom-call | tf_op jit(solution)/shard_map/pallas_call | solution.py:275
  27.9 2.0 %collective-permute-start.6 = (bf16[392,128]{1,0:T(8,128)(2,1)S(1)}, bf16[392,128]{1,0:T(8,128)(2,1)S(1)}, u32[]{:S(2)}, u32[]{:S(2)}) collective-permute-start(bf16[392,128]{1,0:T(8,128)(2,1)S(1)} %get-tuple-element.66), channel_id=1, source_target_pairs={{0,9},{1,8},{2,11},{3,10},{4,13},{5,12},{6,15},{7,14},{8,1},{9,0},... | collective-permute-start | bytes 301064 | tf_op jit(solution)/shard_map/ppermute | solution.py:310
  29.9 1.9 %collective-permute-start.7 = (bf16[392,128]{1,0:T(8,128)(2,1)S(1)}, bf16[392,128]{1,0:T(8,128)(2,1)S(1)}, u32[]{:S(2)}, u32[]{:S(2)}) collective-permute-start(bf16[392,128]{1,0:T(8,128)(2,1)S(1)} %get-tuple-element.67), channel_id=1, source_target_pairs={{0,13},{1,12},{2,15},{3,14},{4,9},{5,8},{6,11},{7,10},{8,5},{9,4},... | collective-permute-start | bytes 301064 | tf_op jit(solution)/shard_map/ppermute | solution.py:310
  31.8 0.8 %shard_map.77 = (f32[96,512]{1,0:T(8,128)S(1)}, f32[96,1]{1,0:T(8,128)S(1)}, f32[96,1]{1,0:T(8,128)S(1)}, bf16[392,128]{1,0:T(8,128)(2,1)S(1)}) custom-call(f32[1,512]{1,0:T(1,128)S(1)} %compare_select_fusion.2.refs_0_, bf16[96,576]{1,0:T(8,128)(2,1)S(1)} %bitcast.24, bf16[96,576]{1,0:T(8,128)(2,1)S(1)} %bitcast.28, ...), custom_call_target="tpu_custom_call" | custom-call | tf_op jit(solution)/shard_map/pallas_call | solution.py:275
  32.5 0.0 copy-start
  32.5 0.0 copy-start.1
  32.6 0.0 copy-start.2
  32.6 0.3 collective-permute-start.8
  32.9 3.6 %broadcast_select_fusion.refs_7_.proj_ref = bf16[512,7168]{1,0:T(8,128)(2,1)S(1)} fusion(bf16[512,7168]{1,0:T(8,128)(2,1)} %param.13, pred[]{:T(512)S(6)} %gt.4), kind=kLoop, calls=%fused_computation | loop fusion | flops 3670016 | bytes 14680065 | tf_op jit(solution)/shard_map/jit(_where)/select_n | solution.py:313
  36.4 0.0 copy-done
  36.5 0.0 copy-done.1
  36.5 0.0 copy-done.2
  36.5 1.0 %shard_map.78 = (f32[96,512]{1,0:T(8,128)S(1)}, f32[96,1]{1,0:T(8,128)S(1)}, f32[96,1]{1,0:T(8,128)S(1)}, bf16[4,512,128]{2,1,0:T(8,128)(2,1)S(1)}) custom-call(bf16[96,576]{1,0:T(8,128)(2,1)S(1)} %bitcast.25, bf16[24,576]{1,0:T(8,128)(2,1)S(1)} %bitcast.35, s32[1,24]{1,0:T(1,128)S(1)} %copy-done.2, bf16[4,512,128]{2,1,0:T(8,128)(2,1)S(1)} %copy-done, ...), custom_call_target="tpu_custom_call" | custom-call | tf_op jit(solution)/shard_map/pallas_call | solution.py:275
  37.4 0.5 collective-permute-done.6.refs_0_
  38.0 0.0 collective-permute-done.7.refs_1_
  38.0 2.4 %collective-permute-done.8.refs_2_ = bf16[392,128]{1,0:T(8,128)(2,1)S(1)} collective-permute-done((bf16[392,128]{1,0:T(8,128)(2,1)S(1)}, bf16[392,128]{1,0:T(8,128)(2,1)S(1)}, u32[]{:S(2)}, u32[]{:S(2)}) %collective-permute-start.8) | collective-permute-done | bytes 100384 | tf_op jit(solution)/shard_map/ppermute | solution.py:310
  40.4 1.1 %shard_map.79 = (bf16[24,512]{1,0:T(8,128)(2,1)S(1)}, f32[4,24,448]{2,1,0:T(8,128)S(1)}, bf16[4,24,448]{2,1,0:T(8,128)(2,1)S(1)}) custom-call(bf16[392,128]{1,0:T(8,128)(2,1)S(1)} %collective-permute-done.6.refs_0_, bf16[392,128]{1,0:T(8,128)(2,1)S(1)} %collective-permute-done.7.refs_1_, bf16[392,128]{1,0:T(8,128)(2,1)S(1)} %collective-permute-done.8.refs_2_, ...), custom_call_target="tpu_custom_call" | custom-call | tf_op jit(solution)/shard_map/pallas_call | solution.py:275
  41.6 0.2 collective-permute-start.10
  41.7 0.8 %shard_map.80 = (f32[4,24,448]{2,1,0:T(8,128)S(1)}, bf16[4,24,448]{2,1,0:T(8,128)(2,1)S(1)}) custom-call(bf16[24,512]{1,0:T(8,128)(2,1)S(1)} %get-tuple-element.82.flat_ref, bf16[512,7168]{1,0:T(8,128)(2,1)S(1)} %broadcast_select_fusion.refs_7_.proj_ref), custom_call_target="tpu_custom_call" | custom-call | tf_op jit(solution)/shard_map/pallas_call | solution.py:275
  42.5 0.5 collective-permute-start.9
  43.0 0.0 collective-permute-done.10.got_ref
  43.0 1.5 %collective-permute-start.11 = (bf16[4,24,448]{2,1,0:T(8,128)(2,1)S(1)}, bf16[4,24,448]{2,1,0:T(8,128)(2,1)S(1)}, u32[]{:S(2)}, u32[]{:S(2)}) collective-permute-start(bf16[4,24,448]{2,1,0:T(8,128)(2,1)S(1)} %shard_map.82), channel_id=1, source_target_pairs={{0,3},{1,2},{2,1},{3,0},{4,7},{5,6},{6,5},{7,4},{8,11},{9,10},{10,... | collective-permute-start | bytes 258056 | tf_op jit(solution)/shard_map/ppermute | solution.py:310
  44.6 0.0 collective-permute-done.9.got_ref
  44.6 3.3 %collective-permute-done.11.got_ref = bf16[4,24,448]{2,1,0:T(8,128)(2,1)S(1)} collective-permute-done((bf16[4,24,448]{2,1,0:T(8,128)(2,1)S(1)}, bf16[4,24,448]{2,1,0:T(8,128)(2,1)S(1)}, u32[]{:S(2)}, u32[]{:S(2)}) %collective-permute-start.11) | collective-permute-done | bytes 86048 | tf_op jit(solution)/shard_map/ppermute | solution.py:310
  47.9 3.2 %collective-permute-start.12 = (bf16[24,448]{1,0:T(8,128)(2,1)S(1)}, bf16[24,448]{1,0:T(8,128)(2,1)S(1)}, u32[]{:S(2)}, u32[]{:S(2)}) collective-permute-start(bf16[24,448]{1,0:T(8,128)(2,1)S(1)} %get-tuple-element.88), channel_id=1, source_target_pairs={{0,13},{1,12},{2,15},{3,14},{4,9},{5,8},{6,11},{7,10},{8,5},{9,4},... | collective-permute-start | bytes 64520 | tf_op jit(solution)/shard_map/ppermute | solution.py:310
  51.1 0.0 collective-permute-start.13
  51.1 0.7 %collective-permute-start.14 = (bf16[24,448]{1,0:T(8,128)(2,1)S(1)}, bf16[24,448]{1,0:T(8,128)(2,1)S(1)}, u32[]{:S(2)}, u32[]{:S(2)}) collective-permute-start(bf16[24,448]{1,0:T(8,128)(2,1)S(1)} %get-tuple-element.90), channel_id=1, source_target_pairs={{0,5},{1,4},{2,7},{3,6},{4,1},{5,0},{6,3},{7,2},{8,13},{9,12},{10,... | collective-permute-start | bytes 64520 | tf_op jit(solution)/shard_map/ppermute | solution.py:310
  51.8 1.2 %collective-permute-done.12 = bf16[24,448]{1,0:T(8,128)(2,1)S(1)} collective-permute-done((bf16[24,448]{1,0:T(8,128)(2,1)S(1)}, bf16[24,448]{1,0:T(8,128)(2,1)S(1)}, u32[]{:S(2)}, u32[]{:S(2)}) %collective-permute-start.12) | collective-permute-done | bytes 21536 | tf_op jit(solution)/shard_map/ppermute | solution.py:310
  53.0 2.2 %collective-permute-done.13 = bf16[24,448]{1,0:T(8,128)(2,1)S(1)} collective-permute-done((bf16[24,448]{1,0:T(8,128)(2,1)S(1)}, bf16[24,448]{1,0:T(8,128)(2,1)S(1)}, u32[]{:S(2)}, u32[]{:S(2)}) %collective-permute-start.13) | collective-permute-done | bytes 21536 | tf_op jit(solution)/shard_map/ppermute | solution.py:310
  55.3 0.0 collective-permute-done.14
  55.3 0.6 %add_convert_fusion = bf16[24,448]{1,0:T(8,128)(2,1)} fusion(bf16[24,448]{1,0:T(8,128)(2,1)S(1)} %collective-permute-done.14, bf16[24,448]{1,0:T(8,128)(2,1)S(1)} %collective-permute-done.13, f32[24,448]{1,0:T(8,128)S(1)} %get-tuple-element.87, bf16[24,448]{1,0:T(8,128)(2,1)S(1)} %collective-permute-done.12), kind=kLoop, calls=%fused_computation.2 | loop fusion | flops 75264 | bytes 129024 | tf_op jit(solution)/shard_map/convert_element_type | solution.py:410
  (11 shorter events, 0.1 us)
Async XLA Ops:
  0.0 16.5 %collective-permute-start.2 = (bf16[576,512]{1,0:T(8,128)(2,1)}, bf16[576,512]{1,0:T(8,128)(2,1)S(1)}, u32[]{:S(2)}, u32[]{:S(2)}) collective-permute-start(bf16[576,512]{1,0:T(8,128)(2,1)} %bitcast.36), channel_id=1, source_target_pairs={{0,3},{1,2},{2,1},{3,0},{4,7},{5,6},{6,5},{7,4},{8,11},{9,10},{10,... | collective-permute-start | bytes 1769480 | tf_op jit(solution)/shard_map/ppermute | solution.py:310
  2.4 17.7 %collective-permute-start.4 = (bf16[24,4,576]{2,1,0:T(4,128)(2,1)}, bf16[24,4,576]{2,1,0:T(4,128)(2,1)S(1)}, u32[]{:S(2)}, u32[]{:S(2)}) collective-permute-start(bf16[24,4,576]{2,1,0:T(4,128)(2,1)} %bitcast.38), channel_id=1, source_target_pairs={{0,5},{1,4},{2,7},{3,6},{4,1},{5,0},{6,3},{7,2},{8,13},{9,12},{10,... | collective-permute-start | bytes 331784 | tf_op jit(solution)/shard_map/ppermute | solution.py:310
  4.3 13.4 %collective-permute-start = (bf16[24,4,576]{2,1,0:T(4,128)(2,1)}, bf16[24,4,576]{2,1,0:T(4,128)(2,1)S(1)}, u32[]{:S(2)}, u32[]{:S(2)}) collective-permute-start(bf16[24,4,576]{2,1,0:T(4,128)(2,1)} %bitcast.39), channel_id=1, source_target_pairs={{0,9},{1,8},{2,11},{3,10},{4,13},{5,12},{6,15},{7,14},{8,1},{9,0},... | collective-permute-start | bytes 331784 | tf_op jit(solution)/shard_map/ppermute | solution.py:310
  6.3 17.7 %collective-permute-start.5 = (bf16[576,512]{1,0:T(8,128)(2,1)}, bf16[576,512]{1,0:T(8,128)(2,1)S(1)}, u32[]{:S(2)}, u32[]{:S(2)}) collective-permute-start(bf16[576,512]{1,0:T(8,128)(2,1)} %bitcast.37), channel_id=1, source_target_pairs={{0,1},{1,0},{2,3},{3,2},{4,5},{5,4},{6,7},{7,6},{8,9},{9,8},{10,11... | collective-permute-start | bytes 1769480 | tf_op jit(solution)/shard_map/ppermute | solution.py:310
  16.5 10.7 %collective-permute-start.3 = (bf16[576,512]{1,0:T(8,128)(2,1)S(1)}, bf16[576,512]{1,0:T(8,128)(2,1)S(1)}, u32[]{:S(2)}, u32[]{:S(2)}) collective-permute-start(bf16[576,512]{1,0:T(8,128)(2,1)S(1)} %collective-permute-done.2.refs_5_), channel_id=1, source_target_pairs={{0,1},{1,0},{2,3},{3,2},{4,5},{5,4},{6,7},{7,6},{8,9},{9,8},{10,11... | collective-permute-start | bytes 1769480 | tf_op jit(solution)/shard_map/ppermute | solution.py:310
  17.7 6.3 %collective-permute-start.1 = (bf16[24,4,576]{2,1,0:T(4,128)(2,1)S(1)}, bf16[24,4,576]{2,1,0:T(4,128)(2,1)S(1)}, u32[]{:S(2)}, u32[]{:S(2)}) collective-permute-start(bf16[24,4,576]{2,1,0:T(4,128)(2,1)S(1)} %collective-permute-done), channel_id=1, source_target_pairs={{0,4},{1,5},{2,6},{3,7},{4,0},{5,1},{6,2},{7,3},{8,12},{9,13},{10,... | collective-permute-start | bytes 331784 | tf_op jit(solution)/shard_map/ppermute | solution.py:310
  27.9 10.1 %collective-permute-start.6 = (bf16[392,128]{1,0:T(8,128)(2,1)S(1)}, bf16[392,128]{1,0:T(8,128)(2,1)S(1)}, u32[]{:S(2)}, u32[]{:S(2)}) collective-permute-start(bf16[392,128]{1,0:T(8,128)(2,1)S(1)} %get-tuple-element.66), channel_id=1, source_target_pairs={{0,9},{1,8},{2,11},{3,10},{4,13},{5,12},{6,15},{7,14},{8,1},{9,0},... | collective-permute-start | bytes 301064 | tf_op jit(solution)/shard_map/ppermute | solution.py:310
  29.9 8.1 %collective-permute-start.7 = (bf16[392,128]{1,0:T(8,128)(2,1)S(1)}, bf16[392,128]{1,0:T(8,128)(2,1)S(1)}, u32[]{:S(2)}, u32[]{:S(2)}) collective-permute-start(bf16[392,128]{1,0:T(8,128)(2,1)S(1)} %get-tuple-element.67), channel_id=1, source_target_pairs={{0,13},{1,12},{2,15},{3,14},{4,9},{5,8},{6,11},{7,10},{8,5},{9,4},... | collective-permute-start | bytes 301064 | tf_op jit(solution)/shard_map/ppermute | solution.py:310
  32.5 3.9 %copy-start = (bf16[4,512,128]{2,1,0:T(8,128)(2,1)S(1)}, bf16[4,512,128]{2,1,0:T(8,128)(2,1)}, u32[]{:S(2)}) copy-start(bf16[4,512,128]{2,1,0:T(8,128)(2,1)} %up_from.1) | copy-start | bytes 1572868
  32.5 3.9 %copy-start.1 = (bf16[1,24,576]{2,1,0:T(8,128)(2,1)S(1)}, bf16[1,24,576]{2,1,0:T(8,128)(2,1)}, u32[]{:S(2)}) copy-start(bf16[1,24,576]{2,1,0:T(8,128)(2,1)} %param.9) | copy-start | bytes 82948
  32.6 3.9 %copy-start.2 = (s32[1,24]{1,0:T(1,128)S(1)}, s32[1,24]{1,0:T(1,128)}, u32[]{:S(2)}) copy-start(s32[1,24]{1,0:T(1,128)} %parents_ref.1) | copy-start | bytes 292
  32.6 7.8 %collective-permute-start.8 = (bf16[392,128]{1,0:T(8,128)(2,1)S(1)}, bf16[392,128]{1,0:T(8,128)(2,1)S(1)}, u32[]{:S(2)}, u32[]{:S(2)}) collective-permute-start(bf16[392,128]{1,0:T(8,128)(2,1)S(1)} %get-tuple-element.74), channel_id=1, source_target_pairs={{0,5},{1,4},{2,7},{3,6},{4,1},{5,0},{6,3},{7,2},{8,13},{9,12},{10,... | collective-permute-start | bytes 301064 | tf_op jit(solution)/shard_map/ppermute | solution.py:310
  41.6 1.4 %collective-permute-start.10 = (bf16[4,24,448]{2,1,0:T(8,128)(2,1)S(1)}, bf16[4,24,448]{2,1,0:T(8,128)(2,1)S(1)}, u32[]{:S(2)}, u32[]{:S(2)}) collective-permute-start(bf16[4,24,448]{2,1,0:T(8,128)(2,1)S(1)} %get-tuple-element.86), channel_id=1, source_target_pairs={{0,1},{1,0},{2,3},{3,2},{4,5},{5,4},{6,7},{7,6},{8,9},{9,8},{10,11... | collective-permute-start | bytes 258056 | tf_op jit(solution)/shard_map/ppermute | solution.py:310
  42.5 2.0 %collective-permute-start.9 = (bf16[4,24,448]{2,1,0:T(8,128)(2,1)S(1)}, bf16[4,24,448]{2,1,0:T(8,128)(2,1)S(1)}, u32[]{:S(2)}, u32[]{:S(2)}) collective-permute-start(bf16[4,24,448]{2,1,0:T(8,128)(2,1)S(1)} %get-tuple-element.84), channel_id=1, source_target_pairs={{0,1},{1,0},{2,3},{3,2},{4,5},{5,4},{6,7},{7,6},{8,9},{9,8},{10,11... | collective-permute-start | bytes 258056 | tf_op jit(solution)/shard_map/ppermute | solution.py:310
  43.0 4.9 %collective-permute-start.11 = (bf16[4,24,448]{2,1,0:T(8,128)(2,1)S(1)}, bf16[4,24,448]{2,1,0:T(8,128)(2,1)S(1)}, u32[]{:S(2)}, u32[]{:S(2)}) collective-permute-start(bf16[4,24,448]{2,1,0:T(8,128)(2,1)S(1)} %shard_map.82), channel_id=1, source_target_pairs={{0,3},{1,2},{2,1},{3,0},{4,7},{5,6},{6,5},{7,4},{8,11},{9,10},{10,... | collective-permute-start | bytes 258056 | tf_op jit(solution)/shard_map/ppermute | solution.py:310
  47.9 5.1 %collective-permute-start.12 = (bf16[24,448]{1,0:T(8,128)(2,1)S(1)}, bf16[24,448]{1,0:T(8,128)(2,1)S(1)}, u32[]{:S(2)}, u32[]{:S(2)}) collective-permute-start(bf16[24,448]{1,0:T(8,128)(2,1)S(1)} %get-tuple-element.88), channel_id=1, source_target_pairs={{0,13},{1,12},{2,15},{3,14},{4,9},{5,8},{6,11},{7,10},{8,5},{9,4},... | collective-permute-start | bytes 64520 | tf_op jit(solution)/shard_map/ppermute | solution.py:310
  51.1 4.2 %collective-permute-start.13 = (bf16[24,448]{1,0:T(8,128)(2,1)S(1)}, bf16[24,448]{1,0:T(8,128)(2,1)S(1)}, u32[]{:S(2)}, u32[]{:S(2)}) collective-permute-start(bf16[24,448]{1,0:T(8,128)(2,1)S(1)} %get-tuple-element.89), channel_id=1, source_target_pairs={{0,9},{1,8},{2,11},{3,10},{4,13},{5,12},{6,15},{7,14},{8,1},{9,0},... | collective-permute-start | bytes 64520 | tf_op jit(solution)/shard_map/ppermute | solution.py:310
  51.1 4.2 %collective-permute-start.14 = (bf16[24,448]{1,0:T(8,128)(2,1)S(1)}, bf16[24,448]{1,0:T(8,128)(2,1)S(1)}, u32[]{:S(2)}, u32[]{:S(2)}) collective-permute-start(bf16[24,448]{1,0:T(8,128)(2,1)S(1)} %get-tuple-element.90), channel_id=1, source_target_pairs={{0,5},{1,4},{2,7},{3,6},{4,1},{5,0},{6,3},{7,2},{8,13},{9,12},{10,... | collective-permute-start | bytes 64520 | tf_op jit(solution)/shard_map/ppermute | solution.py:310

commit v6 on v5

--- a/solution.py
+++ b/solution.py
@@ -317,12 +317,8 @@
     keys_core = swap(keys_own, 1)
     keys_far = swap(keys_across, 1)
     sent = {0: queries[0]}
-    bit = outer // 2
-    while bit:
-        for peer in list(sent):
-            cross = 0 if peer else 1
-            sent[peer ^ bit] = swap(sent[peer], inner * bit + cross)
-        bit //= 2
+    for peer in range(1, outer):
+        sent[peer] = swap(queries[0], inner * peer + 1)
     rows = {
         peer: jnp.transpose(value, (1, 0, 2)).reshape(each, width) for peer, value in sent.items()
     }
@@ -344,11 +340,12 @@
         for spot, peer in enumerate(peers):
             state[peer] = list(values[3 * spot : 3 * spot + 3])
 
+    early = everyone[:2] + everyone[3:]
     for part in range(2):
-        peers = everyone[part::2]
+        peers = [peer for peer in everyone if (peer in early) == (part == 0)]
         values = call(
-            lambda *refs: first_kernel(outer // 2, *refs),
-            state_of(outer // 2),
+            lambda *refs, size=len(peers): first_kernel(size, *refs),
+            state_of(len(peers)),
             (bias_of(0, 1), *pick(rows, peers), keys_here, keys_core),
         )
         save(peers, values)

time: 56.1 us -> 50.7 us (0.904)
  waiting for transfers between devices: 21.5 us -> 17.9 us
  starting transfers between devices: 19.8 us -> 17.9 us
    ppermute x15, waiting for transfers between devices: 21.5 us -> 17.9 us  [swap(): return lax.ppermute(value, 'ctx', [(i, i ^ bits) for i in range(count)])]
    ppermute x15, starting transfers between devices: 19.8 us -> 17.9 us  [swap(): return lax.ppermute(value, 'ctx', [(i, i ^ bits) for i in range(count)])]
  transfers between devices with their start and end apart: 15 -> 15, of which waited for: 7 -> 7; matrix products, arithmetic and copies ran while one was open for 10% -> 11% of each run, Pallas kernels for 10% -> 11%
where the time goes in v6:
time: 50.7 us; the launch traced here: 50.5 us
  starting transfers between devices  17.9 us (35%)
  waiting for transfers between devices  17.9 us (35%)
  Pallas kernels  7.53 us (15%)
  other arithmetic  5.32 us (10%)
  local copies, waits for them, and re-layouts  0.99 us (2%)
  between operations  0.87 us (2%)
    ppermute x15, waiting for transfers between devices, swap(): return lax.ppermute(value, 'ctx', [(i, i ^ bits) for i in range(count)])  17.9 us
    ppermute x15, starting transfers between devices, swap(): return lax.ppermute(value, 'ctx', [(i, i ^ bits) for i in range(count)])  17.9 us
    pallas_call x11, Pallas kernels, call(): pl.pallas_call(kernel, out_shape=outs, in_specs=specs or [pl.BlockSpec()...  7.53 us
    select_n x2, other arithmetic, on_chip(): return jnp.where(lengths[0] > -1, value, jnp.zeros_like(value))  4.67 us
  transfers between devices with their start and end apart: 15, of which 7 were waited for; matrix products, arithmetic and copies ran while one was open for 11% of the time, Pallas kernels for 11%

profile of v6, /device:TPU:0, one launch (start us, length us, event | category | flops | bytes accessed | tf_op | source)
XLA Modules:
  0.0 50.5 jit_solution(11523052380409571854)
XLA Ops:
  0.0 2.4 %collective-permute-start.2 = (bf16[576,512]{1,0:T(8,128)(2,1)}, bf16[576,512]{1,0:T(8,128)(2,1)S(1)}, u32[]{:S(2)}, u32[]{:S(2)}) collective-permute-start(bf16[576,512]{1,0:T(8,128)(2,1)} %bitcast.36), channel_id=1, source_target_pairs={{0,3},{1,2},{2,1},{3,0},{4,7},{5,6},{6,5},{7,4},{8,11},{9,10},{10,... | collective-permute-start | bytes 1769480 | tf_op jit(solution)/shard_map/ppermute | solution.py:310
  2.4 1.9 %collective-permute-start.4 = (bf16[24,4,576]{2,1,0:T(4,128)(2,1)}, bf16[24,4,576]{2,1,0:T(4,128)(2,1)S(1)}, u32[]{:S(2)}, u32[]{:S(2)}) collective-permute-start(bf16[24,4,576]{2,1,0:T(4,128)(2,1)} %bitcast.38), channel_id=1, source_target_pairs={{0,5},{1,4},{2,7},{3,6},{4,1},{5,0},{6,3},{7,2},{8,13},{9,12},{10,... | collective-permute-start | bytes 331784 | tf_op jit(solution)/shard_map/ppermute | solution.py:310
  4.3 2.0 %collective-permute-start.1 = (bf16[24,4,576]{2,1,0:T(4,128)(2,1)}, bf16[24,4,576]{2,1,0:T(4,128)(2,1)S(1)}, u32[]{:S(2)}, u32[]{:S(2)}) collective-permute-start(bf16[24,4,576]{2,1,0:T(4,128)(2,1)} %bitcast.39), channel_id=1, source_target_pairs={{0,13},{1,12},{2,15},{3,14},{4,9},{5,8},{6,11},{7,10},{8,5},{9,4},... | collective-permute-start | bytes 331784 | tf_op jit(solution)/shard_map/ppermute | solution.py:310
  6.3 0.0 collective-permute-start
  6.3 0.7 %collective-permute-start.5 = (bf16[576,512]{1,0:T(8,128)(2,1)}, bf16[576,512]{1,0:T(8,128)(2,1)S(1)}, u32[]{:S(2)}, u32[]{:S(2)}) collective-permute-start(bf16[576,512]{1,0:T(8,128)(2,1)} %bitcast.37), channel_id=1, source_target_pairs={{0,1},{1,0},{2,3},{3,2},{4,5},{5,4},{6,7},{7,6},{8,9},{9,8},{10,11... | collective-permute-start | bytes 1769480 | tf_op jit(solution)/shard_map/ppermute | solution.py:310
  7.7 0.9 %copy.10 = bf16[4,24,576]{2,1,0:T(8,128)(2,1)S(1)} copy(bf16[4,24,576]{2,0,1:T(4,128)(2,1)} %bitcast.41) | data formatting | bytes 221184 | tf_op jit(solution)/shard_map/transpose | solution.py:323
  8.6 7.9 %collective-permute-done.2.refs_5_ = bf16[576,512]{1,0:T(8,128)(2,1)S(1)} collective-permute-done((bf16[576,512]{1,0:T(8,128)(2,1)}, bf16[576,512]{1,0:T(8,128)(2,1)S(1)}, u32[]{:S(2)}, u32[]{:S(2)}) %collective-permute-start.2) | collective-permute-done | bytes 589856 | tf_op jit(solution)/shard_map/ppermute | solution.py:310
  16.5 0.2 collective-permute-start.3
  16.7 1.1 %broadcast_select_fusion.1.refs_4_.refs_2_ = bf16[576,512]{1,0:T(8,128)(2,1)S(1)} fusion(pred[]{:T(512)S(6)} %gt.4, bf16[1,512,576]{1,2,0:T(8,128)(2,1)} %param.8), kind=kLoop, calls=%fused_computation.1 | loop fusion | flops 294912 | bytes 1179649 | tf_op jit(solution)/shard_map/jit(_where)/select_n | solution.py:313
  17.8 0.0 collective-permute-done.4
  17.8 0.0 collective-permute-done.1
  17.9 0.1 collective-permute-done
  18.0 0.0 collective-permute-done.5.refs_5_.refs_3_
  18.0 0.8 %shard_map.74 = (f32[96,512]{1,0:T(8,128)S(1)}, f32[96,1]{1,0:T(8,128)S(1)}, f32[96,1]{1,0:T(8,128)S(1)}) custom-call(f32[1,1024]{1,0:T(1,128)S(1)} %compare_select_fusion.refs_0_, bf16[96,576]{1,0:T(8,128)(2,1)S(1)} %bitcast.32, bf16[576,512]{1,0:T(8,128)(2,1)S(1)} %broadcast_select_fusion.1.refs_4_.refs_2_, ...), custom_call_target="tpu_custom_call" | custom-call | tf_op jit(solution)/shard_map/pallas_call | solution.py:275
  18.8 1.2 %shard_map.73 = (f32[96,512]{1,0:T(8,128)S(1)}, f32[96,1]{1,0:T(8,128)S(1)}, f32[96,1]{1,0:T(8,128)S(1)}, f32[96,512]{1,0:T(8,128)S(1)}, f32[96,1]{1,0:T(8,128)S...) custom-call(f32[1,1024]{1,0:T(1,128)S(1)} %compare_select_fusion.refs_0_, ...), custom_call_target="tpu_custom_call" | custom-call | tf_op jit(solution)/shard_map/pallas_call | solution.py:275
  20.0 1.1 %shard_map.75 = (f32[96,512]{1,0:T(8,128)S(1)}, f32[96,1]{1,0:T(8,128)S(1)}, f32[96,1]{1,0:T(8,128)S(1)}, f32[96,512]{1,0:T(8,128)S(1)}, f32[96,1]{1,0:T(8,128)S...) custom-call(f32[1,512]{1,0:T(1,128)S(1)} %compare_select_fusion.1.re, ...), custom_call_target="tpu_custom_call" | custom-call | tf_op jit(solution)/shard_map/pallas_call | solution.py:275
  21.1 0.0 collective-permute-done.3.refs_3_
  21.1 0.8 %shard_map.76 = (bf16[392,128]{1,0:T(8,128)(2,1)S(1)}, bf16[392,128]{1,0:T(8,128)(2,1)S(1)}) custom-call(f32[1,512]{1,0:T(1,128)S(1)} %compare_select_fusion.2.refs_0_, bf16[96,576]{1,0:T(8,128)(2,1)S(1)} %bitcast.34, bf16[96,576]{1,0:T(8,128)(2,1)S(1)} %bitcast.31, bf16[576,512]{1,0:T(8,128)(2,1)S(1)} %collective-permute-done.3.refs_3_, ...), custom_call_target="tpu_custom_call" | custom-call | tf_op jit(solution)/shard_map/pallas_call | solution.py:275
  21.8 3.3 %collective-permute-start.6 = (bf16[392,128]{1,0:T(8,128)(2,1)S(1)}, bf16[392,128]{1,0:T(8,128)(2,1)S(1)}, u32[]{:S(2)}, u32[]{:S(2)}) collective-permute-start(bf16[392,128]{1,0:T(8,128)(2,1)S(1)} %get-tuple-element.66), channel_id=1, source_target_pairs={{0,9},{1,8},{2,11},{3,10},{4,13},{5,12},{6,15},{7,14},{8,1},{9,0},... | collective-permute-start | bytes 301064 | tf_op jit(solution)/shard_map/ppermute | solution.py:310
  25.1 1.1 %collective-permute-start.7 = (bf16[392,128]{1,0:T(8,128)(2,1)S(1)}, bf16[392,128]{1,0:T(8,128)(2,1)S(1)}, u32[]{:S(2)}, u32[]{:S(2)}) collective-permute-start(bf16[392,128]{1,0:T(8,128)(2,1)S(1)} %get-tuple-element.67), channel_id=1, source_target_pairs={{0,13},{1,12},{2,15},{3,14},{4,9},{5,8},{6,11},{7,10},{8,5},{9,4},... | collective-permute-start | bytes 301064 | tf_op jit(solution)/shard_map/ppermute | solution.py:310
  26.2 0.8 %shard_map.77 = (f32[96,512]{1,0:T(8,128)S(1)}, f32[96,1]{1,0:T(8,128)S(1)}, f32[96,1]{1,0:T(8,128)S(1)}, bf16[392,128]{1,0:T(8,128)(2,1)S(1)}) custom-call(f32[1,512]{1,0:T(1,128)S(1)} %compare_select_fusion.2.refs_0_, bf16[96,576]{1,0:T(8,128)(2,1)S(1)} %bitcast.24, bf16[96,576]{1,0:T(8,128)(2,1)S(1)} %bitcast.28, ...), custom_call_target="tpu_custom_call" | custom-call | tf_op jit(solution)/shard_map/pallas_call | solution.py:275
  27.0 0.0 copy-start
  27.0 0.0 copy-start.1
  27.0 0.0 copy-start.2
  27.0 0.4 collective-permute-start.8
  27.4 3.6 %broadcast_select_fusion.refs_7_.proj_ref = bf16[512,7168]{1,0:T(8,128)(2,1)S(1)} fusion(bf16[512,7168]{1,0:T(8,128)(2,1)} %param.13, pred[]{:T(512)S(6)} %gt.4), kind=kLoop, calls=%fused_computation | loop fusion | flops 3670016 | bytes 14680065 | tf_op jit(solution)/shard_map/jit(_where)/select_n | solution.py:313
  30.9 0.0 copy-done
  31.0 0.0 copy-done.1
  31.0 0.0 copy-done.2
  31.0 1.0 %shard_map.78 = (f32[96,512]{1,0:T(8,128)S(1)}, f32[96,1]{1,0:T(8,128)S(1)}, f32[96,1]{1,0:T(8,128)S(1)}, bf16[4,512,128]{2,1,0:T(8,128)(2,1)S(1)}) custom-call(bf16[96,576]{1,0:T(8,128)(2,1)S(1)} %bitcast.25, bf16[24,576]{1,0:T(8,128)(2,1)S(1)} %bitcast.35, s32[1,24]{1,0:T(1,128)S(1)} %copy-done.2, bf16[4,512,128]{2,1,0:T(8,128)(2,1)S(1)} %copy-done, ...), custom_call_target="tpu_custom_call" | custom-call | tf_op jit(solution)/shard_map/pallas_call | solution.py:275
  31.9 0.7 %collective-permute-done.6.refs_0_ = bf16[392,128]{1,0:T(8,128)(2,1)S(1)} collective-permute-done((bf16[392,128]{1,0:T(8,128)(2,1)S(1)}, bf16[392,128]{1,0:T(8,128)(2,1)S(1)}, u32[]{:S(2)}, u32[]{:S(2)}) %collective-permute-start.6) | collective-permute-done | bytes 100384 | tf_op jit(solution)/shard_map/ppermute | solution.py:310
  32.7 0.0 collective-permute-done.7.refs_1_
  32.7 2.3 %collective-permute-done.8.refs_2_ = bf16[392,128]{1,0:T(8,128)(2,1)S(1)} collective-permute-done((bf16[392,128]{1,0:T(8,128)(2,1)S(1)}, bf16[392,128]{1,0:T(8,128)(2,1)S(1)}, u32[]{:S(2)}, u32[]{:S(2)}) %collective-permute-start.8) | collective-permute-done | bytes 100384 | tf_op jit(solution)/shard_map/ppermute | solution.py:310
  34.9 1.1 %shard_map.79 = (bf16[24,512]{1,0:T(8,128)(2,1)S(1)}, f32[4,24,448]{2,1,0:T(8,128)S(1)}, bf16[4,24,448]{2,1,0:T(8,128)(2,1)S(1)}) custom-call(bf16[392,128]{1,0:T(8,128)(2,1)S(1)} %collective-permute-done.6.refs_0_, bf16[392,128]{1,0:T(8,128)(2,1)S(1)} %collective-permute-done.7.refs_1_, bf16[392,128]{1,0:T(8,128)(2,1)S(1)} %collective-permute-done.8.refs_2_, ...), custom_call_target="tpu_custom_call" | custom-call | tf_op jit(solution)/shard_map/pallas_call | solution.py:275
  36.1 0.2 collective-permute-start.10
  36.3 0.8 %shard_map.80 = (f32[4,24,448]{2,1,0:T(8,128)S(1)}, bf16[4,24,448]{2,1,0:T(8,128)(2,1)S(1)}) custom-call(bf16[24,512]{1,0:T(8,128)(2,1)S(1)} %get-tuple-element.82.flat_ref, bf16[512,7168]{1,0:T(8,128)(2,1)S(1)} %broadcast_select_fusion.refs_7_.proj_ref), custom_call_target="tpu_custom_call" | custom-call | tf_op jit(solution)/shard_map/pallas_call | solution.py:275
  37.1 0.5 collective-permute-start.9
  37.5 0.0 collective-permute-done.10.got_ref
  37.6 1.4 %collective-permute-start.11 = (bf16[4,24,448]{2,1,0:T(8,128)(2,1)S(1)}, bf16[4,24,448]{2,1,0:T(8,128)(2,1)S(1)}, u32[]{:S(2)}, u32[]{:S(2)}) collective-permute-start(bf16[4,24,448]{2,1,0:T(8,128)(2,1)S(1)} %shard_map.82), channel_id=1, source_target_pairs={{0,3},{1,2},{2,1},{3,0},{4,7},{5,6},{6,5},{7,4},{8,11},{9,10},{10,... | collective-permute-start | bytes 258056 | tf_op jit(solution)/shard_map/ppermute | solution.py:310
  39.0 0.0 collective-permute-done.9.got_ref
  39.0 3.4 %collective-permute-done.11.got_ref = bf16[4,24,448]{2,1,0:T(8,128)(2,1)S(1)} collective-permute-done((bf16[4,24,448]{2,1,0:T(8,128)(2,1)S(1)}, bf16[4,24,448]{2,1,0:T(8,128)(2,1)S(1)}, u32[]{:S(2)}, u32[]{:S(2)}) %collective-permute-start.11) | collective-permute-done | bytes 86048 | tf_op jit(solution)/shard_map/ppermute | solution.py:310
  42.4 3.0 %collective-permute-start.12 = (bf16[24,448]{1,0:T(8,128)(2,1)S(1)}, bf16[24,448]{1,0:T(8,128)(2,1)S(1)}, u32[]{:S(2)}, u32[]{:S(2)}) collective-permute-start(bf16[24,448]{1,0:T(8,128)(2,1)S(1)} %get-tuple-element.88), channel_id=1, source_target_pairs={{0,13},{1,12},{2,15},{3,14},{4,9},{5,8},{6,11},{7,10},{8,5},{9,4},... | collective-permute-start | bytes 64520 | tf_op jit(solution)/shard_map/ppermute | solution.py:310
  45.5 0.0 collective-permute-start.13
  45.5 0.9 %collective-permute-start.14 = (bf16[24,448]{1,0:T(8,128)(2,1)S(1)}, bf16[24,448]{1,0:T(8,128)(2,1)S(1)}, u32[]{:S(2)}, u32[]{:S(2)}) collective-permute-start(bf16[24,448]{1,0:T(8,128)(2,1)S(1)} %get-tuple-element.90), channel_id=1, source_target_pairs={{0,5},{1,4},{2,7},{3,6},{4,1},{5,0},{6,3},{7,2},{8,13},{9,12},{10,... | collective-permute-start | bytes 64520 | tf_op jit(solution)/shard_map/ppermute | solution.py:310
  46.3 1.2 %collective-permute-done.12 = bf16[24,448]{1,0:T(8,128)(2,1)S(1)} collective-permute-done((bf16[24,448]{1,0:T(8,128)(2,1)S(1)}, bf16[24,448]{1,0:T(8,128)(2,1)S(1)}, u32[]{:S(2)}, u32[]{:S(2)}) %collective-permute-start.12) | collective-permute-done | bytes 21536 | tf_op jit(solution)/shard_map/ppermute | solution.py:310
  47.6 2.3 %collective-permute-done.13 = bf16[24,448]{1,0:T(8,128)(2,1)S(1)} collective-permute-done((bf16[24,448]{1,0:T(8,128)(2,1)S(1)}, bf16[24,448]{1,0:T(8,128)(2,1)S(1)}, u32[]{:S(2)}, u32[]{:S(2)}) %collective-permute-start.13) | collective-permute-done | bytes 21536 | tf_op jit(solution)/shard_map/ppermute | solution.py:310
  49.9 0.0 collective-permute-done.14
  49.9 0.6 %add_convert_fusion = bf16[24,448]{1,0:T(8,128)(2,1)} fusion(bf16[24,448]{1,0:T(8,128)(2,1)S(1)} %collective-permute-done.14, bf16[24,448]{1,0:T(8,128)(2,1)S(1)} %collective-permute-done.13, f32[24,448]{1,0:T(8,128)S(1)} %get-tuple-element.87, bf16[24,448]{1,0:T(8,128)(2,1)S(1)} %collective-permute-done.12), kind=kLoop, calls=%fused_computation.2 | loop fusion | flops 75264 | bytes 129024 | tf_op jit(solution)/shard_map/convert_element_type | solution.py:407
  (11 shorter events, 0.1 us)
Async XLA Ops:
  0.0 16.5 %collective-permute-start.2 = (bf16[576,512]{1,0:T(8,128)(2,1)}, bf16[576,512]{1,0:T(8,128)(2,1)S(1)}, u32[]{:S(2)}, u32[]{:S(2)}) collective-permute-start(bf16[576,512]{1,0:T(8,128)(2,1)} %bitcast.36), channel_id=1, source_target_pairs={{0,3},{1,2},{2,1},{3,0},{4,7},{5,6},{6,5},{7,4},{8,11},{9,10},{10,... | collective-permute-start | bytes 1769480 | tf_op jit(solution)/shard_map/ppermute | solution.py:310
  2.4 15.4 %collective-permute-start.4 = (bf16[24,4,576]{2,1,0:T(4,128)(2,1)}, bf16[24,4,576]{2,1,0:T(4,128)(2,1)S(1)}, u32[]{:S(2)}, u32[]{:S(2)}) collective-permute-start(bf16[24,4,576]{2,1,0:T(4,128)(2,1)} %bitcast.38), channel_id=1, source_target_pairs={{0,5},{1,4},{2,7},{3,6},{4,1},{5,0},{6,3},{7,2},{8,13},{9,12},{10,... | collective-permute-start | bytes 331784 | tf_op jit(solution)/shard_map/ppermute | solution.py:310
  4.3 13.5 %collective-permute-start.1 = (bf16[24,4,576]{2,1,0:T(4,128)(2,1)}, bf16[24,4,576]{2,1,0:T(4,128)(2,1)S(1)}, u32[]{:S(2)}, u32[]{:S(2)}) collective-permute-start(bf16[24,4,576]{2,1,0:T(4,128)(2,1)} %bitcast.39), channel_id=1, source_target_pairs={{0,13},{1,12},{2,15},{3,14},{4,9},{5,8},{6,11},{7,10},{8,5},{9,4},... | collective-permute-start | bytes 331784 | tf_op jit(solution)/shard_map/ppermute | solution.py:310
  6.3 11.6 %collective-permute-start = (bf16[24,4,576]{2,1,0:T(4,128)(2,1)}, bf16[24,4,576]{2,1,0:T(4,128)(2,1)S(1)}, u32[]{:S(2)}, u32[]{:S(2)}) collective-permute-start(bf16[24,4,576]{2,1,0:T(4,128)(2,1)} %bitcast.40), channel_id=1, source_target_pairs={{0,9},{1,8},{2,11},{3,10},{4,13},{5,12},{6,15},{7,14},{8,1},{9,0},... | collective-permute-start | bytes 331784 | tf_op jit(solution)/shard_map/ppermute | solution.py:310
  6.3 11.6 %collective-permute-start.5 = (bf16[576,512]{1,0:T(8,128)(2,1)}, bf16[576,512]{1,0:T(8,128)(2,1)S(1)}, u32[]{:S(2)}, u32[]{:S(2)}) collective-permute-start(bf16[576,512]{1,0:T(8,128)(2,1)} %bitcast.37), channel_id=1, source_target_pairs={{0,1},{1,0},{2,3},{3,2},{4,5},{5,4},{6,7},{7,6},{8,9},{9,8},{10,11... | collective-permute-start | bytes 1769480 | tf_op jit(solution)/shard_map/ppermute | solution.py:310
  16.5 4.6 %collective-permute-start.3 = (bf16[576,512]{1,0:T(8,128)(2,1)S(1)}, bf16[576,512]{1,0:T(8,128)(2,1)S(1)}, u32[]{:S(2)}, u32[]{:S(2)}) collective-permute-start(bf16[576,512]{1,0:T(8,128)(2,1)S(1)} %collective-permute-done.2.refs_5_), channel_id=1, source_target_pairs={{0,1},{1,0},{2,3},{3,2},{4,5},{5,4},{6,7},{7,6},{8,9},{9,8},{10,11... | collective-permute-start | bytes 1769480 | tf_op jit(solution)/shard_map/ppermute | solution.py:310
  21.8 10.8 %collective-permute-start.6 = (bf16[392,128]{1,0:T(8,128)(2,1)S(1)}, bf16[392,128]{1,0:T(8,128)(2,1)S(1)}, u32[]{:S(2)}, u32[]{:S(2)}) collective-permute-start(bf16[392,128]{1,0:T(8,128)(2,1)S(1)} %get-tuple-element.66), channel_id=1, source_target_pairs={{0,9},{1,8},{2,11},{3,10},{4,13},{5,12},{6,15},{7,14},{8,1},{9,0},... | collective-permute-start | bytes 301064 | tf_op jit(solution)/shard_map/ppermute | solution.py:310
  25.1 7.5 %collective-permute-start.7 = (bf16[392,128]{1,0:T(8,128)(2,1)S(1)}, bf16[392,128]{1,0:T(8,128)(2,1)S(1)}, u32[]{:S(2)}, u32[]{:S(2)}) collective-permute-start(bf16[392,128]{1,0:T(8,128)(2,1)S(1)} %get-tuple-element.67), channel_id=1, source_target_pairs={{0,13},{1,12},{2,15},{3,14},{4,9},{5,8},{6,11},{7,10},{8,5},{9,4},... | collective-permute-start | bytes 301064 | tf_op jit(solution)/shard_map/ppermute | solution.py:310
  27.0 4.0 %copy-start = (bf16[4,512,128]{2,1,0:T(8,128)(2,1)S(1)}, bf16[4,512,128]{2,1,0:T(8,128)(2,1)}, u32[]{:S(2)}) copy-start(bf16[4,512,128]{2,1,0:T(8,128)(2,1)} %up_from.1) | copy-start | bytes 1572868
  27.0 3.9 %copy-start.1 = (bf16[1,24,576]{2,1,0:T(8,128)(2,1)S(1)}, bf16[1,24,576]{2,1,0:T(8,128)(2,1)}, u32[]{:S(2)}) copy-start(bf16[1,24,576]{2,1,0:T(8,128)(2,1)} %param.9) | copy-start | bytes 82948
  27.0 3.9 %copy-start.2 = (s32[1,24]{1,0:T(1,128)S(1)}, s32[1,24]{1,0:T(1,128)}, u32[]{:S(2)}) copy-start(s32[1,24]{1,0:T(1,128)} %parents_ref.1) | copy-start | bytes 292
  27.0 7.9 %collective-permute-start.8 = (bf16[392,128]{1,0:T(8,128)(2,1)S(1)}, bf16[392,128]{1,0:T(8,128)(2,1)S(1)}, u32[]{:S(2)}, u32[]{:S(2)}) collective-permute-start(bf16[392,128]{1,0:T(8,128)(2,1)S(1)} %get-tuple-element.74), channel_id=1, source_target_pairs={{0,5},{1,4},{2,7},{3,6},{4,1},{5,0},{6,3},{7,2},{8,13},{9,12},{10,... | collective-permute-start | bytes 301064 | tf_op jit(solution)/shard_map/ppermute | solution.py:310
  36.1 1.4 %collective-permute-start.10 = (bf16[4,24,448]{2,1,0:T(8,128)(2,1)S(1)}, bf16[4,24,448]{2,1,0:T(8,128)(2,1)S(1)}, u32[]{:S(2)}, u32[]{:S(2)}) collective-permute-start(bf16[4,24,448]{2,1,0:T(8,128)(2,1)S(1)} %get-tuple-element.86), channel_id=1, source_target_pairs={{0,1},{1,0},{2,3},{3,2},{4,5},{5,4},{6,7},{7,6},{8,9},{9,8},{10,11... | collective-permute-start | bytes 258056 | tf_op jit(solution)/shard_map/ppermute | solution.py:310
  37.1 1.9 %collective-permute-start.9 = (bf16[4,24,448]{2,1,0:T(8,128)(2,1)S(1)}, bf16[4,24,448]{2,1,0:T(8,128)(2,1)S(1)}, u32[]{:S(2)}, u32[]{:S(2)}) collective-permute-start(bf16[4,24,448]{2,1,0:T(8,128)(2,1)S(1)} %get-tuple-element.84), channel_id=1, source_target_pairs={{0,1},{1,0},{2,3},{3,2},{4,5},{5,4},{6,7},{7,6},{8,9},{9,8},{10,11... | collective-permute-start | bytes 258056 | tf_op jit(solution)/shard_map/ppermute | solution.py:310
  37.6 4.9 %collective-permute-start.11 = (bf16[4,24,448]{2,1,0:T(8,128)(2,1)S(1)}, bf16[4,24,448]{2,1,0:T(8,128)(2,1)S(1)}, u32[]{:S(2)}, u32[]{:S(2)}) collective-permute-start(bf16[4,24,448]{2,1,0:T(8,128)(2,1)S(1)} %shard_map.82), channel_id=1, source_target_pairs={{0,3},{1,2},{2,1},{3,0},{4,7},{5,6},{6,5},{7,4},{8,11},{9,10},{10,... | collective-permute-start | bytes 258056 | tf_op jit(solution)/shard_map/ppermute | solution.py:310
  42.4 5.1 %collective-permute-start.12 = (bf16[24,448]{1,0:T(8,128)(2,1)S(1)}, bf16[24,448]{1,0:T(8,128)(2,1)S(1)}, u32[]{:S(2)}, u32[]{:S(2)}) collective-permute-start(bf16[24,448]{1,0:T(8,128)(2,1)S(1)} %get-tuple-element.88), channel_id=1, source_target_pairs={{0,13},{1,12},{2,15},{3,14},{4,9},{5,8},{6,11},{7,10},{8,5},{9,4},... | collective-permute-start | bytes 64520 | tf_op jit(solution)/shard_map/ppermute | solution.py:310
  45.5 4.4 %collective-permute-start.13 = (bf16[24,448]{1,0:T(8,128)(2,1)S(1)}, bf16[24,448]{1,0:T(8,128)(2,1)S(1)}, u32[]{:S(2)}, u32[]{:S(2)}) collective-permute-start(bf16[24,448]{1,0:T(8,128)(2,1)S(1)} %get-tuple-element.89), channel_id=1, source_target_pairs={{0,9},{1,8},{2,11},{3,10},{4,13},{5,12},{6,15},{7,14},{8,1},{9,0},... | collective-permute-start | bytes 64520 | tf_op jit(solution)/shard_map/ppermute | solution.py:310
  45.5 4.4 %collective-permute-start.14 = (bf16[24,448]{1,0:T(8,128)(2,1)S(1)}, bf16[24,448]{1,0:T(8,128)(2,1)S(1)}, u32[]{:S(2)}, u32[]{:S(2)}) collective-permute-start(bf16[24,448]{1,0:T(8,128)(2,1)S(1)} %get-tuple-element.90), channel_id=1, source_target_pairs={{0,5},{1,4},{2,7},{3,6},{4,1},{5,0},{6,3},{7,2},{8,13},{9,12},{10,... | collective-permute-start | bytes 64520 | tf_op jit(solution)/shard_map/ppermute | solution.py:310

commit v7 on v6

--- a/solution.py
+++ b/solution.py
@@ -216,8 +216,10 @@
     for spot in range(keep_ref.shape[0]):
         at = pl.multiple_of((2 * spot + side) * span, span)
         part = jnp.dot(flat, proj_ref[:, pl.ds(at, span)], preferred_element_type=jnp.float32)
-        elsewhere = jnp.where(outer == spot, 0, 1)
-        share(part, 0, spot, keep_ref, send_ref, elsewhere + across)
+        straight = outer == spot
+        if across:
+            straight |= outer == lax.bitwise_xor(spot, keep_ref.shape[0] - 1)
+        share(part, 0, spot, keep_ref, send_ref, jnp.where(straight, 0, 1) + across)
 
 
 def leaving_kernel(peers, *refs):
@@ -230,8 +232,21 @@
     project_kernel(0, flat_ref[...], proj_ref, keep_ref, send_ref)
 
 
-def add_kernel(keep_ref, got_ref, out_ref):
-    out_ref[...] = (keep_ref[...] + got_ref[...].astype(jnp.float32)).astype(out_ref.dtype)
+def add_kernel(keep_ref, got_ref, out_ref, direct_ref):
+    outer = lax.div(lax.axis_index("ctx"), 4)
+    for peer in range(keep_ref.shape[0]):
+        spot = lax.bitwise_xor(outer, peer)
+        value = keep_ref[spot] + got_ref[spot].astype(jnp.float32)
+        if peer < out_ref.shape[0]:
+            out_ref[peer] = value.astype(out_ref.dtype)
+        else:
+            direct_ref[...] = value.astype(direct_ref.dtype)
+
+
+def depart_kernel(stay_ref, got_ref, own_ref, *out_refs):
+    for peer, out_ref in enumerate((own_ref, *out_refs)):
+        value = stay_ref[peer] + got_ref[peer].astype(jnp.float32)
+        out_ref[...] = value.astype(out_ref.dtype)
 
 
 def whole_kernel(peers, *refs):
@@ -387,23 +402,35 @@
         )
         got_leaving = swap(send, 1)
         stay, stay_send = call(staying_kernel, halves_of(chips // 2), (flat, proj_here))
-        send = call(add_kernel, (halves_of(chips // 2)[1],), (keep, got_leaving))[0]
+        thin = shaped(drafts, columns, dtype=bf16)
+        wide, narrow = halves_of(outer - 1)
+        leave, direct_across = call(add_kernel, (narrow, thin), (keep, got_leaving))
         got_staying = swap(stay_send, 1)
-        stay = call(add_kernel, (halves_of(chips // 2)[0],), (stay, got_staying))[0]
+        stay, direct = call(add_kernel, (wide, thin), (stay, got_staying))
+        last = inner * (outer - 1)
+        came = [swap(direct, last + 1), swap(direct_across, last + 3)]
+        own, *parts = call(
+            depart_kernel,
+            (shaped(drafts, columns),) + (thin,) * (outer - 2),
+            (stay, swap(leave, 3)),
+        )
     else:
         flat, keep, send = call(
             lambda *refs: whole_kernel(outer, *refs), (flat_shape, *halves_of(chips)), inputs
         )
         stay, send = call(pair_kernel, halves_of(chips // 2), (keep, swap(send, 1)))
-    own, *parts = call(
-        quad_kernel,
-        (shaped(drafts, columns),)
-        + tuple(shaped(drafts, columns, dtype=bf16) for _ in range(outer - 1)),
-        (stay, swap(send, 2 + cross)),
-    )
+        own, *parts = call(
+            quad_kernel,
+            (shaped(drafts, columns),)
+            + tuple(shaped(drafts, columns, dtype=bf16) for _ in range(outer - 1)),
+            (stay, swap(send, 2)),
+        )
+        came = []
+    for peer in range(len(parts), 0, -1):
+        came.append(swap(parts[peer - 1], inner * peer + cross))
     result = own
-    for peer in range(outer - 1, 0, -1):
-        result = result + swap(parts[peer - 1], inner * peer + cross).astype(jnp.float32)
+    for value in came:
+        result = result + value.astype(jnp.float32)
     return result.astype(bf16)
 
 

time: 50.7 us -> 49.4 us (0.974)
  waiting for transfers between devices: 17.9 us -> 12.8 us
  starting transfers between devices: 17.9 us -> 21.7 us
    ppermute x15 -> x16, waiting for transfers between devices: 17.9 us -> 12.8 us  [swap(): return lax.ppermute(value, 'ctx', [(i, i ^ bits) for i in range(count)])]
    ppermute x15 -> x16, starting transfers between devices: 17.9 us -> 21.7 us  [swap(): return lax.ppermute(value, 'ctx', [(i, i ^ bits) for i in range(count)])]
  transfers between devices with their start and end apart: 15 -> 16, of which waited for: 7 -> 6; matrix products, arithmetic and copies ran while one was open for 11% -> 12% of each run, Pallas kernels for 11% -> 11%
where the time goes in v7:
time: 49.4 us; the launch traced here: 49.2 us
  starting transfers between devices  21.7 us (44%)
  waiting for transfers between devices  12.8 us (26%)
  Pallas kernels  7.52 us (15%)
  other arithmetic  5.33 us (11%)
  local copies, waits for them, and re-layouts  0.99 us (2%)
  between operations  0.87 us (2%)
    ppermute x16, starting transfers between devices, swap(): return lax.ppermute(value, 'ctx', [(i, i ^ bits) for i in range(count)])  21.7 us
    ppermute x16, waiting for transfers between devices, swap(): return lax.ppermute(value, 'ctx', [(i, i ^ bits) for i in range(count)])  12.8 us
    pallas_call x11, Pallas kernels, call(): pl.pallas_call(kernel, out_shape=outs, in_specs=specs or [pl.BlockSpec()...  7.52 us
    select_n x2, other arithmetic, on_chip(): return jnp.where(lengths[0] > -1, value, jnp.zeros_like(value))  4.67 us
  transfers between devices with their start and end apart: 16, of which 6 were waited for; matrix products, arithmetic and copies ran while one was open for 12% of the time, Pallas kernels for 11%

profile of v7, /device:TPU:0, one launch (start us, length us, event | category | flops | bytes accessed | tf_op | source)
XLA Modules:
  0.0 49.2 jit_solution(16362588806551457549)
XLA Ops:
  0.0 2.4 %collective-permute-start.2 = (bf16[576,512]{1,0:T(8,128)(2,1)}, bf16[576,512]{1,0:T(8,128)(2,1)S(1)}, u32[]{:S(2)}, u32[]{:S(2)}) collective-permute-start(bf16[576,512]{1,0:T(8,128)(2,1)} %bitcast.36), channel_id=1, source_target_pairs={{0,3},{1,2},{2,1},{3,0},{4,7},{5,6},{6,5},{7,4},{8,11},{9,10},{10,... | collective-permute-start | bytes 1769480 | tf_op jit(solution)/shard_map/ppermute | solution.py:325
  2.4 1.9 %collective-permute-start.4 = (bf16[24,4,576]{2,1,0:T(4,128)(2,1)}, bf16[24,4,576]{2,1,0:T(4,128)(2,1)S(1)}, u32[]{:S(2)}, u32[]{:S(2)}) collective-permute-start(bf16[24,4,576]{2,1,0:T(4,128)(2,1)} %bitcast.38), channel_id=1, source_target_pairs={{0,5},{1,4},{2,7},{3,6},{4,1},{5,0},{6,3},{7,2},{8,13},{9,12},{10,... | collective-permute-start | bytes 331784 | tf_op jit(solution)/shard_map/ppermute | solution.py:325
  4.3 2.0 %collective-permute-start.1 = (bf16[24,4,576]{2,1,0:T(4,128)(2,1)}, bf16[24,4,576]{2,1,0:T(4,128)(2,1)S(1)}, u32[]{:S(2)}, u32[]{:S(2)}) collective-permute-start(bf16[24,4,576]{2,1,0:T(4,128)(2,1)} %bitcast.39), channel_id=1, source_target_pairs={{0,13},{1,12},{2,15},{3,14},{4,9},{5,8},{6,11},{7,10},{8,5},{9,4},... | collective-permute-start | bytes 331784 | tf_op jit(solution)/shard_map/ppermute | solution.py:325
  6.3 0.0 collective-permute-start
  6.3 0.7 %collective-permute-start.5 = (bf16[576,512]{1,0:T(8,128)(2,1)}, bf16[576,512]{1,0:T(8,128)(2,1)S(1)}, u32[]{:S(2)}, u32[]{:S(2)}) collective-permute-start(bf16[576,512]{1,0:T(8,128)(2,1)} %bitcast.37), channel_id=1, source_target_pairs={{0,1},{1,0},{2,3},{3,2},{4,5},{5,4},{6,7},{7,6},{8,9},{9,8},{10,11... | collective-permute-start | bytes 1769480 | tf_op jit(solution)/shard_map/ppermute | solution.py:325
  7.7 0.9 %copy.10 = bf16[4,24,576]{2,1,0:T(8,128)(2,1)S(1)} copy(bf16[4,24,576]{2,0,1:T(4,128)(2,1)} %bitcast.41) | data formatting | bytes 221184 | tf_op jit(solution)/shard_map/transpose | solution.py:338
  8.6 7.9 %collective-permute-done.2.refs_5_ = bf16[576,512]{1,0:T(8,128)(2,1)S(1)} collective-permute-done((bf16[576,512]{1,0:T(8,128)(2,1)}, bf16[576,512]{1,0:T(8,128)(2,1)S(1)}, u32[]{:S(2)}, u32[]{:S(2)}) %collective-permute-start.2) | collective-permute-done | bytes 589856 | tf_op jit(solution)/shard_map/ppermute | solution.py:325
  16.5 0.2 collective-permute-start.3
  16.7 1.1 %broadcast_select_fusion.1.refs_4_.refs_2_ = bf16[576,512]{1,0:T(8,128)(2,1)S(1)} fusion(pred[]{:T(512)S(6)} %gt.4, bf16[1,512,576]{1,2,0:T(8,128)(2,1)} %param.8), kind=kLoop, calls=%fused_computation.1 | loop fusion | flops 294912 | bytes 1179649 | tf_op jit(solution)/shard_map/jit(_where)/select_n | solution.py:328
  17.8 0.0 collective-permute-done.4
  17.8 0.0 collective-permute-done.1
  17.9 0.1 collective-permute-done
  18.0 0.0 collective-permute-done.5.refs_5_.refs_3_
  18.0 0.8 %shard_map.74 = (f32[96,512]{1,0:T(8,128)S(1)}, f32[96,1]{1,0:T(8,128)S(1)}, f32[96,1]{1,0:T(8,128)S(1)}) custom-call(f32[1,1024]{1,0:T(1,128)S(1)} %compare_select_fusion.refs_0_, bf16[96,576]{1,0:T(8,128)(2,1)S(1)} %bitcast.32, bf16[576,512]{1,0:T(8,128)(2,1)S(1)} %broadcast_select_fusion.1.refs_4_.refs_2_, ...), custom_call_target="tpu_custom_call" | custom-call | tf_op jit(solution)/shard_map/pallas_call | solution.py:290
  18.8 1.2 %shard_map.73 = (f32[96,512]{1,0:T(8,128)S(1)}, f32[96,1]{1,0:T(8,128)S(1)}, f32[96,1]{1,0:T(8,128)S(1)}, f32[96,512]{1,0:T(8,128)S(1)}, f32[96,1]{1,0:T(8,128)S...) custom-call(f32[1,1024]{1,0:T(1,128)S(1)} %compare_select_fusion.refs_0_, ...), custom_call_target="tpu_custom_call" | custom-call | tf_op jit(solution)/shard_map/pallas_call | solution.py:290
  20.0 1.1 %shard_map.75 = (f32[96,512]{1,0:T(8,128)S(1)}, f32[96,1]{1,0:T(8,128)S(1)}, f32[96,1]{1,0:T(8,128)S(1)}, f32[96,512]{1,0:T(8,128)S(1)}, f32[96,1]{1,0:T(8,128)S...) custom-call(f32[1,512]{1,0:T(1,128)S(1)} %compare_select_fusion.1.re, ...), custom_call_target="tpu_custom_call" | custom-call | tf_op jit(solution)/shard_map/pallas_call | solution.py:290
  21.1 0.0 collective-permute-done.3.refs_3_
  21.1 0.8 %shard_map.76 = (bf16[392,128]{1,0:T(8,128)(2,1)S(1)}, bf16[392,128]{1,0:T(8,128)(2,1)S(1)}) custom-call(f32[1,512]{1,0:T(1,128)S(1)} %compare_select_fusion.2.refs_0_, bf16[96,576]{1,0:T(8,128)(2,1)S(1)} %bitcast.34, bf16[96,576]{1,0:T(8,128)(2,1)S(1)} %bitcast.31, bf16[576,512]{1,0:T(8,128)(2,1)S(1)} %collective-permute-done.3.refs_3_, ...), custom_call_target="tpu_custom_call" | custom-call | tf_op jit(solution)/shard_map/pallas_call | solution.py:290
  21.8 3.3 %collective-permute-start.6 = (bf16[392,128]{1,0:T(8,128)(2,1)S(1)}, bf16[392,128]{1,0:T(8,128)(2,1)S(1)}, u32[]{:S(2)}, u32[]{:S(2)}) collective-permute-start(bf16[392,128]{1,0:T(8,128)(2,1)S(1)} %get-tuple-element.69), channel_id=1, source_target_pairs={{0,9},{1,8},{2,11},{3,10},{4,13},{5,12},{6,15},{7,14},{8,1},{9,0},... | collective-permute-start | bytes 301064 | tf_op jit(solution)/shard_map/ppermute | solution.py:325
  25.1 1.1 %collective-permute-start.7 = (bf16[392,128]{1,0:T(8,128)(2,1)S(1)}, bf16[392,128]{1,0:T(8,128)(2,1)S(1)}, u32[]{:S(2)}, u32[]{:S(2)}) collective-permute-start(bf16[392,128]{1,0:T(8,128)(2,1)S(1)} %get-tuple-element.70), channel_id=1, source_target_pairs={{0,13},{1,12},{2,15},{3,14},{4,9},{5,8},{6,11},{7,10},{8,5},{9,4},... | collective-permute-start | bytes 301064 | tf_op jit(solution)/shard_map/ppermute | solution.py:325
  26.2 0.8 %shard_map.77 = (f32[96,512]{1,0:T(8,128)S(1)}, f32[96,1]{1,0:T(8,128)S(1)}, f32[96,1]{1,0:T(8,128)S(1)}, bf16[392,128]{1,0:T(8,128)(2,1)S(1)}) custom-call(f32[1,512]{1,0:T(1,128)S(1)} %compare_select_fusion.2.refs_0_, bf16[96,576]{1,0:T(8,128)(2,1)S(1)} %bitcast.24, bf16[96,576]{1,0:T(8,128)(2,1)S(1)} %bitcast.28, ...), custom_call_target="tpu_custom_call" | custom-call | tf_op jit(solution)/shard_map/pallas_call | solution.py:290
  27.0 0.0 copy-start
  27.0 0.0 copy-start.1
  27.0 0.0 copy-start.2
  27.0 0.4 collective-permute-start.8
  27.4 3.6 %broadcast_select_fusion.refs_7_.proj_ref = bf16[512,7168]{1,0:T(8,128)(2,1)S(1)} fusion(bf16[512,7168]{1,0:T(8,128)(2,1)} %param.13, pred[]{:T(512)S(6)} %gt.4), kind=kLoop, calls=%fused_computation | loop fusion | flops 3670016 | bytes 14680065 | tf_op jit(solution)/shard_map/jit(_where)/select_n | solution.py:328
  30.9 0.0 copy-done
  31.0 0.0 copy-done.1
  31.0 0.0 copy-done.2
  31.0 1.0 %shard_map.78 = (f32[96,512]{1,0:T(8,128)S(1)}, f32[96,1]{1,0:T(8,128)S(1)}, f32[96,1]{1,0:T(8,128)S(1)}, bf16[4,512,128]{2,1,0:T(8,128)(2,1)S(1)}) custom-call(bf16[96,576]{1,0:T(8,128)(2,1)S(1)} %bitcast.25, bf16[24,576]{1,0:T(8,128)(2,1)S(1)} %bitcast.35, s32[1,24]{1,0:T(1,128)S(1)} %copy-done.2, bf16[4,512,128]{2,1,0:T(8,128)(2,1)S(1)} %copy-done, ...), custom_call_target="tpu_custom_call" | custom-call | tf_op jit(solution)/shard_map/pallas_call | solution.py:290
  31.9 0.7 %collective-permute-done.6.refs_0_ = bf16[392,128]{1,0:T(8,128)(2,1)S(1)} collective-permute-done((bf16[392,128]{1,0:T(8,128)(2,1)S(1)}, bf16[392,128]{1,0:T(8,128)(2,1)S(1)}, u32[]{:S(2)}, u32[]{:S(2)}) %collective-permute-start.6) | collective-permute-done | bytes 100384 | tf_op jit(solution)/shard_map/ppermute | solution.py:325
  32.7 0.0 collective-permute-done.7.refs_1_
  32.7 2.3 %collective-permute-done.8.refs_2_ = bf16[392,128]{1,0:T(8,128)(2,1)S(1)} collective-permute-done((bf16[392,128]{1,0:T(8,128)(2,1)S(1)}, bf16[392,128]{1,0:T(8,128)(2,1)S(1)}, u32[]{:S(2)}, u32[]{:S(2)}) %collective-permute-start.8) | collective-permute-done | bytes 100384 | tf_op jit(solution)/shard_map/ppermute | solution.py:325
  34.9 1.1 %shard_map.79 = (bf16[24,512]{1,0:T(8,128)(2,1)S(1)}, f32[4,24,448]{2,1,0:T(8,128)S(1)}, bf16[4,24,448]{2,1,0:T(8,128)(2,1)S(1)}) custom-call(bf16[392,128]{1,0:T(8,128)(2,1)S(1)} %collective-permute-done.6.refs_0_, bf16[392,128]{1,0:T(8,128)(2,1)S(1)} %collective-permute-done.7.refs_1_, bf16[392,128]{1,0:T(8,128)(2,1)S(1)} %collective-permute-done.8.refs_2_, ...), custom_call_target="tpu_custom_call" | custom-call | tf_op jit(solution)/shard_map/pallas_call | solution.py:290
  36.1 0.2 collective-permute-start.10
  36.3 0.8 %shard_map.80 = (f32[4,24,448]{2,1,0:T(8,128)S(1)}, bf16[4,24,448]{2,1,0:T(8,128)(2,1)S(1)}) custom-call(bf16[24,512]{1,0:T(8,128)(2,1)S(1)} %get-tuple-element.85.flat_ref, bf16[512,7168]{1,0:T(8,128)(2,1)S(1)} %broadcast_select_fusion.refs_7_.proj_ref), custom_call_target="tpu_custom_call" | custom-call | tf_op jit(solution)/shard_map/pallas_call | solution.py:290
  37.1 0.5 collective-permute-start.9
  37.5 0.0 collective-permute-done.10.got_ref
  37.6 1.4 %collective-permute-start.11 = (bf16[3,24,448]{2,1,0:T(8,128)(2,1)S(1)}, bf16[3,24,448]{2,1,0:T(8,128)(2,1)S(1)}, u32[]{:S(2)}, u32[]{:S(2)}) collective-permute-start(bf16[3,24,448]{2,1,0:T(8,128)(2,1)S(1)} %get-tuple-element.91), channel_id=1, source_target_pairs={{0,3},{1,2},{2,1},{3,0},{4,7},{5,6},{6,5},{7,4},{8,11},{9,10},{10,... | collective-permute-start | bytes 193544 | tf_op jit(solution)/shard_map/ppermute | solution.py:325
  39.0 0.0 collective-permute-done.9.got_ref
  39.0 3.3 %collective-permute-start.12 = (bf16[24,448]{1,0:T(8,128)(2,1)S(1)}, bf16[24,448]{1,0:T(8,128)(2,1)S(1)}, u32[]{:S(2)}, u32[]{:S(2)}) collective-permute-start(bf16[24,448]{1,0:T(8,128)(2,1)S(1)} %get-tuple-element.93), channel_id=1, source_target_pairs={{0,13},{1,12},{2,15},{3,14},{4,9},{5,8},{6,11},{7,10},{8,5},{9,4},... | collective-permute-start | bytes 64520 | tf_op jit(solution)/shard_map/ppermute | solution.py:325
  42.3 0.9 %collective-permute-start.13 = (bf16[24,448]{1,0:T(8,128)(2,1)S(1)}, bf16[24,448]{1,0:T(8,128)(2,1)S(1)}, u32[]{:S(2)}, u32[]{:S(2)}) collective-permute-start(bf16[24,448]{1,0:T(8,128)(2,1)S(1)} %get-tuple-element.94), channel_id=1, source_target_pairs={{0,15},{1,14},{2,13},{3,12},{4,11},{5,10},{6,9},{7,8},{8,7},{9,6},... | collective-permute-start | bytes 64520 | tf_op jit(solution)/shard_map/ppermute | solution.py:325
  43.2 0.0 collective-permute-done.11.got_ref
  43.2 1.5 %collective-permute-start.14 = (bf16[24,448]{1,0:T(8,128)(2,1)S(1)}, bf16[24,448]{1,0:T(8,128)(2,1)S(1)}, u32[]{:S(2)}, u32[]{:S(2)}) collective-permute-start(bf16[24,448]{1,0:T(8,128)(2,1)S(1)} %get-tuple-element.95), channel_id=1, source_target_pairs={{0,9},{1,8},{2,11},{3,10},{4,13},{5,12},{6,15},{7,14},{8,1},{9,0},... | collective-permute-start | bytes 64520 | tf_op jit(solution)/shard_map/ppermute | solution.py:325
  44.7 2.1 %collective-permute-start.15 = (bf16[24,448]{1,0:T(8,128)(2,1)S(1)}, bf16[24,448]{1,0:T(8,128)(2,1)S(1)}, u32[]{:S(2)}, u32[]{:S(2)}) collective-permute-start(bf16[24,448]{1,0:T(8,128)(2,1)S(1)} %get-tuple-element.96), channel_id=1, source_target_pairs={{0,5},{1,4},{2,7},{3,6},{4,1},{5,0},{6,3},{7,2},{8,13},{9,12},{10,... | collective-permute-start | bytes 64520 | tf_op jit(solution)/shard_map/ppermute | solution.py:325
  46.8 0.0 collective-permute-done.12
  46.8 1.5 %collective-permute-done.13 = bf16[24,448]{1,0:T(8,128)(2,1)S(1)} collective-permute-done((bf16[24,448]{1,0:T(8,128)(2,1)S(1)}, bf16[24,448]{1,0:T(8,128)(2,1)S(1)}, u32[]{:S(2)}, u32[]{:S(2)}) %collective-permute-start.13) | collective-permute-done | bytes 21536 | tf_op jit(solution)/shard_map/ppermute | solution.py:325
  48.2 0.0 collective-permute-done.14
  48.2 0.3 collective-permute-done.15
  48.6 0.6 %add_convert_fusion = bf16[24,448]{1,0:T(8,128)(2,1)} fusion(bf16[24,448]{1,0:T(8,128)(2,1)S(1)} %collective-permute-done.15, bf16[24,448]{1,0:T(8,128)(2,1)S(1)} %collective-permute-done.14, bf16[24,448]{1,0:T(8,128)(2,1)S(1)} %collective-permute-done.13, f32[24,448]{1,0:T(8,128)S(1)} %get-tuple-element.92, bf16[24,448]{1,0:T(8,128)(2,1)S(1)} %collective-permute-done.12), kind=kLoop, calls=%fused_computation.2 | loop fusion | flops 96768 | bytes 150528 | tf_op jit(solution)/shard_map/convert_element_type | solution.py:434
  (11 shorter events, 0.1 us)
Async XLA Ops:
  0.0 16.5 %collective-permute-start.2 = (bf16[576,512]{1,0:T(8,128)(2,1)}, bf16[576,512]{1,0:T(8,128)(2,1)S(1)}, u32[]{:S(2)}, u32[]{:S(2)}) collective-permute-start(bf16[576,512]{1,0:T(8,128)(2,1)} %bitcast.36), channel_id=1, source_target_pairs={{0,3},{1,2},{2,1},{3,0},{4,7},{5,6},{6,5},{7,4},{8,11},{9,10},{10,... | collective-permute-start | bytes 1769480 | tf_op jit(solution)/shard_map/ppermute | solution.py:325
  2.4 15.4 %collective-permute-start.4 = (bf16[24,4,576]{2,1,0:T(4,128)(2,1)}, bf16[24,4,576]{2,1,0:T(4,128)(2,1)S(1)}, u32[]{:S(2)}, u32[]{:S(2)}) collective-permute-start(bf16[24,4,576]{2,1,0:T(4,128)(2,1)} %bitcast.38), channel_id=1, source_target_pairs={{0,5},{1,4},{2,7},{3,6},{4,1},{5,0},{6,3},{7,2},{8,13},{9,12},{10,... | collective-permute-start | bytes 331784 | tf_op jit(solution)/shard_map/ppermute | solution.py:325
  4.3 13.5 %collective-permute-start.1 = (bf16[24,4,576]{2,1,0:T(4,128)(2,1)}, bf16[24,4,576]{2,1,0:T(4,128)(2,1)S(1)}, u32[]{:S(2)}, u32[]{:S(2)}) collective-permute-start(bf16[24,4,576]{2,1,0:T(4,128)(2,1)} %bitcast.39), channel_id=1, source_target_pairs={{0,13},{1,12},{2,15},{3,14},{4,9},{5,8},{6,11},{7,10},{8,5},{9,4},... | collective-permute-start | bytes 331784 | tf_op jit(solution)/shard_map/ppermute | solution.py:325
  6.3 11.6 %collective-permute-start = (bf16[24,4,576]{2,1,0:T(4,128)(2,1)}, bf16[24,4,576]{2,1,0:T(4,128)(2,1)S(1)}, u32[]{:S(2)}, u32[]{:S(2)}) collective-permute-start(bf16[24,4,576]{2,1,0:T(4,128)(2,1)} %bitcast.40), channel_id=1, source_target_pairs={{0,9},{1,8},{2,11},{3,10},{4,13},{5,12},{6,15},{7,14},{8,1},{9,0},... | collective-permute-start | bytes 331784 | tf_op jit(solution)/shard_map/ppermute | solution.py:325
  6.3 11.6 %collective-permute-start.5 = (bf16[576,512]{1,0:T(8,128)(2,1)}, bf16[576,512]{1,0:T(8,128)(2,1)S(1)}, u32[]{:S(2)}, u32[]{:S(2)}) collective-permute-start(bf16[576,512]{1,0:T(8,128)(2,1)} %bitcast.37), channel_id=1, source_target_pairs={{0,1},{1,0},{2,3},{3,2},{4,5},{5,4},{6,7},{7,6},{8,9},{9,8},{10,11... | collective-permute-start | bytes 1769480 | tf_op jit(solution)/shard_map/ppermute | solution.py:325
  16.5 4.6 %collective-permute-start.3 = (bf16[576,512]{1,0:T(8,128)(2,1)S(1)}, bf16[576,512]{1,0:T(8,128)(2,1)S(1)}, u32[]{:S(2)}, u32[]{:S(2)}) collective-permute-start(bf16[576,512]{1,0:T(8,128)(2,1)S(1)} %collective-permute-done.2.refs_5_), channel_id=1, source_target_pairs={{0,1},{1,0},{2,3},{3,2},{4,5},{5,4},{6,7},{7,6},{8,9},{9,8},{10,11... | collective-permute-start | bytes 1769480 | tf_op jit(solution)/shard_map/ppermute | solution.py:325
  21.8 10.8 %collective-permute-start.6 = (bf16[392,128]{1,0:T(8,128)(2,1)S(1)}, bf16[392,128]{1,0:T(8,128)(2,1)S(1)}, u32[]{:S(2)}, u32[]{:S(2)}) collective-permute-start(bf16[392,128]{1,0:T(8,128)(2,1)S(1)} %get-tuple-element.69), channel_id=1, source_target_pairs={{0,9},{1,8},{2,11},{3,10},{4,13},{5,12},{6,15},{7,14},{8,1},{9,0},... | collective-permute-start | bytes 301064 | tf_op jit(solution)/shard_map/ppermute | solution.py:325
  25.1 7.5 %collective-permute-start.7 = (bf16[392,128]{1,0:T(8,128)(2,1)S(1)}, bf16[392,128]{1,0:T(8,128)(2,1)S(1)}, u32[]{:S(2)}, u32[]{:S(2)}) collective-permute-start(bf16[392,128]{1,0:T(8,128)(2,1)S(1)} %get-tuple-element.70), channel_id=1, source_target_pairs={{0,13},{1,12},{2,15},{3,14},{4,9},{5,8},{6,11},{7,10},{8,5},{9,4},... | collective-permute-start | bytes 301064 | tf_op jit(solution)/shard_map/ppermute | solution.py:325
  27.0 4.0 %copy-start = (bf16[4,512,128]{2,1,0:T(8,128)(2,1)S(1)}, bf16[4,512,128]{2,1,0:T(8,128)(2,1)}, u32[]{:S(2)}) copy-start(bf16[4,512,128]{2,1,0:T(8,128)(2,1)} %up_from.1) | copy-start | bytes 1572868
  27.0 3.9 %copy-start.1 = (bf16[1,24,576]{2,1,0:T(8,128)(2,1)S(1)}, bf16[1,24,576]{2,1,0:T(8,128)(2,1)}, u32[]{:S(2)}) copy-start(bf16[1,24,576]{2,1,0:T(8,128)(2,1)} %param.9) | copy-start | bytes 82948
  27.0 3.9 %copy-start.2 = (s32[1,24]{1,0:T(1,128)S(1)}, s32[1,24]{1,0:T(1,128)}, u32[]{:S(2)}) copy-start(s32[1,24]{1,0:T(1,128)} %parents_ref.1) | copy-start | bytes 292
  27.0 7.9 %collective-permute-start.8 = (bf16[392,128]{1,0:T(8,128)(2,1)S(1)}, bf16[392,128]{1,0:T(8,128)(2,1)S(1)}, u32[]{:S(2)}, u32[]{:S(2)}) collective-permute-start(bf16[392,128]{1,0:T(8,128)(2,1)S(1)} %get-tuple-element.77), channel_id=1, source_target_pairs={{0,5},{1,4},{2,7},{3,6},{4,1},{5,0},{6,3},{7,2},{8,13},{9,12},{10,... | collective-permute-start | bytes 301064 | tf_op jit(solution)/shard_map/ppermute | solution.py:325
  36.1 1.4 %collective-permute-start.10 = (bf16[4,24,448]{2,1,0:T(8,128)(2,1)S(1)}, bf16[4,24,448]{2,1,0:T(8,128)(2,1)S(1)}, u32[]{:S(2)}, u32[]{:S(2)}) collective-permute-start(bf16[4,24,448]{2,1,0:T(8,128)(2,1)S(1)} %get-tuple-element.90), channel_id=1, source_target_pairs={{0,1},{1,0},{2,3},{3,2},{4,5},{5,4},{6,7},{7,6},{8,9},{9,8},{10,11... | collective-permute-start | bytes 258056 | tf_op jit(solution)/shard_map/ppermute | solution.py:325
  37.1 1.9 %collective-permute-start.9 = (bf16[4,24,448]{2,1,0:T(8,128)(2,1)S(1)}, bf16[4,24,448]{2,1,0:T(8,128)(2,1)S(1)}, u32[]{:S(2)}, u32[]{:S(2)}) collective-permute-start(bf16[4,24,448]{2,1,0:T(8,128)(2,1)S(1)} %get-tuple-element.87), channel_id=1, source_target_pairs={{0,1},{1,0},{2,3},{3,2},{4,5},{5,4},{6,7},{7,6},{8,9},{9,8},{10,11... | collective-permute-start | bytes 258056 | tf_op jit(solution)/shard_map/ppermute | solution.py:325
  37.6 5.6 %collective-permute-start.11 = (bf16[3,24,448]{2,1,0:T(8,128)(2,1)S(1)}, bf16[3,24,448]{2,1,0:T(8,128)(2,1)S(1)}, u32[]{:S(2)}, u32[]{:S(2)}) collective-permute-start(bf16[3,24,448]{2,1,0:T(8,128)(2,1)S(1)} %get-tuple-element.91), channel_id=1, source_target_pairs={{0,3},{1,2},{2,1},{3,0},{4,7},{5,6},{6,5},{7,4},{8,11},{9,10},{10,... | collective-permute-start | bytes 193544 | tf_op jit(solution)/shard_map/ppermute | solution.py:325
  39.0 7.8 %collective-permute-start.12 = (bf16[24,448]{1,0:T(8,128)(2,1)S(1)}, bf16[24,448]{1,0:T(8,128)(2,1)S(1)}, u32[]{:S(2)}, u32[]{:S(2)}) collective-permute-start(bf16[24,448]{1,0:T(8,128)(2,1)S(1)} %get-tuple-element.93), channel_id=1, source_target_pairs={{0,13},{1,12},{2,15},{3,14},{4,9},{5,8},{6,11},{7,10},{8,5},{9,4},... | collective-permute-start | bytes 64520 | tf_op jit(solution)/shard_map/ppermute | solution.py:325
  42.3 6.0 %collective-permute-start.13 = (bf16[24,448]{1,0:T(8,128)(2,1)S(1)}, bf16[24,448]{1,0:T(8,128)(2,1)S(1)}, u32[]{:S(2)}, u32[]{:S(2)}) collective-permute-start(bf16[24,448]{1,0:T(8,128)(2,1)S(1)} %get-tuple-element.94), channel_id=1, source_target_pairs={{0,15},{1,14},{2,13},{3,12},{4,11},{5,10},{6,9},{7,8},{8,7},{9,6},... | collective-permute-start | bytes 64520 | tf_op jit(solution)/shard_map/ppermute | solution.py:325
  43.2 5.1 %collective-permute-start.14 = (bf16[24,448]{1,0:T(8,128)(2,1)S(1)}, bf16[24,448]{1,0:T(8,128)(2,1)S(1)}, u32[]{:S(2)}, u32[]{:S(2)}) collective-permute-start(bf16[24,448]{1,0:T(8,128)(2,1)S(1)} %get-tuple-element.95), channel_id=1, source_target_pairs={{0,9},{1,8},{2,11},{3,10},{4,13},{5,12},{6,15},{7,14},{8,1},{9,0},... | collective-permute-start | bytes 64520 | tf_op jit(solution)/shard_map/ppermute | solution.py:325
  44.7 3.9 %collective-permute-start.15 = (bf16[24,448]{1,0:T(8,128)(2,1)S(1)}, bf16[24,448]{1,0:T(8,128)(2,1)S(1)}, u32[]{:S(2)}, u32[]{:S(2)}) collective-permute-start(bf16[24,448]{1,0:T(8,128)(2,1)S(1)} %get-tuple-element.96), channel_id=1, source_target_pairs={{0,5},{1,4},{2,7},{3,6},{4,1},{5,0},{6,3},{7,2},{8,13},{9,12},{10,... | collective-permute-start | bytes 64520 | tf_op jit(solution)/shard_map/ppermute | solution.py:325

commit v8 on v7

--- a/solution.py
+++ b/solution.py
@@ -208,6 +208,15 @@
     send_ref[spot] = jnp.where(first_core, halves[1], halves[0]).astype(jnp.bfloat16)
 
 
+def direct_peer():
+    return 1
+
+
+def sum_order(outer):
+    direct = direct_peer()
+    return [peer for peer in range(outer) if peer != direct] + [direct]
+
+
 def project_kernel(across, flat, proj_ref, keep_ref, send_ref):
     side = lax.rem(lax.div(lax.axis_index("ctx"), 2), 2)
     side = 1 - side if across else side
@@ -218,7 +227,7 @@
         part = jnp.dot(flat, proj_ref[:, pl.ds(at, span)], preferred_element_type=jnp.float32)
         straight = outer == spot
         if across:
-            straight |= outer == lax.bitwise_xor(spot, keep_ref.shape[0] - 1)
+            straight |= outer == lax.bitwise_xor(spot, direct_peer())
         share(part, 0, spot, keep_ref, send_ref, jnp.where(straight, 0, 1) + across)
 
 
@@ -234,11 +243,11 @@
 
 def add_kernel(keep_ref, got_ref, out_ref, direct_ref):
     outer = lax.div(lax.axis_index("ctx"), 4)
-    for peer in range(keep_ref.shape[0]):
+    for place, peer in enumerate(sum_order(keep_ref.shape[0])):
         spot = lax.bitwise_xor(outer, peer)
         value = keep_ref[spot] + got_ref[spot].astype(jnp.float32)
-        if peer < out_ref.shape[0]:
-            out_ref[peer] = value.astype(out_ref.dtype)
+        if place < out_ref.shape[0]:
+            out_ref[place] = value.astype(out_ref.dtype)
         else:
             direct_ref[...] = value.astype(direct_ref.dtype)
 
@@ -407,7 +416,8 @@
         leave, direct_across = call(add_kernel, (narrow, thin), (keep, got_leaving))
         got_staying = swap(stay_send, 1)
         stay, direct = call(add_kernel, (wide, thin), (stay, got_staying))
-        last = inner * (outer - 1)
+        last = inner * direct_peer()
+        later = sum_order(outer)[1:-1]
         came = [swap(direct, last + 1), swap(direct_across, last + 3)]
         own, *parts = call(
             depart_kernel,
@@ -426,8 +436,9 @@
             (stay, swap(send, 2)),
         )
         came = []
-    for peer in range(len(parts), 0, -1):
-        came.append(swap(parts[peer - 1], inner * peer + cross))
+        later = list(range(1, outer))
+    for peer, value in zip(later, parts):
+        came.append(swap(value, inner * peer + cross))
     result = own
     for value in came:
         result = result + value.astype(jnp.float32)

time: 49.4 us -> 50.6 us (1.024)
  waiting for transfers between devices: 12.8 us -> 15.9 us
  starting transfers between devices: 21.7 us -> 19.8 us
    ppermute x16, waiting for transfers between devices: 12.8 us -> 15.9 us  [swap(): return lax.ppermute(value, 'ctx', [(i, i ^ bits) for i in range(count)])]
    ppermute x16, starting transfers between devices: 21.7 us -> 19.8 us  [swap(): return lax.ppermute(value, 'ctx', [(i, i ^ bits) for i in range(count)])]
  transfers between devices with their start and end apart: 16 -> 16, of which waited for: 6 -> 7; matrix products, arithmetic and copies ran while one was open for 12% -> 11% of each run, Pallas kernels for 11% -> 11%
where the time goes in v8:
time: 50.6 us; the launch traced here: 50.3 us
  starting transfers between devices  19.8 us (39%)
  waiting for transfers between devices  15.9 us (31%)
  Pallas kernels  7.52 us (15%)
  other arithmetic  5.33 us (11%)
  local copies, waits for them, and re-layouts  0.99 us (2%)
  between operations  0.87 us (2%)
    ppermute x16, starting transfers between devices, swap(): return lax.ppermute(value, 'ctx', [(i, i ^ bits) for i in range(count)])  19.8 us
    ppermute x16, waiting for transfers between devices, swap(): return lax.ppermute(value, 'ctx', [(i, i ^ bits) for i in range(count)])  15.9 us
    pallas_call x11, Pallas kernels, call(): pl.pallas_call(kernel, out_shape=outs, in_specs=specs or [pl.BlockSpec()...  7.52 us
    select_n x2, other arithmetic, on_chip(): return jnp.where(lengths[0] > -1, value, jnp.zeros_like(value))  4.67 us
  transfers between devices with their start and end apart: 16, of which 7 were waited for; matrix products, arithmetic and copies ran while one was open for 11% of the time, Pallas kernels for 11%

profile of v8, /device:TPU:0, one launch (start us, length us, event | category | flops | bytes accessed | tf_op | source)
XLA Modules:
  0.0 50.3 jit_solution(18354536997349084455)
XLA Ops:
  0.0 2.4 %collective-permute-start.2 = (bf16[576,512]{1,0:T(8,128)(2,1)}, bf16[576,512]{1,0:T(8,128)(2,1)S(1)}, u32[]{:S(2)}, u32[]{:S(2)}) collective-permute-start(bf16[576,512]{1,0:T(8,128)(2,1)} %bitcast.36), channel_id=1, source_target_pairs={{0,3},{1,2},{2,1},{3,0},{4,7},{5,6},{6,5},{7,4},{8,11},{9,10},{10,... | collective-permute-start | bytes 1769480 | tf_op jit(solution)/shard_map/ppermute | solution.py:334
  2.4 1.9 %collective-permute-start.4 = (bf16[24,4,576]{2,1,0:T(4,128)(2,1)}, bf16[24,4,576]{2,1,0:T(4,128)(2,1)S(1)}, u32[]{:S(2)}, u32[]{:S(2)}) collective-permute-start(bf16[24,4,576]{2,1,0:T(4,128)(2,1)} %bitcast.38), channel_id=1, source_target_pairs={{0,5},{1,4},{2,7},{3,6},{4,1},{5,0},{6,3},{7,2},{8,13},{9,12},{10,... | collective-permute-start | bytes 331784 | tf_op jit(solution)/shard_map/ppermute | solution.py:334
  4.3 2.0 %collective-permute-start.1 = (bf16[24,4,576]{2,1,0:T(4,128)(2,1)}, bf16[24,4,576]{2,1,0:T(4,128)(2,1)S(1)}, u32[]{:S(2)}, u32[]{:S(2)}) collective-permute-start(bf16[24,4,576]{2,1,0:T(4,128)(2,1)} %bitcast.39), channel_id=1, source_target_pairs={{0,13},{1,12},{2,15},{3,14},{4,9},{5,8},{6,11},{7,10},{8,5},{9,4},... | collective-permute-start | bytes 331784 | tf_op jit(solution)/shard_map/ppermute | solution.py:334
  6.3 0.0 collective-permute-start
  6.3 0.7 %collective-permute-start.5 = (bf16[576,512]{1,0:T(8,128)(2,1)}, bf16[576,512]{1,0:T(8,128)(2,1)S(1)}, u32[]{:S(2)}, u32[]{:S(2)}) collective-permute-start(bf16[576,512]{1,0:T(8,128)(2,1)} %bitcast.37), channel_id=1, source_target_pairs={{0,1},{1,0},{2,3},{3,2},{4,5},{5,4},{6,7},{7,6},{8,9},{9,8},{10,11... | collective-permute-start | bytes 1769480 | tf_op jit(solution)/shard_map/ppermute | solution.py:334
  7.7 0.9 %copy.10 = bf16[4,24,576]{2,1,0:T(8,128)(2,1)S(1)} copy(bf16[4,24,576]{2,0,1:T(4,128)(2,1)} %bitcast.41) | data formatting | bytes 221184 | tf_op jit(solution)/shard_map/transpose | solution.py:347
  8.6 7.9 %collective-permute-done.2.refs_5_ = bf16[576,512]{1,0:T(8,128)(2,1)S(1)} collective-permute-done((bf16[576,512]{1,0:T(8,128)(2,1)}, bf16[576,512]{1,0:T(8,128)(2,1)S(1)}, u32[]{:S(2)}, u32[]{:S(2)}) %collective-permute-start.2) | collective-permute-done | bytes 589856 | tf_op jit(solution)/shard_map/ppermute | solution.py:334
  16.5 0.2 collective-permute-start.3
  16.7 1.1 %broadcast_select_fusion.1.refs_4_.refs_2_ = bf16[576,512]{1,0:T(8,128)(2,1)S(1)} fusion(pred[]{:T(512)S(6)} %gt.4, bf16[1,512,576]{1,2,0:T(8,128)(2,1)} %param.8), kind=kLoop, calls=%fused_computation.1 | loop fusion | flops 294912 | bytes 1179649 | tf_op jit(solution)/shard_map/jit(_where)/select_n | solution.py:337
  17.8 0.0 collective-permute-done.4
  17.8 0.0 collective-permute-done.1
  17.9 0.1 collective-permute-done
  18.0 0.0 collective-permute-done.5.refs_5_.refs_3_
  18.0 0.8 %shard_map.74 = (f32[96,512]{1,0:T(8,128)S(1)}, f32[96,1]{1,0:T(8,128)S(1)}, f32[96,1]{1,0:T(8,128)S(1)}) custom-call(f32[1,1024]{1,0:T(1,128)S(1)} %compare_select_fusion.refs_0_, bf16[96,576]{1,0:T(8,128)(2,1)S(1)} %bitcast.32, bf16[576,512]{1,0:T(8,128)(2,1)S(1)} %broadcast_select_fusion.1.refs_4_.refs_2_, ...), custom_call_target="tpu_custom_call" | custom-call | tf_op jit(solution)/shard_map/pallas_call | solution.py:299
  18.8 1.2 %shard_map.73 = (f32[96,512]{1,0:T(8,128)S(1)}, f32[96,1]{1,0:T(8,128)S(1)}, f32[96,1]{1,0:T(8,128)S(1)}, f32[96,512]{1,0:T(8,128)S(1)}, f32[96,1]{1,0:T(8,128)S...) custom-call(f32[1,1024]{1,0:T(1,128)S(1)} %compare_select_fusion.refs_0_, ...), custom_call_target="tpu_custom_call" | custom-call | tf_op jit(solution)/shard_map/pallas_call | solution.py:299
  20.0 1.1 %shard_map.75 = (f32[96,512]{1,0:T(8,128)S(1)}, f32[96,1]{1,0:T(8,128)S(1)}, f32[96,1]{1,0:T(8,128)S(1)}, f32[96,512]{1,0:T(8,128)S(1)}, f32[96,1]{1,0:T(8,128)S...) custom-call(f32[1,512]{1,0:T(1,128)S(1)} %compare_select_fusion.1.re, ...), custom_call_target="tpu_custom_call" | custom-call | tf_op jit(solution)/shard_map/pallas_call | solution.py:299
  21.1 0.0 collective-permute-done.3.refs_3_
  21.1 0.8 %shard_map.76 = (bf16[392,128]{1,0:T(8,128)(2,1)S(1)}, bf16[392,128]{1,0:T(8,128)(2,1)S(1)}) custom-call(f32[1,512]{1,0:T(1,128)S(1)} %compare_select_fusion.2.refs_0_, bf16[96,576]{1,0:T(8,128)(2,1)S(1)} %bitcast.34, bf16[96,576]{1,0:T(8,128)(2,1)S(1)} %bitcast.31, bf16[576,512]{1,0:T(8,128)(2,1)S(1)} %collective-permute-done.3.refs_3_, ...), custom_call_target="tpu_custom_call" | custom-call | tf_op jit(solution)/shard_map/pallas_call | solution.py:299
  21.8 3.3 %collective-permute-start.6 = (bf16[392,128]{1,0:T(8,128)(2,1)S(1)}, bf16[392,128]{1,0:T(8,128)(2,1)S(1)}, u32[]{:S(2)}, u32[]{:S(2)}) collective-permute-start(bf16[392,128]{1,0:T(8,128)(2,1)S(1)} %get-tuple-element.69), channel_id=1, source_target_pairs={{0,9},{1,8},{2,11},{3,10},{4,13},{5,12},{6,15},{7,14},{8,1},{9,0},... | collective-permute-start | bytes 301064 | tf_op jit(solution)/shard_map/ppermute | solution.py:334
  25.1 1.1 %collective-permute-start.7 = (bf16[392,128]{1,0:T(8,128)(2,1)S(1)}, bf16[392,128]{1,0:T(8,128)(2,1)S(1)}, u32[]{:S(2)}, u32[]{:S(2)}) collective-permute-start(bf16[392,128]{1,0:T(8,128)(2,1)S(1)} %get-tuple-element.70), channel_id=1, source_target_pairs={{0,13},{1,12},{2,15},{3,14},{4,9},{5,8},{6,11},{7,10},{8,5},{9,4},... | collective-permute-start | bytes 301064 | tf_op jit(solution)/shard_map/ppermute | solution.py:334
  26.2 0.8 %shard_map.77 = (f32[96,512]{1,0:T(8,128)S(1)}, f32[96,1]{1,0:T(8,128)S(1)}, f32[96,1]{1,0:T(8,128)S(1)}, bf16[392,128]{1,0:T(8,128)(2,1)S(1)}) custom-call(f32[1,512]{1,0:T(1,128)S(1)} %compare_select_fusion.2.refs_0_, bf16[96,576]{1,0:T(8,128)(2,1)S(1)} %bitcast.24, bf16[96,576]{1,0:T(8,128)(2,1)S(1)} %bitcast.28, ...), custom_call_target="tpu_custom_call" | custom-call | tf_op jit(solution)/shard_map/pallas_call | solution.py:299
  27.0 0.0 copy-start
  27.0 0.0 copy-start.1
  27.0 0.0 copy-start.2
  27.0 0.4 collective-permute-start.8
  27.4 3.6 %broadcast_select_fusion.refs_7_.proj_ref = bf16[512,7168]{1,0:T(8,128)(2,1)S(1)} fusion(bf16[512,7168]{1,0:T(8,128)(2,1)} %param.13, pred[]{:T(512)S(6)} %gt.4), kind=kLoop, calls=%fused_computation | loop fusion | flops 3670016 | bytes 14680065 | tf_op jit(solution)/shard_map/jit(_where)/select_n | solution.py:337
  30.9 0.0 copy-done
  31.0 0.0 copy-done.1
  31.0 0.0 copy-done.2
  31.0 1.0 %shard_map.78 = (f32[96,512]{1,0:T(8,128)S(1)}, f32[96,1]{1,0:T(8,128)S(1)}, f32[96,1]{1,0:T(8,128)S(1)}, bf16[4,512,128]{2,1,0:T(8,128)(2,1)S(1)}) custom-call(bf16[96,576]{1,0:T(8,128)(2,1)S(1)} %bitcast.25, bf16[24,576]{1,0:T(8,128)(2,1)S(1)} %bitcast.35, s32[1,24]{1,0:T(1,128)S(1)} %copy-done.2, bf16[4,512,128]{2,1,0:T(8,128)(2,1)S(1)} %copy-done, ...), custom_call_target="tpu_custom_call" | custom-call | tf_op jit(solution)/shard_map/pallas_call | solution.py:299
  31.9 0.7 %collective-permute-done.6.refs_0_ = bf16[392,128]{1,0:T(8,128)(2,1)S(1)} collective-permute-done((bf16[392,128]{1,0:T(8,128)(2,1)S(1)}, bf16[392,128]{1,0:T(8,128)(2,1)S(1)}, u32[]{:S(2)}, u32[]{:S(2)}) %collective-permute-start.6) | collective-permute-done | bytes 100384 | tf_op jit(solution)/shard_map/ppermute | solution.py:334
  32.7 0.0 collective-permute-done.7.refs_1_
  32.7 2.3 %collective-permute-done.8.refs_2_ = bf16[392,128]{1,0:T(8,128)(2,1)S(1)} collective-permute-done((bf16[392,128]{1,0:T(8,128)(2,1)S(1)}, bf16[392,128]{1,0:T(8,128)(2,1)S(1)}, u32[]{:S(2)}, u32[]{:S(2)}) %collective-permute-start.8) | collective-permute-done | bytes 100384 | tf_op jit(solution)/shard_map/ppermute | solution.py:334
  34.9 1.1 %shard_map.79 = (bf16[24,512]{1,0:T(8,128)(2,1)S(1)}, f32[4,24,448]{2,1,0:T(8,128)S(1)}, bf16[4,24,448]{2,1,0:T(8,128)(2,1)S(1)}) custom-call(bf16[392,128]{1,0:T(8,128)(2,1)S(1)} %collective-permute-done.6.refs_0_, bf16[392,128]{1,0:T(8,128)(2,1)S(1)} %collective-permute-done.7.refs_1_, bf16[392,128]{1,0:T(8,128)(2,1)S(1)} %collective-permute-done.8.refs_2_, ...), custom_call_target="tpu_custom_call" | custom-call | tf_op jit(solution)/shard_map/pallas_call | solution.py:299
  36.1 0.2 collective-permute-start.10
  36.3 0.8 %shard_map.80 = (f32[4,24,448]{2,1,0:T(8,128)S(1)}, bf16[4,24,448]{2,1,0:T(8,128)(2,1)S(1)}) custom-call(bf16[24,512]{1,0:T(8,128)(2,1)S(1)} %get-tuple-element.85.flat_ref, bf16[512,7168]{1,0:T(8,128)(2,1)S(1)} %broadcast_select_fusion.refs_7_.proj_ref), custom_call_target="tpu_custom_call" | custom-call | tf_op jit(solution)/shard_map/pallas_call | solution.py:299
  37.1 0.5 collective-permute-start.9
  37.5 0.0 collective-permute-done.10.got_ref
  37.6 1.4 %collective-permute-start.11 = (bf16[3,24,448]{2,1,0:T(8,128)(2,1)S(1)}, bf16[3,24,448]{2,1,0:T(8,128)(2,1)S(1)}, u32[]{:S(2)}, u32[]{:S(2)}) collective-permute-start(bf16[3,24,448]{2,1,0:T(8,128)(2,1)S(1)} %get-tuple-element.91), channel_id=1, source_target_pairs={{0,3},{1,2},{2,1},{3,0},{4,7},{5,6},{6,5},{7,4},{8,11},{9,10},{10,... | collective-permute-start | bytes 193544 | tf_op jit(solution)/shard_map/ppermute | solution.py:334
  39.0 0.0 collective-permute-done.9.got_ref
  39.0 0.9 %collective-permute-start.12 = (bf16[24,448]{1,0:T(8,128)(2,1)S(1)}, bf16[24,448]{1,0:T(8,128)(2,1)S(1)}, u32[]{:S(2)}, u32[]{:S(2)}) collective-permute-start(bf16[24,448]{1,0:T(8,128)(2,1)S(1)} %get-tuple-element.93), channel_id=1, source_target_pairs={{0,5},{1,4},{2,7},{3,6},{4,1},{5,0},{6,3},{7,2},{8,13},{9,12},{10,... | collective-permute-start | bytes 64520 | tf_op jit(solution)/shard_map/ppermute | solution.py:334
  39.9 1.5 %collective-permute-start.13 = (bf16[24,448]{1,0:T(8,128)(2,1)S(1)}, bf16[24,448]{1,0:T(8,128)(2,1)S(1)}, u32[]{:S(2)}, u32[]{:S(2)}) collective-permute-start(bf16[24,448]{1,0:T(8,128)(2,1)S(1)} %get-tuple-element.94), channel_id=1, source_target_pairs={{0,7},{1,6},{2,5},{3,4},{4,3},{5,2},{6,1},{7,0},{8,15},{9,14},{10,... | collective-permute-start | bytes 64520 | tf_op jit(solution)/shard_map/ppermute | solution.py:334
  41.4 0.5 %collective-permute-done.11.got_ref = bf16[3,24,448]{2,1,0:T(8,128)(2,1)S(1)} collective-permute-done((bf16[3,24,448]{2,1,0:T(8,128)(2,1)S(1)}, bf16[3,24,448]{2,1,0:T(8,128)(2,1)S(1)}, u32[]{:S(2)}, u32[]{:S(2)}) %collective-permute-start.11) | collective-permute-done | bytes 64544 | tf_op jit(solution)/shard_map/ppermute | solution.py:334
  41.9 2.8 %collective-permute-start.14 = (bf16[24,448]{1,0:T(8,128)(2,1)S(1)}, bf16[24,448]{1,0:T(8,128)(2,1)S(1)}, u32[]{:S(2)}, u32[]{:S(2)}) collective-permute-start(bf16[24,448]{1,0:T(8,128)(2,1)S(1)} %get-tuple-element.95), channel_id=1, source_target_pairs={{0,9},{1,8},{2,11},{3,10},{4,13},{5,12},{6,15},{7,14},{8,1},{9,0},... | collective-permute-start | bytes 64520 | tf_op jit(solution)/shard_map/ppermute | solution.py:334
  44.7 0.7 %collective-permute-start.15 = (bf16[24,448]{1,0:T(8,128)(2,1)S(1)}, bf16[24,448]{1,0:T(8,128)(2,1)S(1)}, u32[]{:S(2)}, u32[]{:S(2)}) collective-permute-start(bf16[24,448]{1,0:T(8,128)(2,1)S(1)} %get-tuple-element.96), channel_id=1, source_target_pairs={{0,13},{1,12},{2,15},{3,14},{4,9},{5,8},{6,11},{7,10},{8,5},{9,4},... | collective-permute-start | bytes 64520 | tf_op jit(solution)/shard_map/ppermute | solution.py:334
  45.3 0.0 collective-permute-done.12
  45.3 0.0 collective-permute-done.13
  45.3 0.9 %collective-permute-done.14 = bf16[24,448]{1,0:T(8,128)(2,1)S(1)} collective-permute-done((bf16[24,448]{1,0:T(8,128)(2,1)S(1)}, bf16[24,448]{1,0:T(8,128)(2,1)S(1)}, u32[]{:S(2)}, u32[]{:S(2)}) %collective-permute-start.14) | collective-permute-done | bytes 21536 | tf_op jit(solution)/shard_map/ppermute | solution.py:334
  46.2 3.5 %collective-permute-done.15 = bf16[24,448]{1,0:T(8,128)(2,1)S(1)} collective-permute-done((bf16[24,448]{1,0:T(8,128)(2,1)S(1)}, bf16[24,448]{1,0:T(8,128)(2,1)S(1)}, u32[]{:S(2)}, u32[]{:S(2)}) %collective-permute-start.15) | collective-permute-done | bytes 21536 | tf_op jit(solution)/shard_map/ppermute | solution.py:334
  49.7 0.6 %add_convert_fusion = bf16[24,448]{1,0:T(8,128)(2,1)} fusion(bf16[24,448]{1,0:T(8,128)(2,1)S(1)} %collective-permute-done.15, bf16[24,448]{1,0:T(8,128)(2,1)S(1)} %collective-permute-done.14, bf16[24,448]{1,0:T(8,128)(2,1)S(1)} %collective-permute-done.13, f32[24,448]{1,0:T(8,128)S(1)} %get-tuple-element.92, bf16[24,448]{1,0:T(8,128)(2,1)S(1)} %collective-permute-done.12), kind=kLoop, calls=%fused_computation.2 | loop fusion | flops 96768 | bytes 150528 | tf_op jit(solution)/shard_map/convert_element_type | solution.py:445
  (11 shorter events, 0.1 us)
Async XLA Ops:
  0.0 16.5 %collective-permute-start.2 = (bf16[576,512]{1,0:T(8,128)(2,1)}, bf16[576,512]{1,0:T(8,128)(2,1)S(1)}, u32[]{:S(2)}, u32[]{:S(2)}) collective-permute-start(bf16[576,512]{1,0:T(8,128)(2,1)} %bitcast.36), channel_id=1, source_target_pairs={{0,3},{1,2},{2,1},{3,0},{4,7},{5,6},{6,5},{7,4},{8,11},{9,10},{10,... | collective-permute-start | bytes 1769480 | tf_op jit(solution)/shard_map/ppermute | solution.py:334
  2.4 15.4 %collective-permute-start.4 = (bf16[24,4,576]{2,1,0:T(4,128)(2,1)}, bf16[24,4,576]{2,1,0:T(4,128)(2,1)S(1)}, u32[]{:S(2)}, u32[]{:S(2)}) collective-permute-start(bf16[24,4,576]{2,1,0:T(4,128)(2,1)} %bitcast.38), channel_id=1, source_target_pairs={{0,5},{1,4},{2,7},{3,6},{4,1},{5,0},{6,3},{7,2},{8,13},{9,12},{10,... | collective-permute-start | bytes 331784 | tf_op jit(solution)/shard_map/ppermute | solution.py:334
  4.3 13.5 %collective-permute-start.1 = (bf16[24,4,576]{2,1,0:T(4,128)(2,1)}, bf16[24,4,576]{2,1,0:T(4,128)(2,1)S(1)}, u32[]{:S(2)}, u32[]{:S(2)}) collective-permute-start(bf16[24,4,576]{2,1,0:T(4,128)(2,1)} %bitcast.39), channel_id=1, source_target_pairs={{0,13},{1,12},{2,15},{3,14},{4,9},{5,8},{6,11},{7,10},{8,5},{9,4},... | collective-permute-start | bytes 331784 | tf_op jit(solution)/shard_map/ppermute | solution.py:334
  6.3 11.6 %collective-permute-start = (bf16[24,4,576]{2,1,0:T(4,128)(2,1)}, bf16[24,4,576]{2,1,0:T(4,128)(2,1)S(1)}, u32[]{:S(2)}, u32[]{:S(2)}) collective-permute-start(bf16[24,4,576]{2,1,0:T(4,128)(2,1)} %bitcast.40), channel_id=1, source_target_pairs={{0,9},{1,8},{2,11},{3,10},{4,13},{5,12},{6,15},{7,14},{8,1},{9,0},... | collective-permute-start | bytes 331784 | tf_op jit(solution)/shard_map/ppermute | solution.py:334
  6.3 11.6 %collective-permute-start.5 = (bf16[576,512]{1,0:T(8,128)(2,1)}, bf16[576,512]{1,0:T(8,128)(2,1)S(1)}, u32[]{:S(2)}, u32[]{:S(2)}) collective-permute-start(bf16[576,512]{1,0:T(8,128)(2,1)} %bitcast.37), channel_id=1, source_target_pairs={{0,1},{1,0},{2,3},{3,2},{4,5},{5,4},{6,7},{7,6},{8,9},{9,8},{10,11... | collective-permute-start | bytes 1769480 | tf_op jit(solution)/shard_map/ppermute | solution.py:334
  16.5 4.6 %collective-permute-start.3 = (bf16[576,512]{1,0:T(8,128)(2,1)S(1)}, bf16[576,512]{1,0:T(8,128)(2,1)S(1)}, u32[]{:S(2)}, u32[]{:S(2)}) collective-permute-start(bf16[576,512]{1,0:T(8,128)(2,1)S(1)} %collective-permute-done.2.refs_5_), channel_id=1, source_target_pairs={{0,1},{1,0},{2,3},{3,2},{4,5},{5,4},{6,7},{7,6},{8,9},{9,8},{10,11... | collective-permute-start | bytes 1769480 | tf_op jit(solution)/shard_map/ppermute | solution.py:334
  21.8 10.8 %collective-permute-start.6 = (bf16[392,128]{1,0:T(8,128)(2,1)S(1)}, bf16[392,128]{1,0:T(8,128)(2,1)S(1)}, u32[]{:S(2)}, u32[]{:S(2)}) collective-permute-start(bf16[392,128]{1,0:T(8,128)(2,1)S(1)} %get-tuple-element.69), channel_id=1, source_target_pairs={{0,9},{1,8},{2,11},{3,10},{4,13},{5,12},{6,15},{7,14},{8,1},{9,0},... | collective-permute-start | bytes 301064 | tf_op jit(solution)/shard_map/ppermute | solution.py:334
  25.1 7.5 %collective-permute-start.7 = (bf16[392,128]{1,0:T(8,128)(2,1)S(1)}, bf16[392,128]{1,0:T(8,128)(2,1)S(1)}, u32[]{:S(2)}, u32[]{:S(2)}) collective-permute-start(bf16[392,128]{1,0:T(8,128)(2,1)S(1)} %get-tuple-element.70), channel_id=1, source_target_pairs={{0,13},{1,12},{2,15},{3,14},{4,9},{5,8},{6,11},{7,10},{8,5},{9,4},... | collective-permute-start | bytes 301064 | tf_op jit(solution)/shard_map/ppermute | solution.py:334
  27.0 4.0 %copy-start = (bf16[4,512,128]{2,1,0:T(8,128)(2,1)S(1)}, bf16[4,512,128]{2,1,0:T(8,128)(2,1)}, u32[]{:S(2)}) copy-start(bf16[4,512,128]{2,1,0:T(8,128)(2,1)} %up_from.1) | copy-start | bytes 1572868
  27.0 3.9 %copy-start.1 = (bf16[1,24,576]{2,1,0:T(8,128)(2,1)S(1)}, bf16[1,24,576]{2,1,0:T(8,128)(2,1)}, u32[]{:S(2)}) copy-start(bf16[1,24,576]{2,1,0:T(8,128)(2,1)} %param.9) | copy-start | bytes 82948
  27.0 3.9 %copy-start.2 = (s32[1,24]{1,0:T(1,128)S(1)}, s32[1,24]{1,0:T(1,128)}, u32[]{:S(2)}) copy-start(s32[1,24]{1,0:T(1,128)} %parents_ref.1) | copy-start | bytes 292
  27.0 7.9 %collective-permute-start.8 = (bf16[392,128]{1,0:T(8,128)(2,1)S(1)}, bf16[392,128]{1,0:T(8,128)(2,1)S(1)}, u32[]{:S(2)}, u32[]{:S(2)}) collective-permute-start(bf16[392,128]{1,0:T(8,128)(2,1)S(1)} %get-tuple-element.77), channel_id=1, source_target_pairs={{0,5},{1,4},{2,7},{3,6},{4,1},{5,0},{6,3},{7,2},{8,13},{9,12},{10,... | collective-permute-start | bytes 301064 | tf_op jit(solution)/shard_map/ppermute | solution.py:334
  36.1 1.4 %collective-permute-start.10 = (bf16[4,24,448]{2,1,0:T(8,128)(2,1)S(1)}, bf16[4,24,448]{2,1,0:T(8,128)(2,1)S(1)}, u32[]{:S(2)}, u32[]{:S(2)}) collective-permute-start(bf16[4,24,448]{2,1,0:T(8,128)(2,1)S(1)} %get-tuple-element.90), channel_id=1, source_target_pairs={{0,1},{1,0},{2,3},{3,2},{4,5},{5,4},{6,7},{7,6},{8,9},{9,8},{10,11... | collective-permute-start | bytes 258056 | tf_op jit(solution)/shard_map/ppermute | solution.py:334
  37.1 1.9 %collective-permute-start.9 = (bf16[4,24,448]{2,1,0:T(8,128)(2,1)S(1)}, bf16[4,24,448]{2,1,0:T(8,128)(2,1)S(1)}, u32[]{:S(2)}, u32[]{:S(2)}) collective-permute-start(bf16[4,24,448]{2,1,0:T(8,128)(2,1)S(1)} %get-tuple-element.87), channel_id=1, source_target_pairs={{0,1},{1,0},{2,3},{3,2},{4,5},{5,4},{6,7},{7,6},{8,9},{9,8},{10,11... | collective-permute-start | bytes 258056 | tf_op jit(solution)/shard_map/ppermute | solution.py:334
  37.6 4.3 %collective-permute-start.11 = (bf16[3,24,448]{2,1,0:T(8,128)(2,1)S(1)}, bf16[3,24,448]{2,1,0:T(8,128)(2,1)S(1)}, u32[]{:S(2)}, u32[]{:S(2)}) collective-permute-start(bf16[3,24,448]{2,1,0:T(8,128)(2,1)S(1)} %get-tuple-element.91), channel_id=1, source_target_pairs={{0,3},{1,2},{2,1},{3,0},{4,7},{5,6},{6,5},{7,4},{8,11},{9,10},{10,... | collective-permute-start | bytes 193544 | tf_op jit(solution)/shard_map/ppermute | solution.py:334
  39.0 6.3 %collective-permute-start.12 = (bf16[24,448]{1,0:T(8,128)(2,1)S(1)}, bf16[24,448]{1,0:T(8,128)(2,1)S(1)}, u32[]{:S(2)}, u32[]{:S(2)}) collective-permute-start(bf16[24,448]{1,0:T(8,128)(2,1)S(1)} %get-tuple-element.93), channel_id=1, source_target_pairs={{0,5},{1,4},{2,7},{3,6},{4,1},{5,0},{6,3},{7,2},{8,13},{9,12},{10,... | collective-permute-start | bytes 64520 | tf_op jit(solution)/shard_map/ppermute | solution.py:334
  39.9 5.5 %collective-permute-start.13 = (bf16[24,448]{1,0:T(8,128)(2,1)S(1)}, bf16[24,448]{1,0:T(8,128)(2,1)S(1)}, u32[]{:S(2)}, u32[]{:S(2)}) collective-permute-start(bf16[24,448]{1,0:T(8,128)(2,1)S(1)} %get-tuple-element.94), channel_id=1, source_target_pairs={{0,7},{1,6},{2,5},{3,4},{4,3},{5,2},{6,1},{7,0},{8,15},{9,14},{10,... | collective-permute-start | bytes 64520 | tf_op jit(solution)/shard_map/ppermute | solution.py:334
  41.9 4.3 %collective-permute-start.14 = (bf16[24,448]{1,0:T(8,128)(2,1)S(1)}, bf16[24,448]{1,0:T(8,128)(2,1)S(1)}, u32[]{:S(2)}, u32[]{:S(2)}) collective-permute-start(bf16[24,448]{1,0:T(8,128)(2,1)S(1)} %get-tuple-element.95), channel_id=1, source_target_pairs={{0,9},{1,8},{2,11},{3,10},{4,13},{5,12},{6,15},{7,14},{8,1},{9,0},... | collective-permute-start | bytes 64520 | tf_op jit(solution)/shard_map/ppermute | solution.py:334
  44.7 5.0 %collective-permute-start.15 = (bf16[24,448]{1,0:T(8,128)(2,1)S(1)}, bf16[24,448]{1,0:T(8,128)(2,1)S(1)}, u32[]{:S(2)}, u32[]{:S(2)}) collective-permute-start(bf16[24,448]{1,0:T(8,128)(2,1)S(1)} %get-tuple-element.96), channel_id=1, source_target_pairs={{0,13},{1,12},{2,15},{3,14},{4,9},{5,8},{6,11},{7,10},{8,5},{9,4},... | collective-permute-start | bytes 64520 | tf_op jit(solution)/shard_map/ppermute | solution.py:334
